TPU v7x, 32 devices: a whole 2x2x4 slice. The times are simulated.
32 devices in a mesh: dp: 8 (over y, x, core), tensor: 4 (over z).
Axes of the slice: x: 2, y: 2, z: 4, core: 2. Of those that a mesh axis runs over, the one named last changes fastest.
Arguments:
- tokens: bfloat16 [32, 256, 1152], P(('dp', 'tensor')), may hold values from -6 to 6
- timesteps: int32 [32], P('dp'), may hold values from 0 to 999
- labels: int32 [32], P('dp'), may hold values from 0 to 999
- item_counts: int32 [8], P('dp'), may hold values from 1 to 4
- cotangent: bfloat16 [32, 256, 1152], P(('dp', 'tensor')), may hold values from -6 to 6
- project_weight: bfloat16 [1152, 3, 1152], P(None, None, 'tensor'), may hold values from -0.1875 to 0.1875
- query_gain: bfloat16 [72], replicated, may hold values from 0.099609375 to 1.8984375
- key_gain: bfloat16 [72], replicated, may hold values from 0.099609375 to 1.8984375
- output_weight: bfloat16 [1152, 1152], P('tensor'), may hold values from -0.5 to 0.5
- output_bias: bfloat16 [1152], replicated, may hold values from -3 to 3
- expand_weight: bfloat16 [1152, 2, 3072], P(None, None, 'tensor'), may hold values from -0.1875 to 0.1875
- down_weight: bfloat16 [3072, 1152], P('tensor'), may hold values from -0.15625 to 0.15625
- down_bias: bfloat16 [1152], replicated, may hold values from -3 to 3
- modulate_weight: bfloat16 [1152, 6, 1152], P(None, None, 'tensor'), may hold values from -0.1875 to 0.1875
- modulate_bias: bfloat16 [6, 1152], P(None, 'tensor'), may hold values from -3 to 3
- time_weight: bfloat16 [256, 1152], replicated, may hold values from -0.5 to 0.5
- time_bias: bfloat16 [1152], replicated, may hold values from -3 to 3
- embed_weight: bfloat16 [1152, 1152], replicated, may hold values from -0.25 to 0.25
- embed_bias: bfloat16 [1152], replicated, may hold values from -3 to 3
- class_table: bfloat16 [1000, 1152], replicated, may hold values from -6 to 6
Outputs:
- result: bfloat16 [32, 256, 1152], P(('dp', 'tensor'))
- tokens_grad: bfloat16 [32, 256, 1152], P(('dp', 'tensor'))
- project_grad: float32 [1152, 3, 1152], P('dp', None, 'tensor')
- query_gain_grad: float32 [72], replicated
- key_gain_grad: float32 [72], replicated
- output_weight_grad: float32 [1152, 1152], P('tensor', 'dp')
- output_bias_grad: float32 [1152], replicated
- expand_grad: float32 [1152, 2, 3072], P('dp', None, 'tensor')
- down_grad: float32 [3072, 1152], P('tensor', 'dp')
- down_bias_grad: float32 [1152], replicated
- modulate_grad: float32 [1152, 6, 1152], P('dp', None, 'tensor')
- modulate_bias_grad: float32 [6, 1152], replicated
- time_grad: float32 [256, 1152], P(None, 'dp')
- time_bias_grad: float32 [1152], P('dp')
- embed_grad: float32 [1152, 1152], P('dp')
- embed_bias_grad: float32 [1152], P('dp')
- class_grad: float32 [1000, 1152], P(None, 'dp')
Inputs may be any that keep to these rules, and one draw needn't show every extreme that they name: `item_counts`: entry i counts the real items among the 4 items of index i of dp; they are its first ones.
All inputs are finite; a program needn't handle non-finite values.
Results may differ from a plain program's by a relative error of at most 0.03.
Values may be sent and summed in bfloat16 or wider, within the bound.
A program may use at most 256 MiB of HBM per device.

v0:
```python
import math

import jax
import jax.numpy as jnp
from jax import lax
from jax.sharding import PartitionSpec as P

HD = 72
FREQ = 256
GRID = 16


EPS = 1e-06


def layer_norm(value):
    center = value - jnp.mean(value, axis=-1, keepdims=True)
    inverse = lax.rsqrt(jnp.mean(center * center, axis=-1, keepdims=True) + EPS)
    return (center * inverse, inverse)


def layer_norm_back(normed, inverse, grad):
    return inverse * (
        grad
        - jnp.mean(grad, axis=-1, keepdims=True)
        - normed * jnp.mean(grad * normed, axis=-1, keepdims=True)
    )


def silu_slope(value):
    sigma = jax.nn.sigmoid(value)
    return sigma * (1.0 + value * (1.0 - sigma))


def rotate(value, positions):
    quarter = HD // 4
    rates = 10000.0 ** (-jnp.arange(quarter, dtype=jnp.float32) / quarter)
    places = ((positions // GRID).astype(jnp.float32), (positions % GRID).astype(jnp.float32))
    pieces = []
    for which_half in range(2):
        half_value = value[..., which_half * 2 * quarter : (which_half + 1) * 2 * quarter]
        angle = places[which_half][:, None] * rates[None, :]
        cosine = jnp.cos(angle)[None, :, None, :]
        sine = jnp.sin(angle)[None, :, None, :]
        first = half_value[..., :quarter]
        second = half_value[..., quarter:]
        pieces.append(first * cosine - second * sine)
        pieces.append(second * cosine + first * sine)
    return jnp.concatenate(pieces, axis=-1)


def head_prepare(raw, gain, positions):
    scaled = raw * lax.rsqrt(jnp.mean(raw * raw, axis=-1, keepdims=True) + EPS) * gain
    return rotate(scaled, positions)


def time_features(steps_in):
    half = FREQ // 2
    rates = jnp.exp(-math.log(10000.0) * jnp.arange(half, dtype=jnp.float32) / half)
    angle = steps_in.astype(jnp.float32)[:, None] * rates[None, :]
    return jnp.concatenate([jnp.cos(angle), jnp.sin(angle)], axis=-1)


def shards(
    tokens,
    timesteps,
    labels,
    item_counts,
    cotangent,
    project_weight,
    query_gain,
    key_gain,
    output_weight,
    output_bias,
    expand_weight,
    down_weight,
    down_bias,
    modulate_weight,
    modulate_bias,
    time_weight,
    time_bias,
    embed_weight,
    embed_bias,
    class_table,
):
    local_items, length, width = tokens.shape
    items = timesteps.shape[0]
    slab = modulate_weight.shape[2]
    heads_here = project_weight.shape[2] // HD
    scale = HD ** (-0.5)
    lane = lax.axis_index("tensor")
    first_item = lane * local_items
    live = (first_item + jnp.arange(local_items) < item_counts[0]).astype(jnp.float32)[
        :, None, None
    ]
    time_feat = time_features(timesteps).astype(jnp.bfloat16)
    pre_hidden = jnp.dot(
        time_feat, time_weight, preferred_element_type=jnp.float32
    ) + time_bias.astype(jnp.float32)
    time_hidden = jax.nn.silu(pre_hidden).astype(jnp.bfloat16)
    condition = (
        jnp.dot(time_hidden, embed_weight, preferred_element_type=jnp.float32)
        + embed_bias.astype(jnp.float32)
        + jnp.take(class_table, labels, axis=0).astype(jnp.float32)
    )
    cond_act = jax.nn.silu(condition).astype(jnp.bfloat16)
    modulation_part = (
        jnp.einsum("bd,dke->bke", cond_act, modulate_weight, preferred_element_type=jnp.float32)
        + modulate_bias.astype(jnp.float32)
    ).astype(jnp.bfloat16)
    token_all, modulation = (
        lax.all_gather(tokens, "tensor", axis=0, tiled=True),
        lax.all_gather(modulation_part, "tensor", axis=2, tiled=True),
    )
    modulation = modulation.astype(jnp.float32)
    modulation_local = lax.dynamic_slice_in_dim(modulation, first_item, local_items, 0)
    attend_shift_all = modulation[:, 0][:, None, :]
    attend_scale_all = modulation[:, 1][:, None, :]
    local_parts = [modulation_local[:, which][:, None, :] for which in range(6)]
    _, attend_scale, attend_gate, feed_shift, feed_scale, feed_gate = local_parts
    positions = jnp.arange(length)
    normed_all, _ = layer_norm(token_all.astype(jnp.float32))
    mod_in = (normed_all * (1.0 + attend_scale_all) + attend_shift_all).astype(jnp.bfloat16)
    projected = jnp.einsum(
        "bld,dke->blke", mod_in, project_weight, preferred_element_type=jnp.float32
    )
    split = projected.reshape(items, length, 3, heads_here, HD)
    query_gain_f = query_gain.astype(jnp.float32)
    key_gain_f = key_gain.astype(jnp.float32)
    queries = head_prepare(split[:, :, 0], query_gain_f, positions).astype(jnp.bfloat16)
    keys = head_prepare(split[:, :, 1], key_gain_f, positions).astype(jnp.bfloat16)
    values = split[:, :, 2].astype(jnp.bfloat16)
    scores = (
        jnp.einsum("bqhd,bkhd->bhqk", queries, keys, preferred_element_type=jnp.float32) * scale
    )
    top = jnp.max(scores, axis=-1, keepdims=True)
    logsum = top + jnp.log(jnp.sum(jnp.exp(scores - top), axis=-1, keepdims=True))
    probs = jnp.exp(scores - logsum).astype(jnp.bfloat16)
    mixed = jnp.einsum("bhqk,bkhd->bqhd", probs, values, preferred_element_type=jnp.float32)
    mixed = mixed.reshape(items, length, heads_here * HD).astype(jnp.bfloat16)
    piece = mixed
    attend_branch = lax.psum_scatter(
        jnp.einsum("blh,hd->bld", piece, output_weight, preferred_element_type=jnp.float32).astype(
            jnp.bfloat16
        ),
        "tensor",
        scatter_dimension=0,
        tiled=True,
    ).astype(jnp.float32) + output_bias.astype(jnp.float32)
    token_local = tokens.astype(jnp.float32)
    normed_local, inverse_local = layer_norm(token_local)
    residual = token_local + attend_gate * attend_branch
    normed_two, inverse_two = layer_norm(residual)
    mod_two = (normed_two * (1.0 + feed_scale) + feed_shift).astype(jnp.bfloat16)
    mod_two_all = lax.all_gather(mod_two, "tensor", axis=0, tiled=True)
    gate_up = jnp.einsum(
        "bld,dkf->blkf", mod_two_all, expand_weight, preferred_element_type=jnp.float32
    )
    gate = gate_up[:, :, 0]
    upper = gate_up[:, :, 1]
    hidden = (jax.nn.silu(gate) * upper).astype(jnp.bfloat16)
    piece = hidden
    feed_branch = lax.psum_scatter(
        jnp.einsum("blf,fd->bld", piece, down_weight, preferred_element_type=jnp.float32).astype(
            jnp.bfloat16
        ),
        "tensor",
        scatter_dimension=0,
        tiled=True,
    ).astype(jnp.float32) + down_bias.astype(jnp.float32)
    result = (live * (residual + feed_gate * feed_branch)).astype(jnp.bfloat16)
    out_grad = cotangent.astype(jnp.float32) * live
    branch_grad = (out_grad * feed_gate).astype(jnp.bfloat16)
    down_bias_part = jnp.sum(branch_grad.astype(jnp.float32), axis=(0, 1))
    piece = lax.all_gather(branch_grad, "tensor", axis=0, tiled=True)
    weight_total = jnp.einsum("blf,bld->fd", hidden, piece, preferred_element_type=jnp.float32)
    rows_grad = jnp.einsum("bld,fd->blf", piece, down_weight, preferred_element_type=jnp.float32)
    hidden_total = rows_grad
    down_grad = weight_total
    gate_up_grad = jnp.stack(
        [hidden_total * upper * silu_slope(gate), hidden_total * jax.nn.silu(gate)], axis=2
    ).astype(jnp.bfloat16)
    expand_grad = jnp.einsum(
        "bld,blkf->dkf", mod_two_all, gate_up_grad, preferred_element_type=jnp.float32
    )
    piece = gate_up_grad
    mod_two_grad = lax.psum_scatter(
        jnp.einsum(
            "blkf,dkf->bld", piece, expand_weight, preferred_element_type=jnp.float32
        ).astype(jnp.bfloat16),
        "tensor",
        scatter_dimension=0,
        tiled=True,
    ).astype(jnp.float32)
    residual_grad = out_grad + layer_norm_back(
        normed_two, inverse_two, mod_two_grad * (1.0 + feed_scale)
    )
    attend_grad = (residual_grad * attend_gate).astype(jnp.bfloat16)
    output_bias_part = jnp.sum(attend_grad.astype(jnp.float32), axis=(0, 1))
    piece = lax.all_gather(attend_grad, "tensor", axis=0, tiled=True)
    weight_total = jnp.einsum("blh,bld->hd", mixed, piece, preferred_element_type=jnp.float32)
    rows_grad = jnp.einsum("bld,hd->blh", piece, output_weight, preferred_element_type=jnp.float32)
    output_weight_grad = weight_total
    mixed_grad = rows_grad
    mixed_grad = mixed_grad.reshape(items, length, heads_here, HD).astype(jnp.bfloat16)
    again = jnp.einsum("bqhd,bkhd->bhqk", queries, keys, preferred_element_type=jnp.float32) * scale
    prob_float = jnp.exp(again - logsum)
    prob_low = prob_float.astype(jnp.bfloat16)
    prob_grad = jnp.einsum(
        "bqhd,bkhd->bhqk", mixed_grad, values, preferred_element_type=jnp.float32
    )
    score_grad = (
        prob_float * (prob_grad - jnp.sum(prob_float * prob_grad, axis=-1, keepdims=True))
    ).astype(jnp.bfloat16)
    query_grad = (
        jnp.einsum("bhqk,bkhd->bqhd", score_grad, keys, preferred_element_type=jnp.float32) * scale
    )
    key_grad = (
        jnp.einsum("bhqk,bqhd->bkhd", score_grad, queries, preferred_element_type=jnp.float32)
        * scale
    )
    value_grad = jnp.einsum(
        "bhqk,bqhd->bkhd", prob_low, mixed_grad, preferred_element_type=jnp.float32
    )

    def prepare_here(raw, gain):
        return head_prepare(raw, gain, positions)

    _, query_back = jax.vjp(prepare_here, split[:, :, 0], query_gain_f)
    raw_query_grad, query_gain_part = query_back(query_grad)
    _, key_back = jax.vjp(prepare_here, split[:, :, 1], key_gain_f)
    raw_key_grad, key_gain_part = key_back(key_grad)
    projected_grad = jnp.stack([raw_query_grad, raw_key_grad, value_grad], axis=2)
    projected_grad = projected_grad.reshape(items, length, 3, heads_here * HD).astype(jnp.bfloat16)
    project_grad = jnp.einsum(
        "bld,blke->dke", mod_in, projected_grad, preferred_element_type=jnp.float32
    )
    piece = projected_grad
    mod_in_grad = lax.psum_scatter(
        jnp.einsum(
            "blke,dke->bld", piece, project_weight, preferred_element_type=jnp.float32
        ).astype(jnp.bfloat16),
        "tensor",
        scatter_dimension=0,
        tiled=True,
    ).astype(jnp.float32)
    tokens_grad = (
        residual_grad
        + layer_norm_back(normed_local, inverse_local, mod_in_grad * (1.0 + attend_scale))
    ).astype(jnp.bfloat16)
    modulation_grad_part = jnp.stack(
        [
            jnp.sum(mod_in_grad, axis=1),
            jnp.sum(mod_in_grad * normed_local, axis=1),
            jnp.sum(residual_grad * attend_branch, axis=1),
            jnp.sum(mod_two_grad, axis=1),
            jnp.sum(mod_two_grad * normed_two, axis=1),
            jnp.sum(out_grad * feed_branch, axis=1),
        ],
        axis=1,
    )
    modulation_grad = lax.all_to_all(
        modulation_grad_part, "tensor", split_axis=2, concat_axis=0, tiled=True
    ).astype(jnp.bfloat16)
    modulate_bias_part = jnp.sum(modulation_grad.astype(jnp.float32), axis=0)
    cond_part = jnp.einsum(
        "bke,dke->bd", modulation_grad, modulate_weight, preferred_element_type=jnp.float32
    )
    cond_total = lax.psum(cond_part, "tensor")
    cond_grad = (cond_total * silu_slope(condition)).astype(jnp.bfloat16)
    one_hot = (labels[:, None] == jnp.arange(class_table.shape[0])[None, :]).astype(jnp.bfloat16)
    class_grad = jnp.einsum("bc,bd->cd", one_hot, cond_grad, preferred_element_type=jnp.float32)
    pre_grad = (
        jnp.einsum("be,de->bd", cond_grad, embed_weight, preferred_element_type=jnp.float32)
        * silu_slope(pre_hidden)
    ).astype(jnp.bfloat16)
    bias_wide = lax.dynamic_update_slice_in_dim(
        jnp.zeros((6, width), jnp.float32), modulate_bias_part, lane * slab, 1
    )
    output_bias_grad, down_bias_grad, query_gain_grad, key_gain_grad, modulate_bias_grad = lax.psum(
        (output_bias_part, down_bias_part, query_gain_part, key_gain_part, bias_wide),
        ("dp", "tensor"),
    )
    modulate_local = jnp.einsum(
        "bd,bke->dke", cond_act, modulation_grad, preferred_element_type=jnp.float32
    )
    embed_local = jnp.einsum(
        "bd,be->de", time_hidden, cond_grad, preferred_element_type=jnp.float32
    )
    embed_bias_local = jnp.sum(cond_grad.astype(jnp.float32), axis=0)
    time_local = jnp.einsum("bf,bd->fd", time_feat, pre_grad, preferred_element_type=jnp.float32)
    time_bias_local = jnp.sum(pre_grad.astype(jnp.float32), axis=0)
    (
        project_grad,
        output_weight_grad,
        expand_grad,
        down_grad,
        class_grad,
        modulate_grad,
        time_grad,
        time_bias_grad,
        embed_grad,
        embed_bias_grad,
    ) = (
        lax.psum_scatter(project_grad, "dp", scatter_dimension=0, tiled=True),
        lax.psum_scatter(output_weight_grad, "dp", scatter_dimension=1, tiled=True),
        lax.psum_scatter(expand_grad, "dp", scatter_dimension=0, tiled=True),
        lax.psum_scatter(down_grad, "dp", scatter_dimension=1, tiled=True),
        lax.psum_scatter(class_grad, "dp", scatter_dimension=1, tiled=True),
        lax.psum_scatter(modulate_local, "dp", scatter_dimension=0, tiled=True),
        lax.psum_scatter(time_local, "dp", scatter_dimension=1, tiled=True),
        lax.psum_scatter(time_bias_local, "dp", scatter_dimension=0, tiled=True),
        lax.psum_scatter(embed_local, "dp", scatter_dimension=0, tiled=True),
        lax.psum_scatter(embed_bias_local, "dp", scatter_dimension=0, tiled=True),
    )
    return (
        result,
        tokens_grad,
        project_grad,
        query_gain_grad,
        key_gain_grad,
        output_weight_grad,
        output_bias_grad,
        expand_grad,
        down_grad,
        down_bias_grad,
        modulate_grad,
        modulate_bias_grad,
        time_grad,
        time_bias_grad,
        embed_grad,
        embed_bias_grad,
        class_grad,
    )


def solution(mesh):
    return jax.shard_map(
        shards,
        mesh=mesh,
        in_specs=(
            P(("dp", "tensor"), None, None),
            P("dp"),
            P("dp"),
            P("dp"),
            P(("dp", "tensor"), None, None),
            P(None, None, "tensor"),
            P(),
            P(),
            P("tensor", None),
            P(),
            P(None, None, "tensor"),
            P("tensor", None),
            P(),
            P(None, None, "tensor"),
            P(None, "tensor"),
            P(),
            P(),
            P(),
            P(),
            P(),
        ),
        out_specs=(
            P(("dp", "tensor"), None, None),
            P(("dp", "tensor"), None, None),
            P("dp", None, "tensor"),
            P(),
            P(),
            P("tensor", "dp"),
            P(),
            P("dp", None, "tensor"),
            P("tensor", "dp"),
            P(),
            P("dp", None, "tensor"),
            P(),
            P(None, "dp"),
            P("dp"),
            P("dp", None),
            P("dp"),
            P(None, "dp"),
        ),
        check_vma=False,
    )
```

profile of v0, /device:TPU:0, one launch (start us, length us, event | category | flops | bytes accessed | tf_op | source)
XLA Modules:
  0.0 962.7 jit_solution(16076023338928004156)
XLA Ops:
  23.1 44.6 %all_gather.15 = bf16[4,6,1152]{1,0,2:T(4,128)(2,1)} all-gather(bf16[4,6,288]{1,0,2:T(4,128)(2,1)S(1)} %copy.105), channel_id=1, replica_groups=mesh['dp'=8,'tensor'=4] {'tensor'}, dimensions={2}, use_global_device_ids=true | all-gather | bytes 69120 | tf_op jit(solution)/shard_map/all_gather | solution.py:113
  70.1 11.2 %all-gather.5.cloned.1.call-done = bf16[4,256,1152]{2,1,0:T(8,128)(2,1)} async-done(((bf16[1,256,1152]{2,1,0:T(8,128)(2,1)}), bf16[4,256,1152]{2,1,0:T(8,128)(2,1)}) %all-gather.5.cloned.1.call-update) | async-done | bytes 2359312 | tf_op jit(solution)/shard_map/all_gather | solution.py:112
  101.9 43.4 %reduce-scatter.13.cloned.1.call-done = bf16[1,256,1152]{2,1,0:T(8,128)(2,1)} async-done(((bf16[4,256,1152]{2,1,0:T(8,128)(2,1)}), bf16[1,256,1152]{2,1,0:T(8,128)(2,1)}) %reduce-scatter.13.cloned.1.call-update) | async-done | bytes 589840 | tf_op jit(solution)/shard_map/reduce_scatter | solution.py:142
  153.1 46.1 %all-gather.7.cloned.1.call-done = bf16[4,256,1152]{2,1,0:T(8,128)(2,1)} async-done(((bf16[1,256,1152]{2,1,0:T(8,128)(2,1)}), bf16[4,256,1152]{2,1,0:T(8,128)(2,1)}) %all-gather.7.cloned.1.call-update) | async-done | bytes 2359312 | tf_op jit(solution)/shard_map/all_gather | solution.py:155
  199.2 9.6 fusion.7
  208.8 41.2 %all-gather.9.cloned.1.call-done = bf16[4,256,1152]{2,1,0:T(8,128)(2,1)} async-done(((bf16[1,256,1152]{2,1,0:T(8,128)(2,1)}), bf16[4,256,1152]{2,1,0:T(8,128)(2,1)}) %all-gather.9.cloned.1.call-update) | async-done | bytes 2359312 | tf_op jit(solution)/shard_map/all_gather | solution.py:175
  250.0 8.4 fusion.30
  260.1 5.5 bitcast_convert_fusion.1
  265.7 5.6 convolution_convert_fusion
  272.8 39.5 %reduce-scatter.17.cloned.1.call-done = bf16[1,256,1152]{2,1,0:T(8,128)(2,1)} async-done(((bf16[4,256,1152]{2,1,0:T(8,128)(2,1)}), bf16[1,256,1152]{2,1,0:T(8,128)(2,1)}) %reduce-scatter.17.cloned.1.call-update) | async-done | bytes 589840 | tf_op jit(solution)/shard_map/reduce_scatter | solution.py:187
  316.8 44.8 %reduce-scatter.15.cloned.1.call-done = bf16[1,256,1152]{2,1,0:T(8,128)(2,1)} async-done(((bf16[4,256,1152]{2,1,0:T(8,128)(2,1)}), bf16[1,256,1152]{2,1,0:T(8,128)(2,1)}) %reduce-scatter.15.cloned.1.call-update) | async-done | bytes 589840 | tf_op jit(solution)/shard_map/reduce_scatter | solution.py:163
  361.5 4.4 multiply_reduce_fusion.3
  368.5 49.5 %all-gather.11.cloned.1.call-done = bf16[4,256,1152]{2,1,0:T(8,128)(2,1)} async-done(((bf16[1,256,1152]{2,1,0:T(8,128)(2,1)}), bf16[4,256,1152]{2,1,0:T(8,128)(2,1)}) %all-gather.11.cloned.1.call-update) | async-done | bytes 2359312 | tf_op jit(solution)/shard_map/all_gather | solution.py:200
  435.0 4.1 bitcast_convert_fusion
  439.4 9.4 convolution_bitcast_fusion
  448.9 5.9 convolution_bitcast_fusion.2
  454.9 4.6 convolution_bitcast_fusion.3
  460.2 8.2 convolution_bitcast_fusion.1
  469.2 16.6 %reduce-scatter.19.cloned.1.call-done = bf16[1,256,1152]{2,1,0:T(8,128)(2,1)} async-done(((bf16[4,256,1152]{2,1,0:T(8,128)(2,1)}), bf16[1,256,1152]{2,1,0:T(8,128)(2,1)}) %reduce-scatter.19.cloned.1.call-update) | async-done | bytes 589840 | tf_op jit(solution)/shard_map/reduce_scatter | solution.py:239
  489.9 7.7 reduce.24
  498.6 8.8 all_to_all.4
  513.0 16.3 %psum.47 = f32[4,1152]{1,0:T(4,128)S(1)} all-reduce(f32[4,1152]{1,0:T(4,128)S(1)} %convolution_bitcast_fusion.4), channel_id=1, replica_groups=mesh['dp'=8,'tensor'=4] {'tensor'}, use_global_device_ids=true, to_apply=%region_42.43 | all-reduce | flops 4608 | bytes 36864 | tf_op jit(solution)/shard_map/psum | solution.py:269
  538.1 5.7 fusion.63
  545.7 8.4 reduce-scatter.25.cloned.1.call-done
  558.5 22.9 %all-reduce.15 = (f32[1152]{0:T(1024)S(1)}, f32[1152]{0:T(1024)S(1)}) all-reduce(f32[1152]{0:T(1024)S(1)} %get-tuple-element.164, f32[1152]{0:T(1024)S(1)} %get-tuple-element.110), channel_id=12, replica_groups=mesh['dp'=8,'tensor'=4] {'dp'}, use_global_device_ids=true, to_apply=%region_45.46.clone | all-reduce | flops 2304 | bytes 18432
  583.0 40.8 %all-reduce.14 = (f32[72]{0:T(128)}, f32[72]{0:T(128)}, f32[1152]{0:T(1024)}, f32[1152]{0:T(1024)}, f32[6,1152]{1,0:T(8,128)}) all-reduce(f32[72]{0:T(128)S(1)} %copy-done.80, f32[72]{0:T(128)S(1)} %copy-done.79, f32[1152]{0:T(1024)S(1)} %copy-done.51, f32[1152]{0:T(1024)S(1)} %copy-done.50, ...), channel_id=1, replica_groups=mesh['dp'=8,'tensor'=4] {'dp','tensor'}, use_global_device_ids=true, to_apply=%region_23.24 | all-reduce | flops 9360 | bytes 74880 | tf_op jit(solution)/shard_map/psum | solution.py:280
  623.9 26.0 %reduce-scatter.23.cloned.1.call-done = f32[288,144]{0,1:T(8,128)} async-done(((f32[288,1152]{0,1:T(8,128)}), f32[288,144]{0,1:T(8,128)}) %reduce-scatter.23.cloned.1.call-update) | async-done | bytes 165904 | tf_op jit(solution)/shard_map/reduce_scatter | solution.py:306
  649.8 60.7 %reduce-scatter.21.cloned.1.call-done = f32[144,3,288]{2,0,1:T(8,128)} async-done(((f32[1152,3,288]{2,0,1:T(8,128)}), f32[144,3,288]{2,0,1:T(8,128)}) %reduce-scatter.21.cloned.1.call-update) | async-done | bytes 497680 | tf_op jit(solution)/shard_map/reduce_scatter | solution.py:305
  710.5 40.5 %reduce-scatter.31.cloned.1.call-done = f32[256,144]{0,1:T(8,128)} async-done(((f32[256,1152]{0,1:T(8,128)}), f32[256,144]{0,1:T(8,128)}) %reduce-scatter.31.cloned.1.call-update) | async-done | bytes 147472 | tf_op jit(solution)/shard_map/reduce_scatter | solution.py:311
  751.0 57.7 %reduce-scatter.35.cloned.1.call-done = f32[1000,144]{0,1:T(8,128)} async-done(((f32[1000,1152]{0,1:T(8,128)}), f32[1000,144]{0,1:T(8,128)}) %reduce-scatter.35.cloned.1.call-update) | async-done | bytes 576016 | tf_op jit(solution)/shard_map/reduce_scatter | solution.py:309
  808.7 60.7 %reduce-scatter.33.cloned.1.call-done = f32[144,1152]{1,0:T(8,128)} async-done(((f32[1152,1152]{1,0:T(8,128)}), f32[144,1152]{1,0:T(8,128)}) %reduce-scatter.33.cloned.1.call-update) | async-done | bytes 663568 | tf_op jit(solution)/shard_map/reduce_scatter | solution.py:313
  869.4 86.3 %reduce-scatter.29.cloned.1.call-done = f32[144,6,288]{2,0,1:T(8,128)} async-done(((f32[1152,6,288]{2,0,1:T(8,128)}), f32[144,6,288]{2,0,1:T(8,128)}) %reduce-scatter.29.cloned.1.call-update) | async-done | bytes 995344 | tf_op jit(solution)/shard_map/reduce_scatter | solution.py:310
  (314 shorter events, 100.8 us)
Async XLA Ops:
  7.2 74.1 %all-gather.5.cloned.1.call-start = ((), (), s32[]{:S(2)}) async-start(), calls=%async_computation.13 | async-start | bytes 2949120 | tf_op jit(solution)/shard_map/all_gather | solution.py:112
  7.9 137.3 %reduce-scatter.13.cloned.1.call-start = ((), (), s32[]{:S(2)}) async-start(), calls=%async_computation.14 | async-start | bytes 2949120 | tf_op jit(solution)/shard_map/reduce_scatter | solution.py:142
  8.7 79.7 %copy-start.70 = (f32[72]{0:T(128)}, f32[72]{0:T(128)S(1)}, u32[]{:S(2)}) copy-start(f32[72]{0:T(128)S(1)} %convert_element_type.252) | copy-start | bytes 868
  9.3 79.3 %copy-start.72 = (f32[72]{0:T(128)}, f32[72]{0:T(128)S(1)}, u32[]{:S(2)}) copy-start(f32[72]{0:T(128)S(1)} %convert_element_type.255) | copy-start | bytes 868
  69.7 14.7 %copy-start.39 = (f32[4,6,1152]{2,0,1:T(4,128)}, f32[4,6,1152]{2,0,1:T(4,128)S(1)}, u32[]{:S(2)}) copy-start(f32[4,6,1152]{2,0,1:T(4,128)S(1)} %convert_element_type.248) | copy-start | bytes 331780
  70.1 14.4 %copy-start.54 = (f32[4,1152]{1,0:T(4,128)}, f32[4,1152]{1,0:T(4,128)S(1)}, u32[]{:S(2)}) copy-start(f32[4,1152]{1,0:T(4,128)S(1)} %get-tuple-element.150) | copy-start | bytes 55300
  70.1 14.4 %copy-start.56 = (f32[4,1152]{1,0:T(4,128)}, f32[4,1152]{1,0:T(4,128)S(1)}, u32[]{:S(2)}) copy-start(f32[4,1152]{1,0:T(4,128)S(1)} %get-tuple-element.151) | copy-start | bytes 55300
  98.6 46.7 %copy-start.3 = (bf16[1,256,1152]{2,1,0:T(8,128)(2,1)S(1)}, bf16[1,256,1152]{2,1,0:T(8,128)(2,1)}, u32[]{:S(2)}) copy-start(bf16[1,256,1152]{2,1,0:T(8,128)(2,1)} %param.20) | copy-start | bytes 1769476
  98.6 100.6 %all-gather.7.cloned.1.call-start = ((), (), s32[]{:S(2)}) async-start(), calls=%async_computation.15 | async-start | bytes 2949120 | tf_op jit(solution)/shard_map/all_gather | solution.py:155
  149.7 100.3 %all-gather.9.cloned.1.call-start = ((), (), s32[]{:S(2)}) async-start(), calls=%async_computation.17 | async-start | bytes 2949120 | tf_op jit(solution)/shard_map/all_gather | solution.py:175
  153.1 159.1 %reduce-scatter.17.cloned.1.call-start = ((), (), s32[]{:S(2)}) async-start(), calls=%async_computation.18 | async-start | bytes 2949120 | tf_op jit(solution)/shard_map/reduce_scatter | solution.py:187
  265.6 95.9 %reduce-scatter.15.cloned.1.call-start = ((), (), s32[]{:S(2)}) async-start(), calls=%async_computation.16 | async-start | bytes 2949120 | tf_op jit(solution)/shard_map/reduce_scatter | solution.py:163
  271.2 146.7 %all-gather.11.cloned.1.call-start = ((), (), s32[]{:S(2)}) async-start(), calls=%async_computation.19 | async-start | bytes 2949120 | tf_op jit(solution)/shard_map/all_gather | solution.py:200
  368.5 117.4 %reduce-scatter.19.cloned.1.call-start = ((), (), s32[]{:S(2)}) async-start(), calls=%async_computation.20 | async-start | bytes 2949120 | tf_op jit(solution)/shard_map/reduce_scatter | solution.py:239
  439.2 115.0 %reduce-scatter.25.cloned.1.call-start = ((), (), s32[]{:S(2)}) async-start(), calls=%async_computation.23 | async-start | bytes 7962624 | tf_op jit(solution)/shard_map/reduce_scatter | solution.py:307
  448.9 175.0 %reduce-scatter.27.cloned.1.call-start = ((), (), s32[]{:S(2)}) async-start(), calls=%async_computation.24 | async-start | bytes 3981312 | tf_op jit(solution)/shard_map/reduce_scatter | solution.py:308
  454.9 194.9 %reduce-scatter.23.cloned.1.call-start = ((), (), s32[]{:S(2)}) async-start(), calls=%async_computation.22 | async-start | bytes 1990656 | tf_op jit(solution)/shard_map/reduce_scatter | solution.py:306
  459.5 250.9 %reduce-scatter.21.cloned.1.call-start = ((), (), s32[]{:S(2)}) async-start(), calls=%async_computation.21 | async-start | bytes 5971968 | tf_op jit(solution)/shard_map/reduce_scatter | solution.py:305
  468.4 17.4 %copy-start.49 = (f32[1152]{0:T(1024)S(1)}, f32[1152]{0:T(1024)}, u32[]{:S(2)}) copy-start(f32[1152]{0:T(1024)} %get-tuple-element.98) | copy-start | bytes 13828
  468.5 17.4 %copy-start.64 = (f32[256]{0:T(256)S(1)}, f32[256]{0:T(256)}, u32[]{:S(2)}) copy-start(f32[256]{0:T(256)} %broadcast_multiply_fusion.3) | copy-start | bytes 3076
  468.5 282.5 %reduce-scatter.31.cloned.1.call-start = ((), (), s32[]{:S(2)}) async-start(), calls=%async_computation.26 | async-start | bytes 1327104 | tf_op jit(solution)/shard_map/reduce_scatter | solution.py:311
  510.2 19.1 %copy-start.36 = (f32[4,1152]{1,0:T(4,128)S(1)}, f32[4,1152]{1,0:T(4,128)}, u32[]{:S(2)}) copy-start(f32[4,1152]{1,0:T(4,128)} %copy-done.35) | copy-start | bytes 55300
  510.2 19.1 %copy-start.38 = (f32[4,1152]{1,0:T(4,128)S(1)}, f32[4,1152]{1,0:T(4,128)}, u32[]{:S(2)}) copy-start(f32[4,1152]{1,0:T(4,128)} %copy-done.37) | copy-start | bytes 55300
  513.0 17.2 %copy-start.67 = (bf16[4,128]{1,0:T(4,128)(2,1)S(1)}, bf16[4,128]{1,0:T(4,128)(2,1)}, u32[]{:S(2)}) copy-start(bf16[4,128]{1,0:T(4,128)(2,1)} %copy-done.66) | copy-start | bytes 3076
  513.0 17.2 %copy-start.69 = (bf16[4,128]{1,0:T(4,128)(2,1)S(1)}, bf16[4,128]{1,0:T(4,128)(2,1)}, u32[]{:S(2)}) copy-start(bf16[4,128]{1,0:T(4,128)(2,1)} %copy-done.68) | copy-start | bytes 3076
  531.6 277.0 %reduce-scatter.35.cloned.1.call-start = ((), (), s32[]{:S(2)}) async-start(), calls=%async_computation.28 | async-start | bytes 5308416 | tf_op jit(solution)/shard_map/reduce_scatter | solution.py:309
  534.7 334.7 %reduce-scatter.33.cloned.1.call-start = ((), (), s32[]{:S(2)}) async-start(), calls=%async_computation.27 | async-start | bytes 5971968 | tf_op jit(solution)/shard_map/reduce_scatter | solution.py:313
  538.1 417.7 %reduce-scatter.29.cloned.1.call-start = ((), (), s32[]{:S(2)}) async-start(), calls=%async_computation.25 | async-start | bytes 11943936 | tf_op jit(solution)/shard_map/reduce_scatter | solution.py:310
  557.1 25.9 %copy-start.50 = (f32[1152]{0:T(1024)S(1)}, f32[1152]{0:T(1024)}, u32[]{:S(2)}) copy-start(f32[1152]{0:T(1024)} %get-tuple-element.114) | copy-start | bytes 13828
  557.1 25.9 %copy-start.51 = (f32[1152]{0:T(1024)S(1)}, f32[1152]{0:T(1024)}, u32[]{:S(2)}) copy-start(f32[1152]{0:T(1024)} %get-tuple-element.116) | copy-start | bytes 13828
  557.1 25.9 %copy-start.79 = (f32[72]{0:T(128)S(1)}, f32[72]{0:T(128)}, u32[]{:S(2)}) copy-start(f32[72]{0:T(128)} %get-tuple-element.85) | copy-start | bytes 868
  557.1 25.9 %copy-start.80 = (f32[72]{0:T(128)S(1)}, f32[72]{0:T(128)}, u32[]{:S(2)}) copy-start(f32[72]{0:T(128)} %get-tuple-element.87) | copy-start | bytes 868
  (73 other events, 167.5 us)
Sparse Core Ops, SparseCore 0:
  9.6 71.6 all-gather.4
  98.7 46.4 reduce-scatter.12
  149.8 49.3 all-gather.6
  201.2 48.7 all-gather.8
  265.7 46.4 reduce-scatter.16
  314.4 47.0 reduce-scatter.14
  368.6 49.3 all-gather.10
  439.3 46.4 reduce-scatter.18
  489.3 64.7 reduce-scatter.24
  558.1 48.4 reduce-scatter.26
  610.5 39.2 reduce-scatter.22
  653.7 56.7 reduce-scatter.20
  714.3 36.6 reduce-scatter.30
  754.9 53.7 reduce-scatter.34
  812.5 56.8 reduce-scatter.32
  873.4 82.3 reduce-scatter.28
where the time goes:
time: 972 us; the launch traced here: 963 us
  waiting for transfers between devices  633 us (65%)
  blocking collectives  133 us (14%)
  matrix products  99 us (10%)
  other arithmetic  47.9 us (5%)
  local copies, waits for them, and re-layouts  30.3 us (3%)
  between operations  16.9 us (2%)
    reduce_scatter x1, waiting for transfers between devices, shards(): lax.psum_scatter(modulate_local, 'dp', scatter_dimension=0, tiled=True)  86.3 us
    reduce_scatter x1, waiting for transfers between devices, shards(): lax.psum_scatter(embed_local, 'dp', scatter_dimension=0, tiled=True)  60.7 us
    reduce_scatter x1, waiting for transfers between devices, shards(): lax.psum_scatter(project_grad, 'dp', scatter_dimension=0, tiled=True)  60.7 us
    reduce_scatter x1, waiting for transfers between devices, shards(): lax.psum_scatter(class_grad, 'dp', scatter_dimension=1, tiled=True)  57.7 us
    all_gather x1, waiting for transfers between devices, shards(): piece = lax.all_gather(attend_grad, 'tensor', axis=0, tiled=True)  49.5 us
    all_gather x1, waiting for transfers between devices, shards(): mod_two_all = lax.all_gather(mod_two, 'tensor', axis=0, tiled=True)  46.1 us
    reduce_scatter x1, waiting for transfers between devices, shards(): lax.psum_scatter(jnp.einsum('blf,fd->bld', piece, down_weight, preferred_...  44.8 us
    all_gather x1, blocking collectives, shards(): lax.all_gather(modulation_part, 'tensor', axis=2, tiled=True)  44.6 us
  transfers between devices with their start and end apart: 16, of which 15 were waited for; matrix products, arithmetic and copies ran while one was open for 11% of the time, Pallas kernels for 0%

commit v1 on v0

--- a/solution.py
+++ b/solution.py
@@ -93,7 +93,9 @@
     live = (first_item + jnp.arange(local_items) < item_counts[0]).astype(jnp.float32)[
         :, None, None
     ]
-    time_feat = time_features(timesteps).astype(jnp.bfloat16)
+    index = lax.axis_index("dp")
+    tags = lax.all_gather(jnp.stack([timesteps, labels]), "dp", axis=1, tiled=True)
+    time_feat = time_features(tags[0]).astype(jnp.bfloat16)
     pre_hidden = jnp.dot(
         time_feat, time_weight, preferred_element_type=jnp.float32
     ) + time_bias.astype(jnp.float32)
@@ -101,26 +103,29 @@
     condition = (
         jnp.dot(time_hidden, embed_weight, preferred_element_type=jnp.float32)
         + embed_bias.astype(jnp.float32)
-        + jnp.take(class_table, labels, axis=0).astype(jnp.float32)
+        + jnp.take(class_table, tags[1], axis=0).astype(jnp.float32)
     )
     cond_act = jax.nn.silu(condition).astype(jnp.bfloat16)
+    cond_act_here = lax.dynamic_slice_in_dim(cond_act, index * items, items, 0)
+    condition_here = lax.dynamic_slice_in_dim(condition, index * items, items, 0)
     modulation_part = (
-        jnp.einsum("bd,dke->bke", cond_act, modulate_weight, preferred_element_type=jnp.float32)
+        jnp.einsum("bd,dke->bke", cond_act_here, modulate_weight, preferred_element_type=jnp.float32)
         + modulate_bias.astype(jnp.float32)
     ).astype(jnp.bfloat16)
-    token_all, modulation = (
-        lax.all_gather(tokens, "tensor", axis=0, tiled=True),
-        lax.all_gather(modulation_part, "tensor", axis=2, tiled=True),
-    )
-    modulation = modulation.astype(jnp.float32)
-    modulation_local = lax.dynamic_slice_in_dim(modulation, first_item, local_items, 0)
-    attend_shift_all = modulation[:, 0][:, None, :]
-    attend_scale_all = modulation[:, 1][:, None, :]
+    modulation_local = lax.all_to_all(
+        modulation_part, "tensor", split_axis=0, concat_axis=2, tiled=True
+    ).astype(jnp.float32)
     local_parts = [modulation_local[:, which][:, None, :] for which in range(6)]
-    _, attend_scale, attend_gate, feed_shift, feed_scale, feed_gate = local_parts
+    attend_shift, attend_scale, attend_gate, feed_shift, feed_scale, feed_gate = local_parts
     positions = jnp.arange(length)
-    normed_all, _ = layer_norm(token_all.astype(jnp.float32))
-    mod_in = (normed_all * (1.0 + attend_scale_all) + attend_shift_all).astype(jnp.bfloat16)
+    token_local = tokens.astype(jnp.float32)
+    normed_local, inverse_local = layer_norm(token_local)
+    mod_in = lax.all_gather(
+        (normed_local * (1.0 + attend_scale) + attend_shift).astype(jnp.bfloat16),
+        "tensor",
+        axis=0,
+        tiled=True,
+    )
     projected = jnp.einsum(
         "bld,dke->blke", mod_in, project_weight, preferred_element_type=jnp.float32
     )
@@ -147,8 +152,6 @@
         scatter_dimension=0,
         tiled=True,
     ).astype(jnp.float32) + output_bias.astype(jnp.float32)
-    token_local = tokens.astype(jnp.float32)
-    normed_local, inverse_local = layer_norm(token_local)
     residual = token_local + attend_gate * attend_branch
     normed_two, inverse_two = layer_norm(residual)
     mod_two = (normed_two * (1.0 + feed_scale) + feed_shift).astype(jnp.bfloat16)
@@ -267,52 +270,65 @@
         "bke,dke->bd", modulation_grad, modulate_weight, preferred_element_type=jnp.float32
     )
     cond_total = lax.psum(cond_part, "tensor")
-    cond_grad = (cond_total * silu_slope(condition)).astype(jnp.bfloat16)
-    one_hot = (labels[:, None] == jnp.arange(class_table.shape[0])[None, :]).astype(jnp.bfloat16)
-    class_grad = jnp.einsum("bc,bd->cd", one_hot, cond_grad, preferred_element_type=jnp.float32)
+    cond_grad_here = (cond_total * silu_slope(condition_here)).astype(jnp.bfloat16)
+    packed = jnp.concatenate([cond_grad_here, modulation_grad.reshape(items, 6 * slab)], axis=1)
+    packed = lax.all_gather(packed, "dp", axis=0, tiled=True)
+    cond_grad = packed[:, :width]
+    modulation_grad_all = packed[:, width:].reshape(-1, 6, slab)
+    share = width // lax.axis_size("dp")
+
+    def mine(value, axis):
+        return lax.dynamic_slice_in_dim(value, index * share, share, axis)
+
+    one_hot = (tags[1][:, None] == jnp.arange(class_table.shape[0])[None, :]).astype(jnp.bfloat16)
+    cond_grad_mine = mine(cond_grad, 1)
+    class_grad = jnp.einsum(
+        "bc,bd->cd", one_hot, cond_grad_mine, preferred_element_type=jnp.float32
+    )
     pre_grad = (
-        jnp.einsum("be,de->bd", cond_grad, embed_weight, preferred_element_type=jnp.float32)
-        * silu_slope(pre_hidden)
-    ).astype(jnp.bfloat16)
+        jnp.einsum(
+            "be,de->bd", cond_grad, mine(embed_weight, 0), preferred_element_type=jnp.float32
+        )
+        * silu_slope(mine(pre_hidden, 1))
+    ).astype(jnp.bfloat16)
+    modulate_grad = jnp.einsum(
+        "bd,bke->dke", mine(cond_act, 1), modulation_grad_all, preferred_element_type=jnp.float32
+    )
+    embed_grad = jnp.einsum(
+        "bd,be->de", mine(time_hidden, 1), cond_grad, preferred_element_type=jnp.float32
+    )
+    embed_bias_grad = jnp.sum(cond_grad_mine.astype(jnp.float32), axis=0)
+    time_grad = jnp.einsum("bf,bd->fd", time_feat, pre_grad, preferred_element_type=jnp.float32)
+    time_bias_grad = jnp.sum(pre_grad.astype(jnp.float32), axis=0)
     bias_wide = lax.dynamic_update_slice_in_dim(
         jnp.zeros((6, width), jnp.float32), modulate_bias_part, lane * slab, 1
     )
-    output_bias_grad, down_bias_grad, query_gain_grad, key_gain_grad, modulate_bias_grad = lax.psum(
-        (output_bias_part, down_bias_part, query_gain_part, key_gain_part, bias_wide),
-        ("dp", "tensor"),
-    )
-    modulate_local = jnp.einsum(
-        "bd,bke->dke", cond_act, modulation_grad, preferred_element_type=jnp.float32
-    )
-    embed_local = jnp.einsum(
-        "bd,be->de", time_hidden, cond_grad, preferred_element_type=jnp.float32
-    )
-    embed_bias_local = jnp.sum(cond_grad.astype(jnp.float32), axis=0)
-    time_local = jnp.einsum("bf,bd->fd", time_feat, pre_grad, preferred_element_type=jnp.float32)
-    time_bias_local = jnp.sum(pre_grad.astype(jnp.float32), axis=0)
-    (
-        project_grad,
-        output_weight_grad,
-        expand_grad,
-        down_grad,
-        class_grad,
-        modulate_grad,
-        time_grad,
-        time_bias_grad,
-        embed_grad,
-        embed_bias_grad,
-    ) = (
-        lax.psum_scatter(project_grad, "dp", scatter_dimension=0, tiled=True),
-        lax.psum_scatter(output_weight_grad, "dp", scatter_dimension=1, tiled=True),
-        lax.psum_scatter(expand_grad, "dp", scatter_dimension=0, tiled=True),
-        lax.psum_scatter(down_grad, "dp", scatter_dimension=1, tiled=True),
-        lax.psum_scatter(class_grad, "dp", scatter_dimension=1, tiled=True),
-        lax.psum_scatter(modulate_local, "dp", scatter_dimension=0, tiled=True),
-        lax.psum_scatter(time_local, "dp", scatter_dimension=1, tiled=True),
-        lax.psum_scatter(time_bias_local, "dp", scatter_dimension=0, tiled=True),
-        lax.psum_scatter(embed_local, "dp", scatter_dimension=0, tiled=True),
-        lax.psum_scatter(embed_bias_local, "dp", scatter_dimension=0, tiled=True),
-    )
+    small = jnp.concatenate(
+        [
+            output_bias_part,
+            down_bias_part,
+            bias_wide.reshape(-1),
+            query_gain_part,
+            key_gain_part,
+        ]
+    )
+    small = lax.psum(small, ("dp", "tensor"))
+    output_bias_grad = small[:width]
+    down_bias_grad = small[width : 2 * width]
+    modulate_bias_grad = small[2 * width : 8 * width].reshape(6, width)
+    query_gain_grad = small[8 * width : 8 * width + HD]
+    key_gain_grad = small[8 * width + HD :]
+
+    def scatter(value, axis):
+        value = value.astype(jnp.bfloat16)
+        return lax.psum_scatter(value, "dp", scatter_dimension=axis, tiled=True).astype(
+            jnp.float32
+        )
+
+    project_grad = scatter(project_grad, 0)
+    output_weight_grad = scatter(output_weight_grad, 1)
+    expand_grad = scatter(expand_grad, 0)
+    down_grad = scatter(down_grad, 1)
     return (
         result,
         tokens_grad,

time: 972 us -> 774 us (0.80)
  waiting for transfers between devices: 633 us -> 480 us
  blocking collectives: 133 us -> 77.2 us
  starting transfers between devices: 1.76 us -> 20.2 us
    reduce_scatter x8 -> x4, waiting for transfers between devices: 340 us -> 134 us  [scatter(): lax.psum_scatter(value, 'dp', scatter_dimension=axis, tiled=True)]
    all_gather x1, waiting for transfers between devices: 11.2 us -> 47.1 us  [shards(): lax.all_gather((normed_local * (1.0 + attend_scale) + attend_shift).astyp...]
    reduce_scatter x1, waiting for transfers between devices: 16.6 us -> 48 us  [shards(): lax.psum_scatter(jnp.einsum('blke,dke->bld', piece, project_weight, prefe...]
    all_gather x1, waiting for transfers between devices: 49.5 us -> 24.6 us  [shards(): piece = lax.all_gather(attend_grad, 'tensor', axis=0, tiled=True)]
    all_gather x1 -> x2, blocking collectives: 44.6 us -> 20.4 us  [the longest x1 10.4 us: shards(): lax.all_gather(jnp.stack([timesteps, labels]), 'dp', axis=1, tiled=True)]
    unnamed x1 -> x0, blocking collectives: 22.9 us -> none
    reduce_scatter x8 -> x4, starting transfers between devices: 0.8 us -> 11.3 us  [scatter(): lax.psum_scatter(value, 'dp', scatter_dimension=axis, tiled=True)]
    unnamed x185 -> x172, local copies, waits for them, and re-layouts: 22.1 us -> 17.4 us
  transfers between devices with their start and end apart: 16 -> 14, of which waited for: 15 -> 14; matrix products, arithmetic and copies ran while one was open for 11% -> 11% of each run, Pallas kernels for 0% -> 0%
where the time goes in v1:
time: 774 us; the launch traced here: 764 us
  waiting for transfers between devices  480 us (62%)
  matrix products  92 us (12%)
  blocking collectives  77.2 us (10%)
  other arithmetic  53.3 us (7%)
  local copies, waits for them, and re-layouts  25.5 us (3%)
  starting transfers between devices  20.2 us (3%)
  between operations  16.4 us (2%)
    reduce_scatter x4, waiting for transfers between devices, scatter(): lax.psum_scatter(value, 'dp', scatter_dimension=axis, tiled=True)  134 us
    reduce_scatter x1, waiting for transfers between devices, shards(): lax.psum_scatter(jnp.einsum('blke,dke->bld', piece, project_weight, prefe...  48 us
    all_gather x1, waiting for transfers between devices, shards(): lax.all_gather((normed_local * (1.0 + attend_scale) + attend_shift).astyp...  47.1 us
    all_gather x1, waiting for transfers between devices, shards(): mod_two_all = lax.all_gather(mod_two, 'tensor', axis=0, tiled=True)  45.8 us
    reduce_scatter x1, waiting for transfers between devices, shards(): lax.psum_scatter(jnp.einsum('blf,fd->bld', piece, down_weight, preferred_...  45.5 us
    reduce_scatter x1, waiting for transfers between devices, shards(): lax.psum_scatter(jnp.einsum('blh,hd->bld', piece, output_weight, preferre...  45.3 us
    all_gather x1, waiting for transfers between devices, shards(): piece = lax.all_gather(branch_grad, 'tensor', axis=0, tiled=True)  41.2 us
    psum x1, blocking collectives, shards(): small = lax.psum(small, ('dp', 'tensor'))  39.6 us
  transfers between devices with their start and end apart: 14, of which 14 were waited for; matrix products, arithmetic and copies ran while one was open for 11% of the time, Pallas kernels for 0%

profile of v1, /device:TPU:0, one launch (start us, length us, event | category | flops | bytes accessed | tf_op | source)
XLA Modules:
  0.0 764.2 jit_solution(1192706459011180409)
XLA Ops:
  8.1 10.4 %all-gather = s32[8,4,2]{1,2,0:T(2,128)S(1)} all-gather(s32[1,4,2]{1,2,0:T(2,128)S(1)} %add_bitcast_fusion), channel_id=1, replica_groups=mesh['dp'=8,'tensor'=4] {'dp'}, dimensions={0}, use_global_device_ids=true | all-gather | bytes 288 | tf_op jit(solution)/shard_map/all_gather | solution.py:97
  29.4 4.9 all-to-all-start
  34.8 5.1 all-to-all-done
  42.8 47.1 %all-gather.7.cloned.1.call-done = bf16[4,256,1152]{2,1,0:T(8,128)(2,1)} async-done(((bf16[1,256,1152]{2,1,0:T(8,128)(2,1)}), bf16[4,256,1152]{2,1,0:T(8,128)(2,1)}) %all-gather.7.cloned.1.call-update) | async-done | bytes 2359312 | tf_op jit(solution)/shard_map/all_gather | solution.py:123
  90.0 4.7 fusion.10
  107.8 45.3 %reduce-scatter.9.cloned.1.call-done = bf16[1,256,1152]{2,1,0:T(8,128)(2,1)} async-done(((bf16[4,256,1152]{2,1,0:T(8,128)(2,1)}), bf16[1,256,1152]{2,1,0:T(8,128)(2,1)}) %reduce-scatter.9.cloned.1.call-update) | async-done | bytes 589840 | tf_op jit(solution)/shard_map/reduce_scatter | solution.py:147
  160.6 45.8 %all-gather.9.cloned.1.call-done = bf16[4,256,1152]{2,1,0:T(8,128)(2,1)} async-done(((bf16[1,256,1152]{2,1,0:T(8,128)(2,1)}), bf16[4,256,1152]{2,1,0:T(8,128)(2,1)}) %all-gather.9.cloned.1.call-update) | async-done | bytes 2359312 | tf_op jit(solution)/shard_map/all_gather | solution.py:158
  206.4 9.6 %fusion.1 = f32[4,256,2,768]{3,1,2,0:T(8,128)} fusion(bf16[1152,2,768]{2,1,0:T(2,128)(2,1)} %param.30, bf16[4,256,1152]{2,1,0:T(8,128)(2,1)} %all-gather.9.cloned.1.call-done), kind=kOutput, calls=%fused_computation.14 | convolution fusion | flops 3623878656 | bytes 12189696 | tf_op jit(solution)/shard_map/bld,dkf->blkf/dot_general | solution.py:159
  216.0 41.2 %all-gather.11.cloned.1.call-done = bf16[4,256,1152]{2,1,0:T(8,128)(2,1)} async-done(((bf16[1,256,1152]{2,1,0:T(8,128)(2,1)}), bf16[4,256,1152]{2,1,0:T(8,128)(2,1)}) %all-gather.11.cloned.1.call-update) | async-done | bytes 2359312 | tf_op jit(solution)/shard_map/all_gather | solution.py:178
  257.2 8.4 %fusion.26 = (bf16[4,256,1,768]{3,1,0,2:T(8,128)(2,1)S(1)}, bf16[4,256,1,768]{3,1,0,2:T(8,128)(2,1)S(1)}, bf16[4,256,768]{2,1,0:T(8,128)(2,1)}) fusion(f32[4,256,2,768]{3,1,2,0:T(8,128)} %fusion.1, bf16[4,256,1152]{2,1,0:T(8,128)(2,1)} %all-gather.11.cloned.1.call-done, bf16[768,1152]{1,0:T(8,128)(2,1)} %param.31), kind=kOutput, calls=%fused_computation.62 | convolution fusion | flops 1823735808 | bytes 15138816 | tf_op jit(solution)/shard_map/bld,fd->blf/dot_general | solution.py:180
  267.2 5.6 bitcast_convert_fusion.3
  272.8 5.6 convolution_convert_fusion
  279.8 39.6 %reduce-scatter.13.cloned.1.call-done = bf16[1,256,1152]{2,1,0:T(8,128)(2,1)} async-done(((bf16[4,256,1152]{2,1,0:T(8,128)(2,1)}), bf16[1,256,1152]{2,1,0:T(8,128)(2,1)}) %reduce-scatter.13.cloned.1.call-update) | async-done | bytes 589840 | tf_op jit(solution)/shard_map/reduce_scatter | solution.py:190
  323.2 45.5 %reduce-scatter.11.cloned.1.call-done = bf16[1,256,1152]{2,1,0:T(8,128)(2,1)} async-done(((bf16[4,256,1152]{2,1,0:T(8,128)(2,1)}), bf16[1,256,1152]{2,1,0:T(8,128)(2,1)}) %reduce-scatter.11.cloned.1.call-update) | async-done | bytes 589840 | tf_op jit(solution)/shard_map/reduce_scatter | solution.py:166
  368.7 4.1 multiply_reduce_fusion.5
  375.4 11.2 %reduce-scatter.23.cloned.1.call-start = ((), (), s32[]{:S(2)}) async-start(), calls=%async_computation.21 | async-start | bytes 1990656 | tf_op jit(solution)/shard_map/reduce_scatter | solution.py:324
  386.6 5.4 fusion.4
  392.1 8.2 %bitcast_convert_fusion = bf16[1152,2,768]{2,0,1:T(8,128)(2,1)} fusion(bf16[4,256,1152]{2,1,0:T(8,128)(2,1)} %all-gather.9.cloned.1.call-done, bf16[4,256,1,768]{3,1,0,2:T(8,128)(2,1)} %copy-done.82, bf16[4,256,1,768]{3,1,0,2:T(8,128)(2,1)} %copy-done.81), kind=kOutput, calls=%fused_computation.1 | convolution fusion | flops 3631939584 | bytes 9043968 | tf_op jit(solution)/shard_map/bld,blkf->dkf/dot_general | solution.py:186
  400.4 24.6 %all-gather.13.cloned.1.call-done = bf16[4,256,1152]{2,1,0:T(8,128)(2,1)} async-done(((bf16[1,256,1152]{2,1,0:T(8,128)(2,1)}), bf16[4,256,1152]{2,1,0:T(8,128)(2,1)}) %all-gather.13.cloned.1.call-update) | async-done | bytes 2359312 | tf_op jit(solution)/shard_map/all_gather | solution.py:203
  445.4 3.5 convolution_convert_fusion.2
  449.8 5.3 bitcast_convert_fusion.1
  455.4 6.5 bitcast_convert_fusion.2
  461.9 4.4 reduce-scatter.23.cloned.1.call-done
  468.1 49.6 %reduce-scatter.21.cloned.1.call-done = bf16[144,2,768]{2,0,1:T(8,128)(2,1)} async-done(((bf16[1152,2,768]{2,0,1:T(8,128)(2,1)}), bf16[144,2,768]{2,0,1:T(8,128)(2,1)}) %reduce-scatter.21.cloned.1.call-update) | async-done | bytes 442384 | tf_op jit(solution)/shard_map/reduce_scatter | solution.py:324
  520.0 35.5 %reduce-scatter.19.cloned.1.call-done = bf16[288,144]{0,1:T(8,128)(2,1)} async-done(((bf16[288,1152]{0,1:T(8,128)(2,1)}), bf16[288,144]{0,1:T(8,128)(2,1)}) %reduce-scatter.19.cloned.1.call-update) | async-done | bytes 82960 | tf_op jit(solution)/shard_map/reduce_scatter | solution.py:324
  557.0 44.9 %reduce-scatter.17.cloned.1.call-done = bf16[144,3,288]{2,0,1:T(8,128)(2,1)} async-done(((bf16[1152,3,288]{2,0,1:T(8,128)(2,1)}), bf16[144,3,288]{2,0,1:T(8,128)(2,1)}) %reduce-scatter.17.cloned.1.call-update) | async-done | bytes 248848 | tf_op jit(solution)/shard_map/reduce_scatter | solution.py:324
  603.8 48.0 %reduce-scatter.15.cloned.1.call-done = bf16[1,256,1152]{2,1,0:T(8,128)(2,1)} async-done(((bf16[4,256,1152]{2,1,0:T(8,128)(2,1)}), bf16[1,256,1152]{2,1,0:T(8,128)(2,1)}) %reduce-scatter.15.cloned.1.call-update) | async-done | bytes 589840 | tf_op jit(solution)/shard_map/reduce_scatter | solution.py:242
  656.5 7.7 %reduce.26 = bf16[1152,6]{1,0:T(8,128)(2,1)S(1)} reduce(bf16[1152,1,6]{2,1,0:T(2,128)(2,1)} %bitcast.210, bf16[]{:T(256)} %broadcast.432), dimensions={1}, to_apply=%bitcast.178.reduce_sub_computation | reduce | bytes 27650
  665.2 3.3 all-to-all-start.1
  675.8 39.6 %psum.14 = f32[9360]{0:T(1024)S(1)} all-reduce(f32[9360]{0:T(1024)S(1)} %concatenate.23), channel_id=1, replica_groups=mesh['dp'=8,'tensor'=4] {'dp','tensor'}, use_global_device_ids=true, to_apply=%region_31.32 | all-reduce | flops 9360 | bytes 74880 | tf_op jit(solution)/shard_map/psum | solution.py:315
  719.4 17.1 %psum.15 = f32[4,1152]{1,0:T(4,128)S(1)} all-reduce(f32[4,1152]{1,0:T(4,128)S(1)} %convolution_bitcast_fusion.2), channel_id=1, replica_groups=mesh['dp'=8,'tensor'=4] {'tensor'}, use_global_device_ids=true, to_apply=%region_35.36 | all-reduce | flops 4608 | bytes 36864 | tf_op jit(solution)/shard_map/psum | solution.py:272
  737.5 10.0 %all-gather.1 = bf16[8,4,2880]{2,1,0:T(4,128)(2,1)S(1)} all-gather(bf16[1,4,2880]{2,1,0:T(4,128)(2,1)S(1)} %maximum_bitcast_fusion), channel_id=1, replica_groups=mesh['dp'=8,'tensor'=4] {'dp'}, dimensions={0}, use_global_device_ids=true | all-gather | bytes 207360 | tf_op jit(solution)/shard_map/all_gather | solution.py:275
  (309 shorter events, 100.1 us)
Async XLA Ops:
  7.2 19.0 %copy-start = (bf16[1152,1152]{1,0:T(8,128)(2,1)S(1)}, bf16[1152,1152]{1,0:T(8,128)(2,1)}, u32[]{:S(2)}) copy-start(bf16[1152,1152]{1,0:T(8,128)(2,1)} %param.37) | copy-start | bytes 7962628
  21.4 6.0 copy-start.54
  21.4 6.0 copy-start.56
  27.4 6.9 copy-start.3
  29.4 10.5 %all-to-all-start = ((bf16[4,6,288]{2,1,0:T(8,128)(2,1)}), bf16[4,6,288]{2,1,0:T(8,128)(2,1)S(1)}, u32[]{:S(2)}, u32[]{:S(2)}) async-start(bf16[4,6,288]{2,1,0:T(8,128)(2,1)} %copy.133), calls=%async_computation | async-start | bytes 49152 | tf_op jit(solution)/shard_map/all_to_all | solution.py:115
  34.3 55.7 %all-gather.7.cloned.1.call-start = ((), (), s32[]{:S(2)}) async-start(), calls=%async_computation.10 | async-start | bytes 2949120 | tf_op jit(solution)/shard_map/all_gather | solution.py:123
  34.4 8.0 %copy-start.58 = (f32[256]{0:T(256)}, f32[256]{0:T(256)S(1)}, u32[]{:S(2)}) copy-start(f32[256]{0:T(256)S(1)} %broadcast_multiply_fusion.5) | copy-start | bytes 3076
  34.8 7.7 %copy-start.79 = (bf16[72]{0:T(256)(128)(2,1)S(1)}, bf16[72]{0:T(256)(128)(2,1)}, u32[]{:S(2)}) copy-start(bf16[72]{0:T(256)(128)(2,1)} %param.26) | copy-start | bytes 436
  34.8 7.7 %copy-start.80 = (bf16[72]{0:T(256)(128)(2,1)S(1)}, bf16[72]{0:T(256)(128)(2,1)}, u32[]{:S(2)}) copy-start(bf16[72]{0:T(256)(128)(2,1)} %param.27) | copy-start | bytes 436
  34.8 59.9 %copy-start.61 = (f32[256]{0:T(256)}, f32[256]{0:T(256)S(1)}, u32[]{:S(2)}) copy-start(f32[256]{0:T(256)S(1)} %add_rsqrt_fusion.1) | copy-start | bytes 3076
  42.4 110.7 %reduce-scatter.9.cloned.1.call-start = ((), (), s32[]{:S(2)}) async-start(), calls=%async_computation.11 | async-start | bytes 2949120 | tf_op jit(solution)/shard_map/reduce_scatter | solution.py:147
  42.5 52.8 %copy-start.68 = (f32[72]{0:T(128)}, f32[72]{0:T(128)S(1)}, u32[]{:S(2)}) copy-start(f32[72]{0:T(128)S(1)} %convert_element_type.306) | copy-start | bytes 868
  42.5 53.9 %copy-start.70 = (f32[72]{0:T(128)}, f32[72]{0:T(128)S(1)}, u32[]{:S(2)}) copy-start(f32[72]{0:T(128)S(1)} %convert_element_type.309) | copy-start | bytes 868
  106.5 99.9 %all-gather.9.cloned.1.call-start = ((), (), s32[]{:S(2)}) async-start(), calls=%async_computation.12 | async-start | bytes 2949120 | tf_op jit(solution)/shard_map/all_gather | solution.py:158
  156.9 100.3 %all-gather.11.cloned.1.call-start = ((), (), s32[]{:S(2)}) async-start(), calls=%async_computation.14 | async-start | bytes 2949120 | tf_op jit(solution)/shard_map/all_gather | solution.py:178
  160.3 159.2 %reduce-scatter.13.cloned.1.call-start = ((), (), s32[]{:S(2)}) async-start(), calls=%async_computation.15 | async-start | bytes 2949120 | tf_op jit(solution)/shard_map/reduce_scatter | solution.py:190
  257.2 10.0 %copy-start.75 = (bf16[1152,2,768]{2,1,0:T(2,128)(2,1)S(1)}, bf16[1152,2,768]{2,1,0:T(2,128)(2,1)}, u32[]{:S(2)}) copy-start(bf16[1152,2,768]{2,1,0:T(2,128)(2,1)} %param.30) | copy-start | bytes 10616836
  272.8 95.9 %reduce-scatter.11.cloned.1.call-start = ((), (), s32[]{:S(2)}) async-start(), calls=%async_computation.13 | async-start | bytes 2949120 | tf_op jit(solution)/shard_map/reduce_scatter | solution.py:166
  278.5 146.5 %all-gather.13.cloned.1.call-start = ((), (), s32[]{:S(2)}) async-start(), calls=%async_computation.16 | async-start | bytes 2949120 | tf_op jit(solution)/shard_map/all_gather | solution.py:203
  375.4 90.9 %reduce-scatter.23.cloned.1.call-start = ((), (), s32[]{:S(2)}) async-start(), calls=%async_computation.21 | async-start | bytes 1990656 | tf_op jit(solution)/shard_map/reduce_scatter | solution.py:324
  392.0 125.7 %reduce-scatter.21.cloned.1.call-start = ((), (), s32[]{:S(2)}) async-start(), calls=%async_computation.20 | async-start | bytes 3981312 | tf_op jit(solution)/shard_map/reduce_scatter | solution.py:324
  400.3 155.1 %reduce-scatter.19.cloned.1.call-start = ((), (), s32[]{:S(2)}) async-start(), calls=%async_computation.19 | async-start | bytes 995328 | tf_op jit(solution)/shard_map/reduce_scatter | solution.py:324
  443.3 158.7 %reduce-scatter.17.cloned.1.call-start = ((), (), s32[]{:S(2)}) async-start(), calls=%async_computation.18 | async-start | bytes 2985984 | tf_op jit(solution)/shard_map/reduce_scatter | solution.py:324
  455.1 196.7 %reduce-scatter.15.cloned.1.call-start = ((), (), s32[]{:S(2)}) async-start(), calls=%async_computation.17 | async-start | bytes 2949120 | tf_op jit(solution)/shard_map/reduce_scatter | solution.py:242
  461.9 6.2 copy-start.64
  461.9 6.2 copy-start.63
  461.9 6.2 copy-start.67
  461.9 6.2 copy-start.66
  468.1 183.7 %copy-start.48 = (f32[1152]{0:T(1024)S(1)}, f32[1152]{0:T(1024)}, u32[]{:S(2)}) copy-start(f32[1152]{0:T(1024)} %copy-done.47) | copy-start | bytes 13828
  468.1 183.7 %copy-start.59 = (f32[256]{0:T(256)S(1)}, f32[256]{0:T(256)}, u32[]{:S(2)}) copy-start(f32[256]{0:T(256)} %copy-done.58) | copy-start | bytes 3076
  468.1 183.7 %copy-start.62 = (f32[256]{0:T(256)S(1)}, f32[256]{0:T(256)}, u32[]{:S(2)}) copy-start(f32[256]{0:T(256)} %copy-done.61) | copy-start | bytes 3076
  665.2 8.8 %all-to-all-start.1 = ((bf16[4,2,864]{2,1,0:T(2,128)(2,1)}), bf16[4,2,864]{2,1,0:T(2,128)(2,1)S(1)}, u32[]{:S(2)}, u32[]{:S(2)}) async-start(bf16[4,2,864]{2,1,0:T(2,128)(2,1)} %reshape.475), calls=%async_computation.6 | async-start | bytes 28672 | tf_op jit(solution)/shard_map/all_to_all | solution.py:265
  (65 other events, 135.1 us)
Sparse Core Ops, SparseCore 0:
  42.5 47.3 all-gather.6
  106.6 46.4 reduce-scatter.8
  157.0 49.3 all-gather.8
  208.4 48.7 all-gather.10
  272.9 46.4 reduce-scatter.12
  321.6 47.0 reduce-scatter.10
  375.5 49.3 all-gather.12
  428.3 37.9 reduce-scatter.22
  469.8 47.8 reduce-scatter.20
  520.8 34.6 reduce-scatter.18
  558.9 42.9 reduce-scatter.16
  604.1 47.6 reduce-scatter.14

commit v2 on v1

--- a/solution.py
+++ b/solution.py
@@ -1,8 +1,11 @@
+import functools
 import math
 
 import jax
 import jax.numpy as jnp
 from jax import lax
+from jax.experimental import pallas as pl
+from jax.experimental.pallas import tpu as pltpu
 from jax.sharding import PartitionSpec as P
 
 HD = 72
@@ -59,6 +62,359 @@
     rates = jnp.exp(-math.log(10000.0) * jnp.arange(half, dtype=jnp.float32) / half)
     angle = steps_in.astype(jnp.float32)[:, None] * rates[None, :]
     return jnp.concatenate([jnp.cos(angle), jnp.sin(angle)], axis=-1)
+
+
+CHUNKS = 4
+
+
+def rows_of(block, total):
+    size = total // CHUNKS
+    return pl.ds(pl.multiple_of(block * size, size), size)
+
+
+class Line:
+    def __init__(self, count, gathered, summed, ag_sems, rs_sems):
+        self.count = count
+        self.place = lax.axis_index("tensor")
+        self.gathered = gathered
+        self.summed = summed
+        self.ag_send, self.ag_recv = ag_sems
+        self.rs_send, self.rs_recv = rs_sems
+
+    def barrier(self):
+        place, count = self.place, self.count
+        sem = pltpu.get_barrier_semaphore()
+
+        @pl.when(place > 0)
+        def _():
+            pl.semaphore_signal(sem, inc=1, device_id={"tensor": place - 1})
+
+        @pl.when(place < count - 1)
+        def _():
+            pl.semaphore_signal(sem, inc=1, device_id={"tensor": place + 1})
+
+        peers = jnp.where(place > 0, 1, 0) + jnp.where(place < count - 1, 1, 0)
+        pl.semaphore_wait(sem, peers)
+
+    def item_copy(self, which, way, item, own=False):
+        mine, everyone = self.gathered[which]
+        target = self.place + (1 if way == 0 else -1)
+        return pltpu.make_async_remote_copy(
+            src_ref=mine if own else everyone.at[item],
+            dst_ref=everyone.at[item],
+            send_sem=self.ag_send.at[which, way, item],
+            recv_sem=self.ag_recv.at[which, way, item],
+            device_id={"tensor": target},
+        )
+
+    def can(self, way):
+        return self.place < self.count - 1 if way == 0 else self.place > 0
+
+    def sum_copy(self, which, way, item, block):
+        part, landed = self.summed[which]
+        target = self.place + (1 if way == 0 else -1)
+        slot = item
+        if way == 1:
+            slot = jnp.where(item == target, self.count, item)
+        rows = rows_of(block, part.shape[1])
+        return pltpu.make_async_remote_copy(
+            src_ref=part.at[item, rows],
+            dst_ref=landed.at[slot, rows],
+            send_sem=self.rs_send.at[which, way, item, block],
+            recv_sem=self.rs_recv.at[which, way, item, block],
+            device_id={"tensor": target},
+        )
+
+    def landed_slot(self, way, item):
+        return jnp.where(item == self.place, self.count, item) if way == 1 else item
+
+    def wait_sum(self, which, way, item, block):
+        part, landed = self.summed[which]
+        rows = rows_of(block, part.shape[1])
+        view = landed.at[self.landed_slot(way, item), rows]
+        pltpu.make_async_remote_copy(
+            src_ref=view,
+            dst_ref=view,
+            send_sem=self.rs_send.at[which, way, item, block],
+            recv_sem=self.rs_recv.at[which, way, item, block],
+            device_id={"tensor": self.place},
+        ).wait_recv()
+        return view
+
+    def start_own(self):
+        for which in range(len(self.gathered)):
+            for way in range(2):
+
+                @pl.when(self.can(way))
+                def _():
+                    self.item_copy(which, way, self.place, own=True).start()
+
+    def receive(self, step):
+        place, count = self.place, self.count
+        for which in range(len(self.gathered)):
+            for way in range(2):
+                item = place - step if way == 0 else place + step
+
+                @pl.when((item >= 0) & (item < count))
+                def _():
+                    self.item_copy(which, way, item).wait_recv()
+
+                    @pl.when(self.can(way))
+                    def _():
+                        self.item_copy(which, way, item).start()
+
+    def items(self, step):
+        place, count = self.place, self.count
+        low, high = place - step, place + step
+        return ((low, (low >= 0)), (high, (high < count) & (step > 0)))
+
+    def pass_sums(self, step):
+        place, count = self.place, self.count
+
+        @pl.loop(0, CHUNKS)
+        def _(block):
+            for which in range(len(self.summed)):
+                part, landed = self.summed[which]
+                rows = rows_of(block, part.shape[1])
+                for way in range(2):
+                    item = step if way == 0 else count - 1 - step
+                    further = item > place if way == 0 else item < place
+                    first = place == 0 if way == 0 else place == count - 1
+
+                    @pl.when(further & jnp.logical_not(first))
+                    def _():
+                        view = self.wait_sum(which, way, item, block)
+                        total = part[item, rows].astype(jnp.float32) + view[...].astype(
+                            jnp.float32
+                        )
+                        part[item, rows] = total.astype(part.dtype)
+
+                    @pl.when(further)
+                    def _():
+                        self.sum_copy(which, way, item, block).start()
+
+    def finish(self, which, out):
+        place, count = self.place, self.count
+        part, landed = self.summed[which]
+
+        @pl.loop(0, CHUNKS)
+        def _(block):
+            rows = rows_of(block, part.shape[1])
+            out[rows] = part[place, rows].astype(jnp.float32)
+            for way in range(2):
+
+                @pl.when(place > 0 if way == 0 else place < count - 1)
+                def _():
+                    view = self.wait_sum(which, way, place, block)
+                    out[rows] += view[...].astype(jnp.float32)
+
+    def drain(self):
+        place, count = self.place, self.count
+
+        @pl.loop(0, count)
+        def _(item):
+            for way in range(2):
+                passed = item <= place if way == 0 else item >= place
+
+                @pl.when(passed & self.can(way))
+                def _():
+                    for which in range(len(self.gathered)):
+                        self.item_copy(which, way, item).wait_send()
+
+                further = item > place if way == 0 else item < place
+
+                @pl.when(further)
+                def _():
+                    @pl.loop(0, CHUNKS)
+                    def _(block):
+                        for which in range(len(self.summed)):
+                            self.sum_copy(which, way, item, block).wait_send()
+
+
+def dot(left, right):
+    return jnp.dot(left, right, preferred_element_type=jnp.float32)
+
+
+def dot_rt(left, right):
+    return lax.dot_general(
+        left, right, (((1,), (1,)), ((), ())), preferred_element_type=jnp.float32
+    )
+
+
+def dot_lt(left, right):
+    return lax.dot_general(
+        left, right, (((0,), (0,)), ((), ())), preferred_element_type=jnp.float32
+    )
+
+
+def cut(total, most):
+    size = max(s for s in range(128, most + 1, 128) if total % s == 0)
+    return size, total // size
+
+
+def span(index, size):
+    return pl.ds(pl.multiple_of(index * size, size), size)
+
+
+def feed_kernel(
+    count,
+    mod_ref,
+    grad_ref,
+    expand_hbm,
+    down_hbm,
+    feed_out,
+    back_out,
+    weight_out,
+    expand,
+    down,
+    mod_all,
+    grad_all,
+    hidden,
+    slopes,
+    feed_part,
+    back_part,
+    feed_land,
+    back_land,
+    total,
+    load_sem,
+    ag_send,
+    ag_recv,
+    rs_send,
+    rs_recv,
+):
+    line = Line(
+        count,
+        [(mod_ref, mod_all), (grad_ref, grad_all)],
+        [(back_part, back_land), (feed_part, feed_land)],
+        (ag_send, ag_recv),
+        (rs_send, rs_recv),
+    )
+    width, units = expand.shape[1], expand.shape[2]
+    loads = (
+        pltpu.make_async_copy(expand_hbm, expand, load_sem.at[0]),
+        pltpu.make_async_copy(down_hbm, down, load_sem.at[1]),
+    )
+    for load in loads:
+        load.start()
+    line.barrier()
+    line.start_own()
+    mod_all[line.place] = mod_ref[...]
+    grad_all[line.place] = grad_ref[...]
+    total[...] = jnp.zeros_like(total)
+    for load in loads:
+        load.wait()
+    unit_size, unit_count = cut(units, 256)
+    wide_size, wide_count = cut(width, 384)
+    tall_size, tall_count = cut(width, 128)
+
+    def compute(item):
+        @pl.loop(0, unit_count)
+        def _(index):
+            cols = span(index, unit_size)
+            mod = mod_all[item]
+            gate = dot(mod, expand[0, :, cols])
+            upper = dot(mod, expand[1, :, cols])
+            back = dot_rt(grad_all[item], down[cols, :])
+            sigma = jax.nn.sigmoid(gate)
+            active = gate * sigma
+            hidden[item, :, cols] = (active * upper).astype(jnp.bfloat16)
+            slopes[0, item, :, cols] = (
+                back * upper * (sigma * (1.0 + gate * (1.0 - sigma)))
+            ).astype(jnp.bfloat16)
+            slopes[1, item, :, cols] = (back * active).astype(jnp.bfloat16)
+
+        @pl.loop(0, wide_count)
+        def _(index):
+            cols = span(index, wide_size)
+            back_part[item, :, cols] = (
+                dot_rt(slopes[0, item], expand[0, cols, :])
+                + dot_rt(slopes[1, item], expand[1, cols, :])
+            ).astype(jnp.bfloat16)
+            feed_part[item, :, cols] = dot(hidden[item], down[:, cols]).astype(jnp.bfloat16)
+
+    def weigh(item):
+        @pl.loop(0, tall_count)
+        def _(index):
+            rows = span(index, tall_size)
+            mod = mod_all[item, :, rows]
+            total[0, rows, :] += dot_lt(mod, slopes[0, item])
+            total[1, rows, :] += dot_lt(mod, slopes[1, item])
+            total[2, rows, :] += dot_lt(grad_all[item, :, rows], hidden[item])
+
+    @pl.loop(0, count)
+    def _(step):
+        @pl.when(step > 0)
+        def _():
+            for item, valid in line.items(step - 1):
+
+                @pl.when(valid)
+                def _():
+                    weigh(item)
+
+            line.receive(step)
+
+        for item, valid in line.items(step):
+
+            @pl.when(valid)
+            def _():
+                compute(item)
+
+        @pl.when(step > 0)
+        def _():
+            line.pass_sums(step)
+
+    for item, valid in line.items(count - 1):
+
+        @pl.when(valid)
+        def _():
+            weigh(item)
+
+    weight_out[...] = total[...].astype(jnp.bfloat16)
+    line.finish(0, back_out)
+    line.finish(1, feed_out)
+    line.drain()
+
+
+def feed_pass(mod_two, branch_grad, expand_weight, down_weight):
+    count = lax.axis_size("tensor")
+    length, width = mod_two.shape
+    units = down_weight.shape[0]
+    expand = jnp.transpose(expand_weight, (1, 0, 2))
+    vmem, any_space = pl.BlockSpec(memory_space=pltpu.VMEM), pl.BlockSpec(memory_space=pl.ANY)
+    low = jnp.bfloat16
+    item = (length, width)
+    return pl.pallas_call(
+        functools.partial(feed_kernel, count),
+        out_shape=(
+            jax.ShapeDtypeStruct(item, jnp.float32),
+            jax.ShapeDtypeStruct(item, jnp.float32),
+            jax.ShapeDtypeStruct((3, width, units), low),
+        ),
+        in_specs=[vmem, vmem, any_space, any_space],
+        out_specs=(vmem, vmem, vmem),
+        scratch_shapes=[
+            pltpu.VMEM((2, width, units), low),
+            pltpu.VMEM((units, width), low),
+            pltpu.VMEM((count, *item), low),
+            pltpu.VMEM((count, *item), low),
+            pltpu.VMEM((count, length, units), low),
+            pltpu.VMEM((2, count, length, units), low),
+            pltpu.VMEM((count, *item), low),
+            pltpu.VMEM((count, *item), low),
+            pltpu.VMEM((count + 1, *item), low),
+            pltpu.VMEM((count + 1, *item), low),
+            pltpu.VMEM((3, width, units), jnp.float32),
+            pltpu.SemaphoreType.DMA((2,)),
+            pltpu.SemaphoreType.DMA((2, 2, count)),
+            pltpu.SemaphoreType.DMA((2, 2, count)),
+            pltpu.SemaphoreType.DMA((2, 2, count, CHUNKS)),
+            pltpu.SemaphoreType.DMA((2, 2, count, CHUNKS)),
+        ],
+        compiler_params=pltpu.CompilerParams(
+            collective_id=1, has_side_effects=True, vmem_limit_bytes=64000000
+        ),
+        name="feed_pass",
+    )(mod_two, branch_grad, expand, down_weight)
 
 
 def shards(
@@ -155,46 +511,15 @@
     residual = token_local + attend_gate * attend_branch
     normed_two, inverse_two = layer_norm(residual)
     mod_two = (normed_two * (1.0 + feed_scale) + feed_shift).astype(jnp.bfloat16)
-    mod_two_all = lax.all_gather(mod_two, "tensor", axis=0, tiled=True)
-    gate_up = jnp.einsum(
-        "bld,dkf->blkf", mod_two_all, expand_weight, preferred_element_type=jnp.float32
-    )
-    gate = gate_up[:, :, 0]
-    upper = gate_up[:, :, 1]
-    hidden = (jax.nn.silu(gate) * upper).astype(jnp.bfloat16)
-    piece = hidden
-    feed_branch = lax.psum_scatter(
-        jnp.einsum("blf,fd->bld", piece, down_weight, preferred_element_type=jnp.float32).astype(
-            jnp.bfloat16
-        ),
-        "tensor",
-        scatter_dimension=0,
-        tiled=True,
-    ).astype(jnp.float32) + down_bias.astype(jnp.float32)
-    result = (live * (residual + feed_gate * feed_branch)).astype(jnp.bfloat16)
     out_grad = cotangent.astype(jnp.float32) * live
     branch_grad = (out_grad * feed_gate).astype(jnp.bfloat16)
     down_bias_part = jnp.sum(branch_grad.astype(jnp.float32), axis=(0, 1))
-    piece = lax.all_gather(branch_grad, "tensor", axis=0, tiled=True)
-    weight_total = jnp.einsum("blf,bld->fd", hidden, piece, preferred_element_type=jnp.float32)
-    rows_grad = jnp.einsum("bld,fd->blf", piece, down_weight, preferred_element_type=jnp.float32)
-    hidden_total = rows_grad
-    down_grad = weight_total
-    gate_up_grad = jnp.stack(
-        [hidden_total * upper * silu_slope(gate), hidden_total * jax.nn.silu(gate)], axis=2
-    ).astype(jnp.bfloat16)
-    expand_grad = jnp.einsum(
-        "bld,blkf->dkf", mod_two_all, gate_up_grad, preferred_element_type=jnp.float32
-    )
-    piece = gate_up_grad
-    mod_two_grad = lax.psum_scatter(
-        jnp.einsum(
-            "blkf,dkf->bld", piece, expand_weight, preferred_element_type=jnp.float32
-        ).astype(jnp.bfloat16),
-        "tensor",
-        scatter_dimension=0,
-        tiled=True,
-    ).astype(jnp.float32)
+    feed_total, mod_two_grad, feed_weights = feed_pass(
+        mod_two[0], branch_grad[0], expand_weight, down_weight
+    )
+    feed_branch = feed_total[None] + down_bias.astype(jnp.float32)
+    result = (live * (residual + feed_gate * feed_branch)).astype(jnp.bfloat16)
+    mod_two_grad = mod_two_grad[None]
     residual_grad = out_grad + layer_norm_back(
         normed_two, inverse_two, mod_two_grad * (1.0 + feed_scale)
     )
@@ -327,8 +652,9 @@
 
     project_grad = scatter(project_grad, 0)
     output_weight_grad = scatter(output_weight_grad, 1)
-    expand_grad = scatter(expand_grad, 0)
-    down_grad = scatter(down_grad, 1)
+    feed_weights = scatter(feed_weights, 1)
+    expand_grad = jnp.transpose(feed_weights[:2], (1, 0, 2))
+    down_grad = feed_weights[2].T
     return (
         result,
         tokens_grad,

time: 774 us -> 710 us (0.917)
  waiting for transfers between devices: 480 us -> 299 us
  Pallas kernels: 0 us -> 170 us
  matrix products: 92 us -> 48.8 us
  starting transfers between devices: 20.2 us -> 9.01 us
    pallas_call x0 -> x1, Pallas kernels: none -> 170 us  [feed_pass(): pl.pallas_call(functools.partial(feed_kernel, count), out_shape=(jax.Shap...]
    all_gather x2 -> x0, waiting for transfers between devices: 87 us -> none  [the longest x1 45.8 us: shards(): mod_two_all = lax.all_gather(mod_two, 'tensor', axis=0, tiled=True)]
    reduce_scatter x2 -> x0, waiting for transfers between devices: 85.1 us -> none  [the longest x1 45.5 us: shards(): lax.psum_scatter(jnp.einsum('blf,fd->bld', piece, down_weight, preferred_...]
    dot_general x6 -> x0, matrix products: 42.8 us -> none  [the longest x1 9.58 us: shards(): jnp.einsum('bld,dkf->blkf', mod_two_all, expand_weight, preferred_element...]
    all_gather x1, waiting for transfers between devices: 24.6 us -> 48 us  [shards(): piece = lax.all_gather(attend_grad, 'tensor', axis=0, tiled=True)]
    reduce_scatter x4 -> x3, waiting for transfers between devices: 134 us -> 112 us  [scatter(): lax.psum_scatter(value, 'dp', scatter_dimension=axis, tiled=True)]
    reduce_scatter x4 -> x3, starting transfers between devices: 11.3 us -> 0.34 us  [scatter(): lax.psum_scatter(value, 'dp', scatter_dimension=axis, tiled=True)]
    unnamed x172 -> x191, local copies, waits for them, and re-layouts: 17.4 us -> 21.1 us
  transfers between devices with their start and end apart: 14 -> 9, of which waited for: 14 -> 9; matrix products, arithmetic and copies ran while one was open for 11% -> 5% of each run, Pallas kernels for 0% -> 0%
where the time goes in v2:
time: 710 us; the launch traced here: 702 us
  waiting for transfers between devices  299 us (42%)
  Pallas kernels  170 us (24%)
  blocking collectives  77.2 us (11%)
  other arithmetic  50.9 us (7%)
  matrix products  48.8 us (7%)
  local copies, waits for them, and re-layouts  30.1 us (4%)
  between operations  16.5 us (2%)
  starting transfers between devices  9.01 us (1%)
    pallas_call x1, Pallas kernels, feed_pass(): pl.pallas_call(functools.partial(feed_kernel, count), out_shape=(jax.Shap...  170 us
    reduce_scatter x3, waiting for transfers between devices, scatter(): lax.psum_scatter(value, 'dp', scatter_dimension=axis, tiled=True)  112 us
    all_gather x1, waiting for transfers between devices, shards(): piece = lax.all_gather(attend_grad, 'tensor', axis=0, tiled=True)  48 us
    all_gather x1, waiting for transfers between devices, shards(): lax.all_gather((normed_local * (1.0 + attend_scale) + attend_shift).astyp...  47.1 us
    reduce_scatter x1, waiting for transfers between devices, shards(): lax.psum_scatter(jnp.einsum('blke,dke->bld', piece, project_weight, prefe...  46.4 us
    psum x1, blocking collectives, shards(): small = lax.psum(small, ('dp', 'tensor'))  39.6 us
    reduce_scatter x1, waiting for transfers between devices, shards(): lax.psum_scatter(jnp.einsum('blh,hd->bld', piece, output_weight, preferre...  37.6 us
    unnamed x191, local copies, waits for them, and re-layouts  21.1 us
  transfers between devices with their start and end apart: 9, of which 9 were waited for; matrix products, arithmetic and copies ran while one was open for 5% of the time, Pallas kernels for 0%

profile of v2, /device:TPU:0, one launch (start us, length us, event | category | flops | bytes accessed | tf_op | source)
XLA Modules:
  0.0 701.8 jit_solution(14135785840254427007)
XLA Ops:
  8.1 10.4 %all-gather = s32[8,4,2]{1,2,0:T(2,128)S(1)} all-gather(s32[1,4,2]{1,2,0:T(2,128)S(1)} %add_bitcast_fusion), channel_id=1, replica_groups=mesh['dp'=8,'tensor'=4] {'dp'}, dimensions={0}, use_global_device_ids=true | all-gather | bytes 288 | tf_op jit(solution)/shard_map/all_gather | solution.py:453
  21.3 2.6 gather_fusion
  29.4 4.9 all-to-all-start
  34.8 5.1 all-to-all-done
  42.8 47.1 %all-gather.5.cloned.1.call-done = bf16[4,256,1152]{2,1,0:T(8,128)(2,1)} async-done(((bf16[1,256,1152]{2,1,0:T(8,128)(2,1)}), bf16[4,256,1152]{2,1,0:T(8,128)(2,1)}) %all-gather.5.cloned.1.call-update) | async-done | bytes 2359312 | tf_op jit(solution)/shard_map/all_gather | solution.py:479
  89.9 4.7 fusion.3
  103.5 2.9 convolution_convert_fusion
  109.9 4.7 copy.181
  115.6 37.6 %reduce-scatter.6.cloned.1.call-done = bf16[1,256,1152]{2,1,0:T(8,128)(2,1)} async-done(((bf16[4,256,1152]{2,1,0:T(8,128)(2,1)}), bf16[1,256,1152]{2,1,0:T(8,128)(2,1)}) %reduce-scatter.6.cloned.1.call-update) | async-done | bytes 589840 | tf_op jit(solution)/shard_map/reduce_scatter | solution.py:503
  156.3 169.9 %feed_pass.1 = (f32[256,1152]{1,0:T(8,128)}, f32[256,1152]{1,0:T(8,128)}, bf16[3,1152,768]{2,1,0:T(8,128)(2,1)}) custom-call(bf16[256,1152]{1,0:T(8,128)(2,1)} %fusion.39.mod_ref, bf16[256,1152]{1,0:T(8,128)(2,1)} %fusion.41.grad_ref, bf16[2,1152,768]{2,1,0:T(8,128)(2,1)} %bitcast.185, bf16[768,1152]{1,0:T(8,128)(2,1)} %down_hbm.1), custom_call_target="tpu_custom_call" | custom-call | tf_op jit(solution)/shard_map/feed_pass/pallas_call | solution.py:386
  326.2 2.1 fusion.90
  328.5 2.6 fusion.29
  331.1 4.0 fusion.28
  338.0 48.0 %all-gather.7.cloned.1.call-done = bf16[4,256,1152]{2,1,0:T(8,128)(2,1)} async-done(((bf16[1,256,1152]{2,1,0:T(8,128)(2,1)}), bf16[4,256,1152]{2,1,0:T(8,128)(2,1)}) %all-gather.7.cloned.1.call-update) | async-done | bytes 2359312 | tf_op jit(solution)/shard_map/all_gather | solution.py:528
  386.0 2.9 convolution_convert_fusion.2
  389.1 2.4 multiply_reduce_fusion
  396.9 2.4 fusion
  410.5 5.3 bitcast_convert_fusion
  416.7 6.6 bitcast_convert_fusion.1
  424.1 8.8 %reduce-scatter.12.cloned.1.call-done = bf16[288,144]{0,1:T(8,128)(2,1)} async-done(((bf16[288,1152]{0,1:T(8,128)(2,1)}), bf16[288,144]{0,1:T(8,128)(2,1)}) %reduce-scatter.12.cloned.1.call-update) | async-done | bytes 82960 | tf_op jit(solution)/shard_map/reduce_scatter | solution.py:649
  434.4 44.8 %reduce-scatter.10.cloned.1.call-done = bf16[144,3,288]{2,0,1:T(8,128)(2,1)} async-done(((bf16[1152,3,288]{2,0,1:T(8,128)(2,1)}), bf16[144,3,288]{2,0,1:T(8,128)(2,1)}) %reduce-scatter.10.cloned.1.call-update) | async-done | bytes 248848 | tf_op jit(solution)/shard_map/reduce_scatter | solution.py:649
  481.1 58.2 %reduce-scatter.14.cloned.1.call-done = bf16[3,144,768]{2,1,0:T(8,128)(2,1)} async-done(((bf16[3,1152,768]{2,1,0:T(8,128)(2,1)}), bf16[3,144,768]{2,1,0:T(8,128)(2,1)}) %reduce-scatter.14.cloned.1.call-update) | async-done | bytes 663568 | tf_op jit(solution)/shard_map/reduce_scatter | solution.py:649
  543.0 46.4 %reduce-scatter.8.cloned.1.call-done = bf16[1,256,1152]{2,1,0:T(8,128)(2,1)} async-done(((bf16[4,256,1152]{2,1,0:T(8,128)(2,1)}), bf16[1,256,1152]{2,1,0:T(8,128)(2,1)}) %reduce-scatter.8.cloned.1.call-update) | async-done | bytes 589840 | tf_op jit(solution)/shard_map/reduce_scatter | solution.py:567
  594.0 7.7 %reduce.28 = bf16[1152,6]{1,0:T(8,128)(2,1)S(1)} reduce(bf16[1152,1,6]{2,1,0:T(2,128)(2,1)} %bitcast.191, bf16[]{:T(256)} %broadcast.432), dimensions={1}, to_apply=%bitcast.162.reduce_sub_computation | reduce | bytes 27650
  602.7 3.3 all-to-all-start.1
  606.0 2.8 fusion.22
  608.7 2.8 all-to-all-done.1
  613.3 39.6 %psum.14 = f32[9360]{0:T(1024)S(1)} all-reduce(f32[9360]{0:T(1024)S(1)} %concatenate.23), channel_id=1, replica_groups=mesh['dp'=8,'tensor'=4] {'dp','tensor'}, use_global_device_ids=true, to_apply=%region_29.30 | all-reduce | flops 9360 | bytes 74880 | tf_op jit(solution)/shard_map/psum | solution.py:640
  654.1 2.8 convolution_bitcast_fusion.1
  656.9 17.1 %psum.15 = f32[4,1152]{1,0:T(4,128)S(1)} all-reduce(f32[4,1152]{1,0:T(4,128)S(1)} %convolution_bitcast_fusion.1), channel_id=1, replica_groups=mesh['dp'=8,'tensor'=4] {'tensor'}, use_global_device_ids=true, to_apply=%region_32.33 | all-reduce | flops 4608 | bytes 36864 | tf_op jit(solution)/shard_map/psum | solution.py:597
  675.0 10.0 %all-gather.1 = bf16[8,4,2880]{2,1,0:T(4,128)(2,1)S(1)} all-gather(bf16[1,4,2880]{2,1,0:T(4,128)(2,1)S(1)} %maximum_bitcast_fusion), channel_id=1, replica_groups=mesh['dp'=8,'tensor'=4] {'dp'}, dimensions={0}, use_global_device_ids=true | all-gather | bytes 207360 | tf_op jit(solution)/shard_map/all_gather | solution.py:600
  692.2 2.2 fusion.48
  (311 shorter events, 72.4 us)
Async XLA Ops:
  7.2 18.9 %copy-start = (bf16[1152,1152]{1,0:T(8,128)(2,1)S(1)}, bf16[1152,1152]{1,0:T(8,128)(2,1)}, u32[]{:S(2)}) copy-start(bf16[1152,1152]{1,0:T(8,128)(2,1)} %param.37) | copy-start | bytes 7962628
  21.3 6.0 copy-start.64
  21.3 6.0 copy-start.66
  27.4 6.9 copy-start.4
  29.4 10.5 %all-to-all-start = ((bf16[4,6,288]{2,1,0:T(8,128)(2,1)}), bf16[4,6,288]{2,1,0:T(8,128)(2,1)S(1)}, u32[]{:S(2)}, u32[]{:S(2)}) async-start(bf16[4,6,288]{2,1,0:T(8,128)(2,1)} %copy.115), calls=%async_computation | async-start | bytes 49152 | tf_op jit(solution)/shard_map/all_to_all | solution.py:471
  34.2 55.7 %all-gather.5.cloned.1.call-start = ((), (), s32[]{:S(2)}) async-start(), calls=%async_computation.7 | async-start | bytes 2949120 | tf_op jit(solution)/shard_map/all_gather | solution.py:479
  34.4 8.0 %copy-start.68 = (f32[256]{0:T(256)}, f32[256]{0:T(256)S(1)}, u32[]{:S(2)}) copy-start(f32[256]{0:T(256)S(1)} %broadcast_multiply_fusion.5) | copy-start | bytes 3076
  34.7 7.8 %copy-start.90 = (bf16[72]{0:T(256)(128)(2,1)S(1)}, bf16[72]{0:T(256)(128)(2,1)}, u32[]{:S(2)}) copy-start(bf16[72]{0:T(256)(128)(2,1)} %param.26) | copy-start | bytes 436
  34.7 7.8 %copy-start.91 = (bf16[72]{0:T(256)(128)(2,1)S(1)}, bf16[72]{0:T(256)(128)(2,1)}, u32[]{:S(2)}) copy-start(bf16[72]{0:T(256)(128)(2,1)} %param.27) | copy-start | bytes 436
  34.8 59.9 %copy-start.72 = (f32[256]{0:T(256)}, f32[256]{0:T(256)S(1)}, u32[]{:S(2)}) copy-start(f32[256]{0:T(256)S(1)} %add_rsqrt_fusion.1) | copy-start | bytes 3076
  42.4 110.7 %reduce-scatter.6.cloned.1.call-start = ((), (), s32[]{:S(2)}) async-start(), calls=%async_computation.8 | async-start | bytes 2949120 | tf_op jit(solution)/shard_map/reduce_scatter | solution.py:503
  42.5 53.7 %copy-start.80 = (f32[72]{0:T(128)}, f32[72]{0:T(128)S(1)}, u32[]{:S(2)}) copy-start(f32[72]{0:T(128)S(1)} %convert_element_type.281) | copy-start | bytes 868
  42.5 53.9 %copy-start.82 = (f32[72]{0:T(128)}, f32[72]{0:T(128)S(1)}, u32[]{:S(2)}) copy-start(f32[72]{0:T(128)S(1)} %convert_element_type.284) | copy-start | bytes 868
  94.7 5.9 copy-start.16
  106.5 279.5 %all-gather.7.cloned.1.call-start = ((), (), s32[]{:S(2)}) async-start(), calls=%async_computation.9 | async-start | bytes 2949120 | tf_op jit(solution)/shard_map/all_gather | solution.py:528
  109.9 4.7 copy-start.19
  109.9 4.7 copy-start.57
  337.7 95.1 %reduce-scatter.12.cloned.1.call-start = ((), (), s32[]{:S(2)}) async-start(), calls=%async_computation.12 | async-start | bytes 995328 | tf_op jit(solution)/shard_map/reduce_scatter | solution.py:649
  399.3 80.0 %reduce-scatter.10.cloned.1.call-start = ((), (), s32[]{:S(2)}) async-start(), calls=%async_computation.11 | async-start | bytes 2985984 | tf_op jit(solution)/shard_map/reduce_scatter | solution.py:649
  404.2 5.1 copy-start.37
  415.8 123.5 %reduce-scatter.14.cloned.1.call-start = ((), (), s32[]{:S(2)}) async-start(), calls=%async_computation.13 | async-start | bytes 5971968 | tf_op jit(solution)/shard_map/reduce_scatter | solution.py:649
  416.4 172.9 %reduce-scatter.8.cloned.1.call-start = ((), (), s32[]{:S(2)}) async-start(), calls=%async_computation.10 | async-start | bytes 2949120 | tf_op jit(solution)/shard_map/reduce_scatter | solution.py:567
  540.6 48.8 %copy-start.56 = (f32[1152]{0:T(1024)S(1)}, f32[1152]{0:T(1024)}, u32[]{:S(2)}) copy-start(f32[1152]{0:T(1024)} %copy-done.55) | copy-start | bytes 13828
  540.6 48.8 %copy-start.69 = (f32[256]{0:T(256)S(1)}, f32[256]{0:T(256)}, u32[]{:S(2)}) copy-start(f32[256]{0:T(256)} %copy-done.68) | copy-start | bytes 3076
  540.6 48.8 %copy-start.73 = (f32[256]{0:T(256)S(1)}, f32[256]{0:T(256)}, u32[]{:S(2)}) copy-start(f32[256]{0:T(256)} %copy-done.72) | copy-start | bytes 3076
  602.7 8.8 %all-to-all-start.1 = ((bf16[4,2,864]{2,1,0:T(2,128)(2,1)}), bf16[4,2,864]{2,1,0:T(2,128)(2,1)S(1)}, u32[]{:S(2)}, u32[]{:S(2)}) async-start(bf16[4,2,864]{2,1,0:T(2,128)(2,1)} %reshape.471), calls=%async_computation.4 | async-start | bytes 28672 | tf_op jit(solution)/shard_map/all_to_all | solution.py:590
  608.7 4.5 copy-start.63
  608.7 4.5 copy-start.84
  608.7 4.5 copy-start.85
  685.0 5.2 copy-start.65
  685.0 5.2 copy-start.67
  685.1 6.0 copy-start.86
  (69 other events, 115.5 us)
Sparse Core Ops, SparseCore 0:
  42.5 47.3 all-gather.4
  106.6 46.4 reduce-scatter.5
  337.8 48.1 all-gather.6
  399.4 33.3 reduce-scatter.11
  436.2 43.0 reduce-scatter.9
  482.5 56.7 reduce-scatter.13
  541.6 47.6 reduce-scatter.7

commit v3 on v2

--- a/solution.py
+++ b/solution.py
@@ -64,7 +64,7 @@
     return jnp.concatenate([jnp.cos(angle), jnp.sin(angle)], axis=-1)
 
 
-CHUNKS = 4
+CHUNKS = 8
 
 
 def rows_of(block, total):
@@ -170,28 +170,44 @@
 
     def pass_sums(self, step):
         place, count = self.place, self.count
+        ways = []
+        for way in range(2):
+            item = step if way == 0 else count - 1 - step
+            ways.append(
+                (
+                    way,
+                    item,
+                    item > place if way == 0 else item < place,
+                    place if way == 0 else count - 1 - place,
+                )
+            )
 
         @pl.loop(0, CHUNKS)
         def _(block):
-            for which in range(len(self.summed)):
-                part, landed = self.summed[which]
-                rows = rows_of(block, part.shape[1])
-                for way in range(2):
-                    item = step if way == 0 else count - 1 - step
-                    further = item > place if way == 0 else item < place
-                    first = place == 0 if way == 0 else place == count - 1
-
-                    @pl.when(further & jnp.logical_not(first))
+            for way, item, further, hop in ways:
+
+                @pl.when(further & (hop == 0))
+                def _():
+                    for which in range(len(self.summed)):
+                        self.sum_copy(which, way, item, block).start()
+
+        @pl.loop(0, CHUNKS + count - 3)
+        def _(turn):
+            for distance in range(1, count - 1):
+                block = turn - (distance - 1)
+                for way, item, further, hop in ways:
+
+                    @pl.when(further & (hop == distance) & (block >= 0) & (block < CHUNKS))
                     def _():
-                        view = self.wait_sum(which, way, item, block)
-                        total = part[item, rows].astype(jnp.float32) + view[...].astype(
-                            jnp.float32
-                        )
-                        part[item, rows] = total.astype(part.dtype)
-
-                    @pl.when(further)
-                    def _():
-                        self.sum_copy(which, way, item, block).start()
+                        for which in range(len(self.summed)):
+                            part, landed = self.summed[which]
+                            rows = rows_of(block, part.shape[1])
+                            view = self.wait_sum(which, way, item, block)
+                            total = part[item, rows].astype(jnp.float32) + view[...].astype(
+                                jnp.float32
+                            )
+                            part[item, rows] = total.astype(part.dtype)
+                            self.sum_copy(which, way, item, block).start()
 
     def finish(self, which, out):
         place, count = self.place, self.count
@@ -417,6 +433,123 @@
     )(mod_two, branch_grad, expand, down_weight)
 
 
+def swap_kernel(jobs, total, *refs):
+    n = len(jobs)
+    ins, outs = refs[:n], refs[n + total : 2 * n + total]
+    sems = refs[2 * n + 2 * total :]
+    places = [lax.axis_index(axis) for axis, _, _ in jobs]
+    hello = pltpu.get_barrier_semaphore()
+    axes = []
+    for axis, count, _ in jobs:
+        if (axis, count) not in axes:
+            axes.append((axis, count))
+    if total:
+        axes = [("dp", lax.axis_size("dp")), ("tensor", lax.axis_size("tensor"))]
+    for axis, count in axes:
+        here = lax.axis_index(axis)
+
+        @pl.loop(1, count)
+        def _(offset):
+            peer = lax.rem(here + offset, count)
+            pl.semaphore_signal(hello, inc=1, device_id={axis: peer})
+
+    pl.semaphore_wait(hello, sum(count - 1 for _, count in axes))
+
+    def copy(source, target, send, recv, axis, peer, slot):
+        return pltpu.make_async_remote_copy(
+            src_ref=source,
+            dst_ref=target.at[slot],
+            send_sem=send.at[peer],
+            recv_sem=recv.at[slot],
+            device_id={axis: peer},
+        )
+
+    def start(source, target, send, recv, axis, count, split):
+        here = lax.axis_index(axis)
+
+        @pl.loop(1, count)
+        def _(offset):
+            peer = lax.rem(here + offset, count)
+            piece = source.at[peer] if split else source
+            copy(piece, target, send, recv, axis, peer, here).start()
+
+        target[here] = source[here] if split else source[...]
+
+    def finish(source, target, send, recv, axis, count, split):
+        here = lax.axis_index(axis)
+
+        @pl.loop(1, count)
+        def _(offset):
+            peer = lax.rem(here + offset, count)
+            piece = source.at[peer] if split else source
+            step = copy(piece, target, send, recv, axis, peer, peer)
+            step.wait_recv()
+            step.wait_send()
+
+    work = []
+    for index, (axis, count, split) in enumerate(jobs):
+        work.append((ins[index], outs[index], sems[2 * index], sems[2 * index + 1], axis, count, split))
+    if total:
+        source, result = refs[n], refs[2 * n + total]
+        one, two, middle, s1, r1, s2, r2 = sems[2 * n :]
+        wide, deep = lax.axis_size("dp"), lax.axis_size("tensor")
+        first = (source, one, s1, r1, "dp", wide, False)
+        start(*first)
+    for job in work:
+        start(*job)
+    if total:
+        finish(*first)
+        middle[...] = one[0]
+
+        @pl.loop(1, wide)
+        def _(index):
+            middle[...] += one[index]
+
+        second = (middle, two, s2, r2, "tensor", deep, False)
+        start(*second)
+    for job in work:
+        finish(*job)
+    if total:
+        finish(*second)
+        result[...] = two[0]
+
+        @pl.loop(1, deep)
+        def _(index):
+            result[...] += two[index]
+
+
+def swap(name, number, jobs, total=None):
+    vmem = pl.BlockSpec(memory_space=pltpu.VMEM)
+    plan, arrays, shapes, scratch = [], [], [], []
+    for array, axis, split in jobs:
+        count = lax.axis_size(axis)
+        plan.append((axis, count, split))
+        arrays.append(array)
+        piece = array.shape[1:] if split else array.shape
+        shapes.append(jax.ShapeDtypeStruct((count, *piece), array.dtype))
+        scratch += [pltpu.SemaphoreType.DMA((count,)), pltpu.SemaphoreType.DMA((count,))]
+    if total is not None:
+        wide, deep = lax.axis_size("dp"), lax.axis_size("tensor")
+        arrays.append(total)
+        shapes.append(jax.ShapeDtypeStruct(total.shape, total.dtype))
+        scratch += [
+            pltpu.VMEM((wide, *total.shape), total.dtype),
+            pltpu.VMEM((deep, *total.shape), total.dtype),
+            pltpu.VMEM(total.shape, total.dtype),
+        ]
+        for count in (wide, wide, deep, deep):
+            scratch.append(pltpu.SemaphoreType.DMA((count,)))
+    return pl.pallas_call(
+        functools.partial(swap_kernel, tuple(plan), int(total is not None)),
+        out_shape=tuple(shapes),
+        in_specs=[vmem] * len(arrays),
+        out_specs=tuple([vmem] * len(shapes)),
+        scratch_shapes=scratch,
+        compiler_params=pltpu.CompilerParams(collective_id=number, has_side_effects=True),
+        name=name,
+    )(*arrays)
+
+
 def shards(
     tokens,
     timesteps,
@@ -444,14 +577,12 @@
     slab = modulate_weight.shape[2]
     heads_here = project_weight.shape[2] // HD
     scale = HD ** (-0.5)
-    lane = lax.axis_index("tensor")
-    first_item = lane * local_items
+    first_item = lax.axis_index("tensor") * local_items
     live = (first_item + jnp.arange(local_items) < item_counts[0]).astype(jnp.float32)[
         :, None, None
     ]
     index = lax.axis_index("dp")
-    tags = lax.all_gather(jnp.stack([timesteps, labels]), "dp", axis=1, tiled=True)
-    time_feat = time_features(tags[0]).astype(jnp.bfloat16)
+    time_feat = time_features(timesteps).astype(jnp.bfloat16)
     pre_hidden = jnp.dot(
         time_feat, time_weight, preferred_element_type=jnp.float32
     ) + time_bias.astype(jnp.float32)
@@ -459,18 +590,16 @@
     condition = (
         jnp.dot(time_hidden, embed_weight, preferred_element_type=jnp.float32)
         + embed_bias.astype(jnp.float32)
-        + jnp.take(class_table, tags[1], axis=0).astype(jnp.float32)
+        + jnp.take(class_table, labels, axis=0).astype(jnp.float32)
     )
     cond_act = jax.nn.silu(condition).astype(jnp.bfloat16)
-    cond_act_here = lax.dynamic_slice_in_dim(cond_act, index * items, items, 0)
-    condition_here = lax.dynamic_slice_in_dim(condition, index * items, items, 0)
     modulation_part = (
-        jnp.einsum("bd,dke->bke", cond_act_here, modulate_weight, preferred_element_type=jnp.float32)
+        jnp.einsum("bd,dke->bke", cond_act, modulate_weight, preferred_element_type=jnp.float32)
         + modulate_bias.astype(jnp.float32)
     ).astype(jnp.bfloat16)
-    modulation_local = lax.all_to_all(
-        modulation_part, "tensor", split_axis=0, concat_axis=2, tiled=True
-    ).astype(jnp.float32)
+    (modulation_local,) = swap("modulation_swap", 2, [(modulation_part, "tensor", True)])
+    modulation_local = jnp.transpose(modulation_local, (1, 0, 2)).reshape(1, 6, width)
+    modulation_local = modulation_local.astype(jnp.float32)
     local_parts = [modulation_local[:, which][:, None, :] for which in range(6)]
     attend_shift, attend_scale, attend_gate, feed_shift, feed_scale, feed_gate = local_parts
     positions = jnp.arange(length)
@@ -587,62 +716,87 @@
         ],
         axis=1,
     )
-    modulation_grad = lax.all_to_all(
-        modulation_grad_part, "tensor", split_axis=2, concat_axis=0, tiled=True
-    ).astype(jnp.bfloat16)
-    modulate_bias_part = jnp.sum(modulation_grad.astype(jnp.float32), axis=0)
-    cond_part = jnp.einsum(
-        "bke,dke->bd", modulation_grad, modulate_weight, preferred_element_type=jnp.float32
-    )
-    cond_total = lax.psum(cond_part, "tensor")
-    cond_grad_here = (cond_total * silu_slope(condition_here)).astype(jnp.bfloat16)
-    packed = jnp.concatenate([cond_grad_here, modulation_grad.reshape(items, 6 * slab)], axis=1)
-    packed = lax.all_gather(packed, "dp", axis=0, tiled=True)
-    cond_grad = packed[:, :width]
-    modulation_grad_all = packed[:, width:].reshape(-1, 6, slab)
-    share = width // lax.axis_size("dp")
-
-    def mine(value, axis):
-        return lax.dynamic_slice_in_dim(value, index * share, share, axis)
-
-    one_hot = (tags[1][:, None] == jnp.arange(class_table.shape[0])[None, :]).astype(jnp.bfloat16)
-    cond_grad_mine = mine(cond_grad, 1)
-    class_grad = jnp.einsum(
-        "bc,bd->cd", one_hot, cond_grad_mine, preferred_element_type=jnp.float32
-    )
-    pre_grad = (
-        jnp.einsum(
-            "be,de->bd", cond_grad, mine(embed_weight, 0), preferred_element_type=jnp.float32
-        )
-        * silu_slope(mine(pre_hidden, 1))
-    ).astype(jnp.bfloat16)
-    modulate_grad = jnp.einsum(
-        "bd,bke->dke", mine(cond_act, 1), modulation_grad_all, preferred_element_type=jnp.float32
-    )
-    embed_grad = jnp.einsum(
-        "bd,be->de", mine(time_hidden, 1), cond_grad, preferred_element_type=jnp.float32
-    )
-    embed_bias_grad = jnp.sum(cond_grad_mine.astype(jnp.float32), axis=0)
-    time_grad = jnp.einsum("bf,bd->fd", time_feat, pre_grad, preferred_element_type=jnp.float32)
-    time_bias_grad = jnp.sum(pre_grad.astype(jnp.float32), axis=0)
-    bias_wide = lax.dynamic_update_slice_in_dim(
-        jnp.zeros((6, width), jnp.float32), modulate_bias_part, lane * slab, 1
-    )
+    modulation_grad_part = modulation_grad_part[0].astype(jnp.bfloat16)
     small = jnp.concatenate(
         [
             output_bias_part,
             down_bias_part,
-            bias_wide.reshape(-1),
+            modulation_grad_part.astype(jnp.float32).reshape(-1),
             query_gain_part,
             key_gain_part,
         ]
     )
-    small = lax.psum(small, ("dp", "tensor"))
+    small_size = small.shape[0]
+    small = jnp.pad(small, (0, -small_size % 1024)).reshape(-1, 128)
+    tensor_size = width // slab
+    modulation_grad, small = swap(
+        "sums_swap",
+        3,
+        [
+            (
+                jnp.transpose(modulation_grad_part.reshape(6, tensor_size, slab), (1, 0, 2)),
+                "tensor",
+                True,
+            )
+        ],
+        small,
+    )
+    small = small.reshape(-1)
     output_bias_grad = small[:width]
     down_bias_grad = small[width : 2 * width]
     modulate_bias_grad = small[2 * width : 8 * width].reshape(6, width)
     query_gain_grad = small[8 * width : 8 * width + HD]
-    key_gain_grad = small[8 * width + HD :]
+    key_gain_grad = small[8 * width + HD : 8 * width + 2 * HD]
+    cond_part = jnp.einsum(
+        "bke,dke->bd", modulation_grad, modulate_weight, preferred_element_type=jnp.float32
+    )
+    (cond_parts,) = swap("condition_swap", 4, [(cond_part, "tensor", False)])
+    cond_grad = (jnp.sum(cond_parts, axis=0) * silu_slope(condition)).astype(jnp.bfloat16)
+    pre_grad = (
+        jnp.einsum("be,de->bd", cond_grad, embed_weight, preferred_element_type=jnp.float32)
+        * silu_slope(pre_hidden)
+    ).astype(jnp.bfloat16)
+    pieces = [
+        cond_grad,
+        cond_act,
+        time_hidden,
+        pre_grad,
+        time_feat,
+        modulation_grad.reshape(items, 6 * slab),
+    ]
+    packed = jnp.concatenate(pieces, axis=1)
+    tags = jnp.broadcast_to(labels[:, None], (items, 128))
+    packed, tags = swap("items_swap", 5, [(packed, "dp", False), (tags, "dp", False)])
+    packed = packed.reshape(-1, packed.shape[2])
+    tags = tags[:, :, 0].reshape(-1)
+    edges = [0]
+    for piece in pieces:
+        edges.append(edges[-1] + piece.shape[1])
+    cond_grad, cond_act, time_hidden, pre_grad, time_feat, modulation_grad = [
+        packed[:, start:stop] for start, stop in zip(edges[:-1], edges[1:])
+    ]
+    modulation_grad = modulation_grad.reshape(-1, 6, slab)
+    share = width // lax.axis_size("dp")
+
+    def mine(value):
+        return lax.dynamic_slice_in_dim(value, index * share, share, 1)
+
+    one_hot = (tags[:, None] == jnp.arange(class_table.shape[0])[None, :]).astype(jnp.bfloat16)
+    cond_grad_mine, pre_grad_mine = mine(cond_grad), mine(pre_grad)
+    class_grad = jnp.einsum(
+        "bc,bd->cd", one_hot, cond_grad_mine, preferred_element_type=jnp.float32
+    )
+    modulate_grad = jnp.einsum(
+        "bd,bke->dke", mine(cond_act), modulation_grad, preferred_element_type=jnp.float32
+    )
+    embed_grad = jnp.einsum(
+        "bd,be->de", mine(time_hidden), cond_grad, preferred_element_type=jnp.float32
+    )
+    embed_bias_grad = jnp.sum(cond_grad_mine.astype(jnp.float32), axis=0)
+    time_grad = jnp.einsum(
+        "bf,bd->fd", time_feat, pre_grad_mine, preferred_element_type=jnp.float32
+    )
+    time_bias_grad = jnp.sum(pre_grad_mine.astype(jnp.float32), axis=0)
 
     def scatter(value, axis):
         value = value.astype(jnp.bfloat16)

time: 710 us -> 611 us (0.86)
  blocking collectives: 77.2 us -> 0 us
  starting transfers between devices: 9.01 us -> 0.75 us
    psum x2 -> x0, blocking collectives: 56.8 us -> none  [the longest x1 39.6 us: shards(): small = lax.psum(small, ('dp', 'tensor'))]
    pallas_call x1, Pallas kernels: 170 us -> 124 us  [feed_pass(): pl.pallas_call(functools.partial(feed_kernel, count), out_shape=(jax.Shap...]
    pallas_call x0 -> x4, Pallas kernels: none -> 40.5 us  [swap(): pl.pallas_call(functools.partial(swap_kernel, tuple(plan), int(total is n...]
    all_gather x2 -> x0, blocking collectives: 20.4 us -> none  [the longest x1 10.4 us: shards(): lax.all_gather(jnp.stack([timesteps, labels]), 'dp', axis=1, tiled=True)]
    unnamed x3 -> x5, other arithmetic: 8.57 us -> 0.33 us
    all_to_all x2 -> x0, starting transfers between devices: 8.12 us -> none  [the longest x1 4.87 us: shards(): lax.all_to_all(modulation_part, 'tensor', split_axis=0, concat_axis=2, ti...]
    all_to_all x2 -> x0, waiting for transfers between devices: 7.92 us -> none  [the longest x1 5.11 us: shards(): lax.all_to_all(modulation_part, 'tensor', split_axis=0, concat_axis=2, ti...]
    unnamed x191 -> x200, local copies, waits for them, and re-layouts: 21.1 us -> 19 us
  transfers between devices with their start and end apart: 9 -> 7, of which waited for: 9 -> 7; matrix products, arithmetic and copies ran while one was open for 5% -> 5% of each run, Pallas kernels for 0% -> 0%
where the time goes in v3:
time: 611 us; the launch traced here: 601 us
  waiting for transfers between devices  296 us (48%)
  Pallas kernels  165 us (27%)
  matrix products  47.5 us (8%)
  other arithmetic  44.6 us (7%)
  local copies, waits for them, and re-layouts  30.3 us (5%)
  between operations  16.6 us (3%)
    pallas_call x1, Pallas kernels, feed_pass(): pl.pallas_call(functools.partial(feed_kernel, count), out_shape=(jax.Shap...  124 us
    reduce_scatter x3, waiting for transfers between devices, scatter(): lax.psum_scatter(value, 'dp', scatter_dimension=axis, tiled=True)  112 us
    all_gather x1, waiting for transfers between devices, shards(): lax.all_gather((normed_local * (1.0 + attend_scale) + attend_shift).astyp...  50.7 us
    all_gather x1, waiting for transfers between devices, shards(): piece = lax.all_gather(attend_grad, 'tensor', axis=0, tiled=True)  48.8 us
    reduce_scatter x1, waiting for transfers between devices, shards(): lax.psum_scatter(jnp.einsum('blke,dke->bld', piece, project_weight, prefe...  46.4 us
    pallas_call x4, Pallas kernels, swap(): pl.pallas_call(functools.partial(swap_kernel, tuple(plan), int(total is n...  40.5 us
    reduce_scatter x1, waiting for transfers between devices, shards(): lax.psum_scatter(jnp.einsum('blh,hd->bld', piece, output_weight, preferre...  37.8 us
    unnamed x200, local copies, waits for them, and re-layouts  19 us
  transfers between devices with their start and end apart: 7, of which 7 were waited for; matrix products, arithmetic and copies ran while one was open for 5% of the time, Pallas kernels for 0%

profile of v3, /device:TPU:0, one launch (start us, length us, event | category | flops | bytes accessed | tf_op | source)
XLA Modules:
  0.0 601.1 jit_solution(9839592283283895318)
XLA Ops:
  12.4 2.5 gather_fusion
  16.2 3.5 fusion.63
  20.4 8.7 %modulation_swap.1 = bf16[4,6,288]{2,1,0:T(8,128)(2,1)} custom-call(bf16[4,6,288]{2,1,0:T(8,128)(2,1)} %fusion.51.refs_0_), custom_call_target="tpu_custom_call" | custom-call | tf_op jit(solution)/shard_map/modulation_swap/pallas_call | solution.py:542
  32.7 50.7 %all-gather.3.cloned.1.call-done = bf16[4,256,1152]{2,1,0:T(8,128)(2,1)} async-done(((bf16[1,256,1152]{2,1,0:T(8,128)(2,1)}), bf16[4,256,1152]{2,1,0:T(8,128)(2,1)}) %all-gather.3.cloned.1.call-update) | async-done | bytes 2359312 | tf_op jit(solution)/shard_map/all_gather | solution.py:608
  83.4 4.7 fusion.3
  97.0 2.9 convolution_convert_fusion
  103.3 4.6 copy.154
  108.8 37.8 %reduce-scatter.6.cloned.1.call-done = bf16[1,256,1152]{2,1,0:T(8,128)(2,1)} async-done(((bf16[4,256,1152]{2,1,0:T(8,128)(2,1)}), bf16[1,256,1152]{2,1,0:T(8,128)(2,1)}) %reduce-scatter.6.cloned.1.call-update) | async-done | bytes 589840 | tf_op jit(solution)/shard_map/reduce_scatter | solution.py:632
  149.8 124.4 %feed_pass.1 = (f32[256,1152]{1,0:T(8,128)}, f32[256,1152]{1,0:T(8,128)}, bf16[3,1152,768]{2,1,0:T(8,128)(2,1)}) custom-call(bf16[256,1152]{1,0:T(8,128)(2,1)} %fusion.39.mod_ref, bf16[256,1152]{1,0:T(8,128)(2,1)} %fusion.41.grad_ref, bf16[2,1152,768]{2,1,0:T(8,128)(2,1)} %bitcast.156, bf16[768,1152]{1,0:T(8,128)(2,1)} %down_hbm.1), custom_call_target="tpu_custom_call" | custom-call | tf_op jit(solution)/shard_map/feed_pass/pallas_call | solution.py:402
  274.3 2.1 fusion.91
  276.5 2.6 fusion.31
  279.2 4.6 convert_reduce_fusion.1
  284.1 48.8 %all-gather.5.cloned.1.call-done = bf16[4,256,1152]{2,1,0:T(8,128)(2,1)} async-done(((bf16[1,256,1152]{2,1,0:T(8,128)(2,1)}), bf16[4,256,1152]{2,1,0:T(8,128)(2,1)}) %all-gather.5.cloned.1.call-update) | async-done | bytes 2359312 | tf_op jit(solution)/shard_map/all_gather | solution.py:657
  332.9 2.9 convolution_convert_fusion.2
  336.0 2.4 multiply_reduce_fusion
  339.7 1.8 fusion.17
  343.8 2.4 fusion
  346.2 1.8 multiply_add_fusion.7
  357.0 5.3 bitcast_convert_fusion
  363.2 6.6 %bitcast_convert_fusion.1 = bf16[4,256,1152]{2,1,0:T(8,128)(2,1)} fusion(bf16[1152,3,288]{0,2,1:T(8,128)(2,1)} %param.25, bf16[4,256,1,288]{1,3,2,0:T(8,128)(2,1)} %bitcast.169, bf16[4,256,1,288]{1,3,2,0:T(8,128)(2,1)} %bitcast.165, bf16[4,256,1,288]{1,3,2,0:T(8,128)(2,1)} %bitcast.167), kind=kOutput, calls=%fused_computation.2 | convolution fusion | flops 2041380864 | bytes 6119424 | tf_op jit(solution)/shard_map/blke,dke->bld/dot_general | solution.py:697
  370.8 8.9 %reduce-scatter.12.cloned.1.call-done = bf16[288,144]{0,1:T(8,128)(2,1)} async-done(((bf16[288,1152]{0,1:T(8,128)(2,1)}), bf16[288,144]{0,1:T(8,128)(2,1)}) %reduce-scatter.12.cloned.1.call-update) | async-done | bytes 82960 | tf_op jit(solution)/shard_map/reduce_scatter | solution.py:803
  381.3 44.8 %reduce-scatter.10.cloned.1.call-done = bf16[144,3,288]{2,0,1:T(8,128)(2,1)} async-done(((bf16[1152,3,288]{2,0,1:T(8,128)(2,1)}), bf16[144,3,288]{2,0,1:T(8,128)(2,1)}) %reduce-scatter.10.cloned.1.call-update) | async-done | bytes 248848 | tf_op jit(solution)/shard_map/reduce_scatter | solution.py:803
  426.1 1.9 convert_element_type.285
  427.9 58.2 %reduce-scatter.14.cloned.1.call-done = bf16[3,144,768]{2,1,0:T(8,128)(2,1)} async-done(((bf16[3,1152,768]{2,1,0:T(8,128)(2,1)}), bf16[3,144,768]{2,1,0:T(8,128)(2,1)}) %reduce-scatter.14.cloned.1.call-update) | async-done | bytes 663568 | tf_op jit(solution)/shard_map/reduce_scatter | solution.py:803
  489.8 46.4 %reduce-scatter.8.cloned.1.call-done = bf16[1,256,1152]{2,1,0:T(8,128)(2,1)} async-done(((bf16[4,256,1152]{2,1,0:T(8,128)(2,1)}), bf16[1,256,1152]{2,1,0:T(8,128)(2,1)}) %reduce-scatter.8.cloned.1.call-update) | async-done | bytes 589840 | tf_op jit(solution)/shard_map/reduce_scatter | solution.py:696
  537.5 1.7 fusion.27
  539.3 2.7 multiply_reduce_fusion.4
  543.8 14.3 %sums_swap.1 = (bf16[4,6,288]{2,1,0:T(8,128)(2,1)}, f32[80,128]{1,0:T(8,128)}) custom-call(bf16[4,6,288]{2,1,0:T(8,128)(2,1)} %bitcast.174, f32[80,128]{1,0:T(8,128)} %pad_bitcast_fusion.refs_1_), custom_call_target="tpu_custom_call" | custom-call | tf_op jit(solution)/shard_map/sums_swap/pallas_call | solution.py:542
  559.0 3.4 convolution_bitcast_fusion.1.refs_0_
  563.0 7.0 %condition_swap.1 = f32[4,4,1152]{2,1,0:T(4,128)} custom-call(f32[4,1152]{1,0:T(4,128)} %convolution_bitcast_fusion.1.refs_0_), custom_call_target="tpu_custom_call" | custom-call | tf_op jit(solution)/shard_map/condition_swap/pallas_call | solution.py:542
  572.8 10.5 %items_swap.1 = (bf16[8,4,6592]{2,1,0:T(4,128)(2,1)}, s32[8,4,128]{2,1,0:T(4,128)}) custom-call(bf16[4,6592]{1,0:T(4,128)(2,1)} %copy-done.64, s32[4,128]{1,0:T(4,128)} %broadcast_in_dim.26.refs_1_), custom_call_target="tpu_custom_call" | custom-call | tf_op jit(solution)/shard_map/items_swap/pallas_call | solution.py:542
  589.2 1.9 fusion.56
  (324 shorter events, 61.2 us)
Async XLA Ops:
  7.2 8.5 %copy-start = (bf16[1152,1152]{1,0:T(8,128)(2,1)S(1)}, bf16[1152,1152]{1,0:T(8,128)(2,1)}, u32[]{:S(2)}) copy-start(bf16[1152,1152]{1,0:T(8,128)(2,1)} %param.37) | copy-start | bytes 7962628
  7.2 5.0 copy-start.91
  7.2 5.0 copy-start.92
  7.2 5.0 copy-start.82
  7.2 7.7 %copy-start.39 = (bf16[256,1152]{1,0:T(8,128)(2,1)S(1)}, bf16[256,1152]{1,0:T(8,128)(2,1)}, u32[]{:S(2)}) copy-start(bf16[256,1152]{1,0:T(8,128)(2,1)} %param.35) | copy-start | bytes 1769476
  7.2 76.2 %all-gather.3.cloned.1.call-start = ((), (), s32[]{:S(2)}) async-start(), calls=%async_computation.5 | async-start | bytes 2949120 | tf_op jit(solution)/shard_map/all_gather | solution.py:608
  7.3 4.9 copy-start.83
  9.6 6.6 %copy-start.85 = (f32[4]{0:T(128)}, f32[4]{0:T(128)S(1)}, u32[]{:S(2)}) copy-start(f32[4]{0:T(128)S(1)} %convert_element_type.248) | copy-start | bytes 52
  10.8 19.8 %copy-start.73 = (f32[256]{0:T(256)}, f32[256]{0:T(256)S(1)}, u32[]{:S(2)}) copy-start(f32[256]{0:T(256)S(1)} %broadcast_multiply_fusion.5) | copy-start | bytes 3076
  12.2 18.5 %copy-start.77 = (f32[256]{0:T(256)}, f32[256]{0:T(256)S(1)}, u32[]{:S(2)}) copy-start(f32[256]{0:T(256)S(1)} %add_rsqrt_fusion.1) | copy-start | bytes 3076
  16.2 15.0 %copy-start.4 = (bf16[1,256,1152]{2,1,0:T(8,128)(2,1)S(1)}, bf16[1,256,1152]{2,1,0:T(8,128)(2,1)}, u32[]{:S(2)}) copy-start(bf16[1,256,1152]{2,1,0:T(8,128)(2,1)} %param.20) | copy-start | bytes 1769476
  19.7 12.7 %copy-start.97 = (bf16[72]{0:T(256)(128)(2,1)S(1)}, bf16[72]{0:T(256)(128)(2,1)}, u32[]{:S(2)}) copy-start(bf16[72]{0:T(256)(128)(2,1)} %param.26) | copy-start | bytes 436
  19.7 12.7 %copy-start.98 = (bf16[72]{0:T(256)(128)(2,1)S(1)}, bf16[72]{0:T(256)(128)(2,1)}, u32[]{:S(2)}) copy-start(bf16[72]{0:T(256)(128)(2,1)} %param.27) | copy-start | bytes 436
  32.3 114.3 %reduce-scatter.6.cloned.1.call-start = ((), (), s32[]{:S(2)}) async-start(), calls=%async_computation.6 | async-start | bytes 2949120 | tf_op jit(solution)/shard_map/reduce_scatter | solution.py:632
  32.4 57.3 %copy-start.87 = (f32[72]{0:T(128)}, f32[72]{0:T(128)S(1)}, u32[]{:S(2)}) copy-start(f32[72]{0:T(128)S(1)} %convert_element_type.261) | copy-start | bytes 868
  32.4 57.6 %copy-start.89 = (f32[72]{0:T(128)}, f32[72]{0:T(128)S(1)}, u32[]{:S(2)}) copy-start(f32[72]{0:T(128)S(1)} %convert_element_type.264) | copy-start | bytes 868
  88.2 5.9 copy-start.15
  100.0 232.9 %all-gather.5.cloned.1.call-start = ((), (), s32[]{:S(2)}) async-start(), calls=%async_computation.7 | async-start | bytes 2949120 | tf_op jit(solution)/shard_map/all_gather | solution.py:657
  103.3 4.6 copy-start.19
  103.3 4.6 copy-start.62
  283.8 95.9 %reduce-scatter.12.cloned.1.call-start = ((), (), s32[]{:S(2)}) async-start(), calls=%async_computation.10 | async-start | bytes 995328 | tf_op jit(solution)/shard_map/reduce_scatter | solution.py:803
  346.2 79.9 %reduce-scatter.10.cloned.1.call-start = ((), (), s32[]{:S(2)}) async-start(), calls=%async_computation.9 | async-start | bytes 2985984 | tf_op jit(solution)/shard_map/reduce_scatter | solution.py:803
  350.7 5.0 copy-start.37
  362.3 123.8 %reduce-scatter.14.cloned.1.call-start = ((), (), s32[]{:S(2)}) async-start(), calls=%async_computation.11 | async-start | bytes 5971968 | tf_op jit(solution)/shard_map/reduce_scatter | solution.py:803
  362.9 173.3 %reduce-scatter.8.cloned.1.call-start = ((), (), s32[]{:S(2)}) async-start(), calls=%async_computation.8 | async-start | bytes 2949120 | tf_op jit(solution)/shard_map/reduce_scatter | solution.py:696
  489.0 48.5 %copy-start.61 = (f32[1152]{0:T(1024)S(1)}, f32[1152]{0:T(1024)}, u32[]{:S(2)}) copy-start(f32[1152]{0:T(1024)} %copy-done.60) | copy-start | bytes 13828
  489.0 48.5 %copy-start.74 = (f32[256]{0:T(256)S(1)}, f32[256]{0:T(256)}, u32[]{:S(2)}) copy-start(f32[256]{0:T(256)} %copy-done.73) | copy-start | bytes 3076
  489.0 48.5 %copy-start.78 = (f32[256]{0:T(256)S(1)}, f32[256]{0:T(256)}, u32[]{:S(2)}) copy-start(f32[256]{0:T(256)} %copy-done.77) | copy-start | bytes 3076
  489.0 50.3 %copy-start.45 = (f32[1152]{0:T(1024)S(1)}, f32[1152]{0:T(1024)}, u32[]{:S(2)}) copy-start(f32[1152]{0:T(1024)} %convert_element_type.271) | copy-start | bytes 13828
  558.9 12.0 %copy-start.42 = (f32[4,1152]{1,0:T(4,128)S(1)}, f32[4,1152]{1,0:T(4,128)}, u32[]{:S(2)}) copy-start(f32[4,1152]{1,0:T(4,128)} %copy-done.41) | copy-start | bytes 55300
  558.9 12.0 %copy-start.49 = (f32[4,1152]{1,0:T(4,128)S(1)}, f32[4,1152]{1,0:T(4,128)}, u32[]{:S(2)}) copy-start(f32[4,1152]{1,0:T(4,128)} %copy-done.48) | copy-start | bytes 55300
  583.3 4.7 copy-start.79
  (74 other events, 123.6 us)
Sparse Core Ops, SparseCore 0:
  32.5 50.9 all-gather.2
  100.1 46.4 reduce-scatter.5
  283.9 48.9 all-gather.4
  346.3 33.3 reduce-scatter.11
  383.0 42.9 reduce-scatter.9
  429.3 56.7 reduce-scatter.13
  488.4 47.6 reduce-scatter.7

commit v4 on v3

--- a/solution.py
+++ b/solution.py
@@ -548,6 +548,374 @@
         compiler_params=pltpu.CompilerParams(collective_id=number, has_side_effects=True),
         name=name,
     )(*arrays)
+
+
+LANES = 128
+
+
+def turn(value, tables):
+    return (
+        value * tables[0]
+        + pltpu.roll(value, LANES - HD // 4, 1) * tables[1]
+        + pltpu.roll(value, HD // 4, 1) * tables[2]
+    )
+
+
+def turn_back(grad, tables):
+    return (
+        grad * tables[0]
+        + pltpu.roll(grad * tables[1], HD // 4, 1)
+        + pltpu.roll(grad * tables[2], LANES - HD // 4, 1)
+    )
+
+
+def turn_tables(length):
+    quarter = HD // 4
+    lane = jnp.arange(LANES)
+    rates = 10000.0 ** (-(lane % quarter).astype(jnp.float32) / quarter)
+    positions = jnp.arange(length)[:, None]
+    place = jnp.where(lane < 2 * quarter, positions // GRID, positions % GRID)
+    angle = place.astype(jnp.float32) * rates
+    real = lane < HD
+    early = (lane // quarter) % 2 == 0
+    cosine = jnp.where(real, jnp.cos(angle), 0.0)
+    sine = jnp.sin(angle)
+    return jnp.stack(
+        [
+            cosine,
+            jnp.where(real & early, -sine, 0.0),
+            jnp.where(real & ~early, sine, 0.0),
+        ]
+    )
+
+
+def unit_norm(raw):
+    inverse = lax.rsqrt(jnp.sum(raw * raw, axis=-1, keepdims=True) * (1.0 / HD) + EPS)
+    return raw * inverse, inverse
+
+
+def project(mod, weight, raw):
+    size, number = cut(weight.shape[1], 512)
+
+    @pl.loop(0, number)
+    def _(index):
+        cols = span(index, size)
+        raw[:, cols] = dot(mod, weight[:, cols])
+
+
+def soft(queries, keys):
+    scores = dot_rt(queries, keys) * (HD ** (-0.5))
+    shifted = jnp.exp(scores - jnp.max(scores, axis=-1, keepdims=True))
+    return shifted * (1.0 / jnp.sum(shifted, axis=-1, keepdims=True))
+
+
+def attend_kernel(
+    count,
+    mod_ref,
+    tables_ref,
+    gains_ref,
+    weight_hbm,
+    last_hbm,
+    branch_out,
+    mod_out,
+    weight,
+    last,
+    mod_all,
+    raw,
+    mixed,
+    part,
+    land,
+    load_sem,
+    ag_send,
+    ag_recv,
+    rs_send,
+    rs_recv,
+):
+    line = Line(count, [(mod_ref, mod_all)], [(part, land)], (ag_send, ag_recv), (rs_send, rs_recv))
+    loads = (
+        pltpu.make_async_copy(weight_hbm, weight, load_sem.at[0]),
+        pltpu.make_async_copy(last_hbm, last, load_sem.at[1]),
+    )
+    for load in loads:
+        load.start()
+    line.barrier()
+    line.start_own()
+    mod_all[line.place] = mod_ref[...]
+    for load in loads:
+        load.wait()
+    inner = last.shape[0]
+    heads = inner // LANES
+    wide_size, wide_count = cut(last.shape[1], 384)
+
+    def compute(item):
+        project(mod_all[item], weight, raw)
+        tables = (tables_ref[0], tables_ref[1], tables_ref[2])
+
+        @pl.loop(0, heads)
+        def _(head):
+            query_raw = raw[:, span(head, LANES)]
+            key_raw = raw[:, span(heads + head, LANES)]
+            values = raw[:, span(2 * heads + head, LANES)].astype(jnp.bfloat16)
+            queries = turn(unit_norm(query_raw)[0] * gains_ref[0:1, :], tables)
+            keys = turn(unit_norm(key_raw)[0] * gains_ref[1:2, :], tables)
+            probs = soft(queries.astype(jnp.bfloat16), keys.astype(jnp.bfloat16))
+            mixed[:, span(head, LANES)] = dot(probs.astype(jnp.bfloat16), values).astype(
+                jnp.bfloat16
+            )
+
+        @pl.loop(0, wide_count)
+        def _(index):
+            cols = span(index, wide_size)
+            part[item, :, cols] = dot(mixed[...], last[:, cols]).astype(jnp.bfloat16)
+
+    @pl.loop(0, count)
+    def _(step):
+        @pl.when(step > 0)
+        def _():
+            line.receive(step)
+
+        for item, valid in line.items(step):
+
+            @pl.when(valid)
+            def _():
+                compute(item)
+
+        @pl.when(step > 0)
+        def _():
+            line.pass_sums(step)
+
+    mod_out[...] = mod_all[...]
+    line.finish(0, branch_out)
+    line.drain()
+
+
+def attend_back_kernel(
+    count,
+    grad_ref,
+    mod_all,
+    tables_ref,
+    gains_ref,
+    weight_hbm,
+    last_hbm,
+    back_out,
+    weight_out,
+    gain_out,
+    weight,
+    last,
+    grad_all,
+    raw,
+    mixed,
+    mixed_grad,
+    raw_grad,
+    part,
+    land,
+    total,
+    load_sem,
+    ag_send,
+    ag_recv,
+    rs_send,
+    rs_recv,
+):
+    line = Line(count, [(grad_ref, grad_all)], [(part, land)], (ag_send, ag_recv), (rs_send, rs_recv))
+    loads = (
+        pltpu.make_async_copy(weight_hbm, weight, load_sem.at[0]),
+        pltpu.make_async_copy(last_hbm, last, load_sem.at[1]),
+    )
+    for load in loads:
+        load.start()
+    line.barrier()
+    line.start_own()
+    grad_all[line.place] = grad_ref[...]
+    total[...] = jnp.zeros_like(total)
+    gain_out[...] = jnp.zeros_like(gain_out)
+    for load in loads:
+        load.wait()
+    inner, width = last.shape
+    heads = inner // LANES
+    scale = HD ** (-0.5)
+    wide_size, wide_count = cut(width, 384)
+    inner_size, inner_count = cut(inner, 256)
+    tall_size, tall_count = cut(width, 128)
+
+    def compute(item):
+        project(mod_all[item], weight, raw)
+        tables = (tables_ref[0], tables_ref[1], tables_ref[2])
+
+        @pl.loop(0, inner_count)
+        def _(index):
+            cols = span(index, inner_size)
+            mixed_grad[:, cols] = dot_rt(grad_all[item], last[cols, :]).astype(jnp.bfloat16)
+
+        @pl.loop(0, heads)
+        def _(head):
+            query_norm, query_inverse = unit_norm(raw[:, span(head, LANES)])
+            key_norm, key_inverse = unit_norm(raw[:, span(heads + head, LANES)])
+            values = raw[:, span(2 * heads + head, LANES)].astype(jnp.bfloat16)
+            queries = turn(query_norm * gains_ref[0:1, :], tables).astype(jnp.bfloat16)
+            keys = turn(key_norm * gains_ref[1:2, :], tables).astype(jnp.bfloat16)
+            probs = soft(queries, keys)
+            probs_low = probs.astype(jnp.bfloat16)
+            mixed[item, :, span(head, LANES)] = dot(probs_low, values).astype(jnp.bfloat16)
+            grad = mixed_grad[:, span(head, LANES)]
+            prob_grad = dot_rt(grad, values)
+            score_grad = (
+                probs * (prob_grad - jnp.sum(probs * prob_grad, axis=-1, keepdims=True))
+            ).astype(jnp.bfloat16)
+
+            def back(which, value_grad, norm, inverse):
+                turned = turn_back(value_grad, tables)
+                gained = turned * norm
+                gain_out[which] += jnp.sum(gained.reshape(-1, 8, LANES), axis=0)
+                scaled = turned * gains_ref[which : which + 1, :]
+                mean = jnp.sum(scaled * norm, axis=-1, keepdims=True) * (1.0 / HD)
+                raw_grad[item, :, span(which * heads + head, LANES)] = (
+                    inverse * (scaled - norm * mean)
+                ).astype(jnp.bfloat16)
+
+            back(0, dot(score_grad, keys) * scale, query_norm, query_inverse)
+            back(1, dot_lt(score_grad, queries) * scale, key_norm, key_inverse)
+            raw_grad[item, :, span(2 * heads + head, LANES)] = dot_lt(probs_low, grad).astype(
+                jnp.bfloat16
+            )
+
+        @pl.loop(0, wide_count)
+        def _(index):
+            cols = span(index, wide_size)
+            part[item, :, cols] = dot_rt(raw_grad[item], weight[cols, :]).astype(jnp.bfloat16)
+
+    def weigh(item):
+        @pl.loop(0, tall_count)
+        def _(index):
+            rows = span(index, tall_size)
+            total[rows, : 3 * inner] += dot_lt(mod_all[item, :, rows], raw_grad[item])
+            total[rows, 3 * inner :] += dot_lt(grad_all[item, :, rows], mixed[item])
+
+    @pl.loop(0, count)
+    def _(step):
+        @pl.when(step > 0)
+        def _():
+            for item, valid in line.items(step - 1):
+
+                @pl.when(valid)
+                def _():
+                    weigh(item)
+
+            line.receive(step)
+
+        for item, valid in line.items(step):
+
+            @pl.when(valid)
+            def _():
+                compute(item)
+
+        @pl.when(step > 0)
+        def _():
+            line.pass_sums(step)
+
+    for item, valid in line.items(count - 1):
+
+        @pl.when(valid)
+        def _():
+            weigh(item)
+
+    weight_out[...] = total[...].astype(jnp.bfloat16)
+    line.finish(0, back_out)
+    line.drain()
+
+
+def attend_arrays(project_weight, output_weight, query_gain, key_gain, length):
+    width, _, inner = project_weight.shape
+    heads = inner // HD
+    pad = LANES - HD
+    weight = jnp.pad(project_weight.reshape(width, 3, heads, HD), ((0, 0),) * 3 + ((0, pad),))
+    last = jnp.pad(output_weight.reshape(heads, HD, width), ((0, 0), (0, pad), (0, 0)))
+    gains = jnp.pad(jnp.stack([query_gain, key_gain]).astype(jnp.float32), ((0, 6), (0, pad)))
+    return (
+        turn_tables(length),
+        gains,
+        weight.reshape(width, 3 * heads * LANES),
+        last.reshape(heads * LANES, width),
+    )
+
+
+def line_sems(count, gathers, sums):
+    return [
+        pltpu.SemaphoreType.DMA((2,)),
+        pltpu.SemaphoreType.DMA((gathers, 2, count)),
+        pltpu.SemaphoreType.DMA((gathers, 2, count)),
+        pltpu.SemaphoreType.DMA((sums, 2, count, CHUNKS)),
+        pltpu.SemaphoreType.DMA((sums, 2, count, CHUNKS)),
+    ]
+
+
+def attend_pass(mod_in, arrays):
+    count = lax.axis_size("tensor")
+    weight, last = arrays[2:]
+    item = mod_in.shape
+    vmem, any_space = pl.BlockSpec(memory_space=pltpu.VMEM), pl.BlockSpec(memory_space=pl.ANY)
+    low = jnp.bfloat16
+    return pl.pallas_call(
+        functools.partial(attend_kernel, count),
+        out_shape=(
+            jax.ShapeDtypeStruct(item, jnp.float32),
+            jax.ShapeDtypeStruct((count, *item), low),
+        ),
+        in_specs=[vmem, vmem, vmem, any_space, any_space],
+        out_specs=(vmem, vmem),
+        scratch_shapes=[
+            pltpu.VMEM(weight.shape, low),
+            pltpu.VMEM(last.shape, low),
+            pltpu.VMEM((count, *item), low),
+            pltpu.VMEM((item[0], weight.shape[1]), jnp.float32),
+            pltpu.VMEM((item[0], last.shape[0]), low),
+            pltpu.VMEM((count, *item), low),
+            pltpu.VMEM((count + 1, *item), low),
+            *line_sems(count, 1, 1),
+        ],
+        compiler_params=pltpu.CompilerParams(
+            collective_id=6, has_side_effects=True, vmem_limit_bytes=60000000
+        ),
+        name="attend_pass",
+    )(mod_in, *arrays)
+
+
+def attend_back_pass(attend_grad, mod_all, arrays):
+    count = lax.axis_size("tensor")
+    weight, last = arrays[2:]
+    item = attend_grad.shape
+    inner = last.shape[0]
+    vmem, any_space = pl.BlockSpec(memory_space=pltpu.VMEM), pl.BlockSpec(memory_space=pl.ANY)
+    low = jnp.bfloat16
+    return pl.pallas_call(
+        functools.partial(attend_back_kernel, count),
+        out_shape=(
+            jax.ShapeDtypeStruct(item, jnp.float32),
+            jax.ShapeDtypeStruct((item[1], 4 * inner), low),
+            jax.ShapeDtypeStruct((2, 8, LANES), jnp.float32),
+        ),
+        in_specs=[vmem, vmem, vmem, vmem, any_space, any_space],
+        out_specs=(vmem, vmem, vmem),
+        scratch_shapes=[
+            pltpu.VMEM(weight.shape, low),
+            pltpu.VMEM(last.shape, low),
+            pltpu.VMEM((count, *item), low),
+            pltpu.VMEM((item[0], weight.shape[1]), jnp.float32),
+            pltpu.VMEM((count, item[0], inner), low),
+            pltpu.VMEM((item[0], inner), low),
+            pltpu.VMEM((count, item[0], 3 * inner), low),
+            pltpu.VMEM((count, *item), low),
+            pltpu.VMEM((count + 1, *item), low),
+            pltpu.VMEM((item[1], 4 * inner), jnp.float32),
+            *line_sems(count, 1, 1),
+        ],
+        compiler_params=pltpu.CompilerParams(
+            collective_id=7, has_side_effects=True, vmem_limit_bytes=60000000
+        ),
+        cost_estimate=pl.CostEstimate(
+            flops=int(4e10), bytes_accessed=int(2e8), transcendentals=int(1e6)
+        ),
+        name="attend_back_pass",
+    )(attend_grad, mod_all, *arrays)
 
 
 def shards(
@@ -605,38 +973,10 @@
     positions = jnp.arange(length)
     token_local = tokens.astype(jnp.float32)
     normed_local, inverse_local = layer_norm(token_local)
-    mod_in = lax.all_gather(
-        (normed_local * (1.0 + attend_scale) + attend_shift).astype(jnp.bfloat16),
-        "tensor",
-        axis=0,
-        tiled=True,
-    )
-    projected = jnp.einsum(
-        "bld,dke->blke", mod_in, project_weight, preferred_element_type=jnp.float32
-    )
-    split = projected.reshape(items, length, 3, heads_here, HD)
-    query_gain_f = query_gain.astype(jnp.float32)
-    key_gain_f = key_gain.astype(jnp.float32)
-    queries = head_prepare(split[:, :, 0], query_gain_f, positions).astype(jnp.bfloat16)
-    keys = head_prepare(split[:, :, 1], key_gain_f, positions).astype(jnp.bfloat16)
-    values = split[:, :, 2].astype(jnp.bfloat16)
-    scores = (
-        jnp.einsum("bqhd,bkhd->bhqk", queries, keys, preferred_element_type=jnp.float32) * scale
-    )
-    top = jnp.max(scores, axis=-1, keepdims=True)
-    logsum = top + jnp.log(jnp.sum(jnp.exp(scores - top), axis=-1, keepdims=True))
-    probs = jnp.exp(scores - logsum).astype(jnp.bfloat16)
-    mixed = jnp.einsum("bhqk,bkhd->bqhd", probs, values, preferred_element_type=jnp.float32)
-    mixed = mixed.reshape(items, length, heads_here * HD).astype(jnp.bfloat16)
-    piece = mixed
-    attend_branch = lax.psum_scatter(
-        jnp.einsum("blh,hd->bld", piece, output_weight, preferred_element_type=jnp.float32).astype(
-            jnp.bfloat16
-        ),
-        "tensor",
-        scatter_dimension=0,
-        tiled=True,
-    ).astype(jnp.float32) + output_bias.astype(jnp.float32)
+    mod_in = normed_local * (1.0 + attend_scale) + attend_shift
+    arrays = attend_arrays(project_weight, output_weight, query_gain, key_gain, length)
+    attend_total, mod_all = attend_pass(mod_in[0].astype(jnp.bfloat16), arrays)
+    attend_branch = attend_total[None] + output_bias.astype(jnp.float32)
     residual = token_local + attend_gate * attend_branch
     normed_two, inverse_two = layer_norm(residual)
     mod_two = (normed_two * (1.0 + feed_scale) + feed_shift).astype(jnp.bfloat16)
@@ -654,53 +994,9 @@
     )
     attend_grad = (residual_grad * attend_gate).astype(jnp.bfloat16)
     output_bias_part = jnp.sum(attend_grad.astype(jnp.float32), axis=(0, 1))
-    piece = lax.all_gather(attend_grad, "tensor", axis=0, tiled=True)
-    weight_total = jnp.einsum("blh,bld->hd", mixed, piece, preferred_element_type=jnp.float32)
-    rows_grad = jnp.einsum("bld,hd->blh", piece, output_weight, preferred_element_type=jnp.float32)
-    output_weight_grad = weight_total
-    mixed_grad = rows_grad
-    mixed_grad = mixed_grad.reshape(items, length, heads_here, HD).astype(jnp.bfloat16)
-    again = jnp.einsum("bqhd,bkhd->bhqk", queries, keys, preferred_element_type=jnp.float32) * scale
-    prob_float = jnp.exp(again - logsum)
-    prob_low = prob_float.astype(jnp.bfloat16)
-    prob_grad = jnp.einsum(
-        "bqhd,bkhd->bhqk", mixed_grad, values, preferred_element_type=jnp.float32
-    )
-    score_grad = (
-        prob_float * (prob_grad - jnp.sum(prob_float * prob_grad, axis=-1, keepdims=True))
-    ).astype(jnp.bfloat16)
-    query_grad = (
-        jnp.einsum("bhqk,bkhd->bqhd", score_grad, keys, preferred_element_type=jnp.float32) * scale
-    )
-    key_grad = (
-        jnp.einsum("bhqk,bqhd->bkhd", score_grad, queries, preferred_element_type=jnp.float32)
-        * scale
-    )
-    value_grad = jnp.einsum(
-        "bhqk,bqhd->bkhd", prob_low, mixed_grad, preferred_element_type=jnp.float32
-    )
-
-    def prepare_here(raw, gain):
-        return head_prepare(raw, gain, positions)
-
-    _, query_back = jax.vjp(prepare_here, split[:, :, 0], query_gain_f)
-    raw_query_grad, query_gain_part = query_back(query_grad)
-    _, key_back = jax.vjp(prepare_here, split[:, :, 1], key_gain_f)
-    raw_key_grad, key_gain_part = key_back(key_grad)
-    projected_grad = jnp.stack([raw_query_grad, raw_key_grad, value_grad], axis=2)
-    projected_grad = projected_grad.reshape(items, length, 3, heads_here * HD).astype(jnp.bfloat16)
-    project_grad = jnp.einsum(
-        "bld,blke->dke", mod_in, projected_grad, preferred_element_type=jnp.float32
-    )
-    piece = projected_grad
-    mod_in_grad = lax.psum_scatter(
-        jnp.einsum(
-            "blke,dke->bld", piece, project_weight, preferred_element_type=jnp.float32
-        ).astype(jnp.bfloat16),
-        "tensor",
-        scatter_dimension=0,
-        tiled=True,
-    ).astype(jnp.float32)
+    mod_in_grad, attend_weights, gain_parts = attend_back_pass(attend_grad[0], mod_all, arrays)
+    mod_in_grad = mod_in_grad[None]
+    query_gain_part, key_gain_part = jnp.sum(gain_parts, axis=1)[:, :HD]
     tokens_grad = (
         residual_grad
         + layer_norm_back(normed_local, inverse_local, mod_in_grad * (1.0 + attend_scale))
@@ -804,8 +1100,11 @@
             jnp.float32
         )
 
-    project_grad = scatter(project_grad, 0)
-    output_weight_grad = scatter(output_weight_grad, 1)
+    inner = heads_here * HD
+    attend_weights = attend_weights.reshape(width, 4 * heads_here, LANES)[:, :, :HD]
+    attend_weights = scatter(attend_weights.reshape(width, 4 * inner), 0)
+    project_grad = attend_weights[:, : 3 * inner].reshape(-1, 3, inner)
+    output_weight_grad = attend_weights[:, 3 * inner :].T
     feed_weights = scatter(feed_weights, 1)
     expand_grad = jnp.transpose(feed_weights[:2], (1, 0, 2))
     down_grad = feed_weights[2].T

time: 611 us -> 487 us (0.80); the launches traced: 601 us -> 485 us
  waiting for transfers between devices: 296 us -> 30.5 us
  Pallas kernels: 165 us -> 325 us
  local copies, waits for them, and re-layouts: 30.3 us -> 65.4 us
  matrix products: 47.5 us -> 16.7 us
  other arithmetic: 44.6 us -> 31.7 us
    pallas_call x0 -> x2, Pallas kernels: none -> 169 us  [the longest x1 93.3 us: attend_back_pass(): pl.pallas_call(functools.partial(attend_back_kernel, count), out_shape=(j...]
    all_gather x2 -> x0, waiting for transfers between devices: 99.6 us -> none  [the longest x1 50.7 us: shards(): lax.all_gather((normed_local * (1.0 + attend_scale) + attend_shift).astyp...]
    reduce_scatter x2 -> x0, waiting for transfers between devices: 84.2 us -> none  [the longest x1 46.4 us: shards(): lax.psum_scatter(jnp.einsum('blke,dke->bld', piece, project_weight, prefe...]
    reduce_scatter x3 -> x1, waiting for transfers between devices: 112 us -> 30 us  [scatter(): lax.psum_scatter(value, 'dp', scatter_dimension=axis, tiled=True)]
    dot_general x12 -> x0, matrix products: 33.6 us -> none  [the longest x1 6.63 us: shards(): jnp.einsum('blke,dke->bld', piece, project_weight, preferred_element_type...]
    reshape x0 -> x3, local copies, waits for them, and re-layouts: none -> 20.9 us  [the longest x1 7.2 us: attend_arrays(): project_weight.reshape(width, 3, heads, HD)]
    pallas_call x1, Pallas kernels: 124 us -> 115 us  [feed_pass(): pl.pallas_call(functools.partial(feed_kernel, count), out_shape=(jax.Shap...]
    pad x0 -> x2, local copies, waits for them, and re-layouts: none -> 7.85 us  [the longest x1 5.59 us: attend_arrays(): jnp.pad(project_weight.reshape(width, 3, heads, HD), ((0, 0),) * 3 + ((0,...]
  transfers between devices with their start and end apart: 7 -> 2, of which waited for: 7 -> 1; matrix products, arithmetic and copies ran while one was open for 5% -> 8% of each run, Pallas kernels for 0% -> 7%
where the time goes in v4:
time: 487 us; the launch traced here: 485 us
  Pallas kernels  325 us (67%)
  local copies, waits for them, and re-layouts  65.4 us (13%)
  other arithmetic  31.7 us (7%)
  waiting for transfers between devices  30.5 us (6%)
  matrix products  16.7 us (3%)
  between operations  15.2 us (3%)
    pallas_call x1, Pallas kernels, feed_pass(): pl.pallas_call(functools.partial(feed_kernel, count), out_shape=(jax.Shap...  115 us
    pallas_call x1, Pallas kernels, attend_back_pass(): pl.pallas_call(functools.partial(attend_back_kernel, count), out_shape=(j...  93.3 us
    pallas_call x1, Pallas kernels, attend_pass(): pl.pallas_call(functools.partial(attend_kernel, count), out_shape=(jax.Sh...  76.1 us
    pallas_call x4, Pallas kernels, swap(): pl.pallas_call(functools.partial(swap_kernel, tuple(plan), int(total is n...  41.3 us
    reduce_scatter x1, waiting for transfers between devices, scatter(): lax.psum_scatter(value, 'dp', scatter_dimension=axis, tiled=True)  30 us
    unnamed x58, local copies, waits for them, and re-layouts  14.8 us
  transfers between devices with their start and end apart: 2, of which 1 were waited for; matrix products, arithmetic and copies ran while one was open for 8% of the time, Pallas kernels for 7%

profile of v4, /device:TPU:0, one launch (start us, length us, event | category | flops | bytes accessed | tf_op | source)
XLA Modules:
  0.0 485.2 jit_solution(14328926229123288340)
XLA Ops:
  11.6 2.5 gather_fusion
  15.9 3.5 fusion.46
  20.1 8.7 %modulation_swap.1 = bf16[4,6,288]{2,1,0:T(8,128)(2,1)} custom-call(bf16[4,6,288]{2,1,0:T(8,128)(2,1)} %fusion.36.refs_0_), custom_call_target="tpu_custom_call" | custom-call | tf_op jit(solution)/shard_map/modulation_swap/pallas_call | solution.py:542
  30.9 7.2 %copy.61 = bf16[1152,3,4,72]{3,2,1,0:T(4,128)(2,1)} copy(bf16[1152,3,4,72]{0,3,2,1:T(8,128)(2,1)} %bitcast.101) | data formatting | bytes 3981312 | tf_op jit(solution)/shard_map/reshape | solution.py:830
  38.1 5.6 %pad.20 = bf16[1152,3,4,128]{3,2,1,0:T(4,128)(2,1)} pad(bf16[1152,3,4,72]{3,2,1,0:T(4,128)(2,1)} %copy.61, bf16[]{:T(256)} %constant.121.clone.1), padding=0_0x0_0x0_0x0_56 | pad | bytes 5529602 | tf_op jit(solution)/shard_map/jit(_pad)/pad | solution.py:830
  43.7 6.9 %reshape.646.weight_hbm = bf16[1152,1536]{1,0:T(8,128)(2,1)} reshape(bf16[1152,3,4,128]{3,2,1,0:T(4,128)(2,1)} %pad.20) | data formatting | bytes 7077888 | tf_op jit(solution)/shard_map/reshape | solution.py:836
  50.6 2.3 pad.21
  56.2 76.1 %attend_pass.1 = (f32[256,1152]{1,0:T(8,128)}, bf16[4,256,1152]{2,1,0:T(8,128)(2,1)}) custom-call(bf16[256,1152]{1,0:T(8,128)(2,1)} %get-tuple-element.136.mod_ref, f32[3,256,128]{2,1,0:T(8,128)} %pad_maximum_fusion.tables_ref, f32[8,128]{1,0:T(8,128)} %fusion.58.gains_ref, bf16[1152,1536]{1,0:T(8,128)(2,1)} %reshape.646.weight_hbm, bf16[512,1152]{1,0:T(8,128)(2,1)} %bitcast.98), custom_call_target="tpu_custom_call" | custom-call | tf_op jit(solution)/shard_map/attend_pass/pallas_call | solution.py:857
  132.3 1.7 fusion.78
  134.7 2.2 copy.89
  138.0 114.7 %feed_pass.1 = (f32[256,1152]{1,0:T(8,128)}, f32[256,1152]{1,0:T(8,128)}, bf16[3,1152,768]{2,1,0:T(8,128)(2,1)}) custom-call(bf16[256,1152]{1,0:T(8,128)(2,1)} %fusion.26.mod_ref, bf16[256,1152]{1,0:T(8,128)(2,1)} %get-tuple-element.137.grad_ref, bf16[2,1152,768]{2,1,0:T(8,128)(2,1)} %bitcast.95, bf16[768,1152]{1,0:T(8,128)(2,1)} %down_hbm.1), custom_call_target="tpu_custom_call" | custom-call | tf_op jit(solution)/shard_map/feed_pass/pallas_call | solution.py:402
  252.7 1.6 fusion.75
  254.3 1.9 fusion.19
  256.3 3.6 convert_reduce_fusion.1
  261.8 93.3 %attend_back_pass.1 = (f32[256,1152]{1,0:T(8,128)}, bf16[1152,2048]{1,0:T(8,128)(2,1)}, f32[2,8,128]{2,1,0:T(8,128)}) custom-call(bf16[256,1152]{1,0:T(8,128)(2,1)} %fusion.29.grad_ref, bf16[4,256,1152]{2,1,0:T(8,128)(2,1)} %get-tuple-element.32.mod_all, f32[3,256,128]{2,1,0:T(8,128)} %pad_maximum_fusion.tables_ref, f32[8,128]{1,0:T(8,128)} %fusion.58.gains_ref, ...), custom_call_target="tpu_custom_call" | custom-call | flops 40000000000 | bytes 200000000 | tf_op jit(solution)/shard_map/attend_back_pass/pallas_call | solution.py:889
  355.2 6.7 %copy.76 = bf16[1152,2048]{0,1:T(8,128)(2,1)} copy(bf16[1152,2048]{1,0:T(8,128)(2,1)} %get-tuple-element.34) | data formatting | bytes 9437184 | tf_op jit(solution)/shard_map/reshape | solution.py:1104
  361.9 3.5 slice.112
  365.3 5.2 %copy.79 = bf16[1152,1152]{1,0:T(8,128)(2,1)} copy(bf16[1152,1152]{0,1:T(8,128)(2,1)} %bitcast.97) | data formatting | bytes 5308416
  371.4 2.1 fusion.76
  373.6 2.5 fusion.16
  378.1 13.2 %sums_swap.1 = (bf16[4,6,288]{2,1,0:T(8,128)(2,1)}, f32[80,128]{1,0:T(8,128)}) custom-call(bf16[4,6,288]{2,1,0:T(8,128)(2,1)} %bitcast.103, f32[80,128]{1,0:T(8,128)} %pad_bitcast_fusion.refs_1_), custom_call_target="tpu_custom_call" | custom-call | tf_op jit(solution)/shard_map/sums_swap/pallas_call | solution.py:542
  392.1 3.4 convolution_bitcast_fusion.refs_0_
  395.5 7.3 %condition_swap.1 = f32[4,4,1152]{2,1,0:T(4,128)} custom-call(f32[4,1152]{1,0:T(4,128)} %convolution_bitcast_fusion.refs_0_), custom_call_target="tpu_custom_call" | custom-call | tf_op jit(solution)/shard_map/condition_swap/pallas_call | solution.py:542
  405.6 12.1 %items_swap.1 = (bf16[8,4,6592]{2,1,0:T(4,128)(2,1)}, s32[8,4,128]{2,1,0:T(4,128)}) custom-call(bf16[4,6592]{1,0:T(4,128)(2,1)} %copy-done.15, s32[4,128]{1,0:T(4,128)} %broadcast_in_dim.105.refs_1_), custom_call_target="tpu_custom_call" | custom-call | tf_op jit(solution)/shard_map/items_swap/pallas_call | solution.py:542
  417.7 1.9 reshape.655
  430.1 1.7 fusion.38
  431.8 1.9 fusion.34
  433.7 2.2 fusion.41
  435.9 1.5 fusion.30
  441.7 1.8 copy.74
  444.7 30.0 %reduce-scatter.5.cloned.1.call-done = bf16[3,144,768]{2,1,0:T(8,128)(2,1)} async-done(((bf16[3,1152,768]{2,1,0:T(8,128)(2,1)}), bf16[3,144,768]{2,1,0:T(8,128)(2,1)}) %reduce-scatter.5.cloned.1.call-update) | async-done | bytes 663568 | tf_op jit(solution)/shard_map/reduce_scatter | solution.py:1099
  476.7 1.6 copy.75
  (145 shorter events, 39.6 us)
Async XLA Ops:
  7.2 8.2 %copy-start = (bf16[1152,1152]{1,0:T(8,128)(2,1)S(1)}, bf16[1152,1152]{1,0:T(8,128)(2,1)}, u32[]{:S(2)}) copy-start(bf16[1152,1152]{1,0:T(8,128)(2,1)} %param.37) | copy-start | bytes 7962628
  7.2 431.5 %reduce-scatter.7.cloned.1.call-start = ((), (), s32[]{:S(2)}) async-start(), calls=%async_computation.3 | async-start | bytes 2985984
  15.9 13.8 %copy-start.3 = (bf16[1,256,1152]{2,1,0:T(8,128)(2,1)S(1)}, bf16[1,256,1152]{2,1,0:T(8,128)(2,1)}, u32[]{:S(2)}) copy-start(bf16[1,256,1152]{2,1,0:T(8,128)(2,1)} %param.20) | copy-start | bytes 1769476
  29.7 343.8 %copy-start.13 = (f32[1152]{0:T(1024)}, f32[1152]{0:T(1024)S(1)}, u32[]{:S(2)}) copy-start(f32[1152]{0:T(1024)S(1)} %get-tuple-element.108) | copy-start | bytes 13828
  29.9 343.6 %copy-start.16 = (f32[256]{0:T(256)}, f32[256]{0:T(256)S(1)}, u32[]{:S(2)}) copy-start(f32[256]{0:T(256)S(1)} %broadcast_multiply_fusion.5) | copy-start | bytes 3076
  30.2 343.3 %copy-start.18 = (f32[256]{0:T(256)}, f32[256]{0:T(256)S(1)}, u32[]{:S(2)}) copy-start(f32[256]{0:T(256)S(1)} %add_rsqrt_fusion.1) | copy-start | bytes 3076
  50.6 2.3 copy-start.21
  50.6 2.3 copy-start.23
  50.6 2.3 copy-start.24
  50.6 4.2 copy-start.12
  132.3 2.4 copy-start.10
  134.0 2.9 copy-start.1
  252.7 1.6 copy-start.2
  254.3 1.9 copy-start.22
  254.3 1.9 copy-start.6
  254.3 2.0 copy-start.9
  259.9 1.0 copy-start.7
  370.6 104.1 %reduce-scatter.5.cloned.1.call-start = ((), (), s32[]{:S(2)}) async-start(), calls=%async_computation.2 | async-start | bytes 5971968 | tf_op jit(solution)/shard_map/reduce_scatter | solution.py:1099
  371.3 2.2 copy-start.4
  373.5 3.2 copy-start.20
  403.8 1.1 copy-start.25
  404.9 0.7 copy-start.15
  431.8 5.6 %copy-start.8 = (f32[1,256,1152]{2,1,0:T(8,128)S(1)}, f32[1,256,1152]{2,1,0:T(8,128)}, u32[]{:S(2)}) copy-start(f32[1,256,1152]{2,1,0:T(8,128)} %copy-done.7) | copy-start | bytes 3538948
  433.7 3.7 copy-start.5
  433.7 3.7 copy-start.14
  433.7 3.7 copy-start.17
  433.7 3.7 copy-start.19
  441.0 2.5 copy-start.11
Sparse Core Ops, SparseCore 0:
  370.7 44.2 reduce-scatter.6
  418.4 56.2 reduce-scatter.4

commit v5 on v4

--- a/solution.py
+++ b/solution.py
@@ -81,7 +81,7 @@
         self.ag_send, self.ag_recv = ag_sems
         self.rs_send, self.rs_recv = rs_sems
 
-    def barrier(self):
+    def barrier(self, wide=1):
         place, count = self.place, self.count
         sem = pltpu.get_barrier_semaphore()
 
@@ -94,7 +94,14 @@
             pl.semaphore_signal(sem, inc=1, device_id={"tensor": place + 1})
 
         peers = jnp.where(place > 0, 1, 0) + jnp.where(place < count - 1, 1, 0)
-        pl.semaphore_wait(sem, peers)
+        here = lax.axis_index("dp")
+
+        @pl.loop(1, wide)
+        def _(offset):
+            peer = lax.rem(here + offset, wide)
+            pl.semaphore_signal(sem, inc=1, device_id={"dp": peer})
+
+        pl.semaphore_wait(sem, peers + (wide - 1))
 
     def item_copy(self, which, way, item, own=False):
         mine, everyone = self.gathered[which]
@@ -168,34 +175,29 @@
         low, high = place - step, place + step
         return ((low, (low >= 0)), (high, (high < count) & (step > 0)))
 
-    def pass_sums(self, step):
+    def moves(self, step):
         place, count = self.place, self.count
-        ways = []
-        for way in range(2):
-            item = step if way == 0 else count - 1 - step
-            ways.append(
-                (
-                    way,
-                    item,
-                    item > place if way == 0 else item < place,
-                    place if way == 0 else count - 1 - place,
-                )
-            )
-
+        return (
+            (0, step, step > place, place),
+            (1, count - 1 - step, count - 1 - step < place, count - 1 - place),
+        )
+
+    def first_sums(self, step):
         @pl.loop(0, CHUNKS)
         def _(block):
-            for way, item, further, hop in ways:
+            for way, item, further, hop in self.moves(step):
 
                 @pl.when(further & (hop == 0))
                 def _():
                     for which in range(len(self.summed)):
                         self.sum_copy(which, way, item, block).start()
 
-        @pl.loop(0, CHUNKS + count - 3)
+    def relay_sums(self, step):
+        @pl.loop(0, CHUNKS + self.count - 3)
         def _(turn):
-            for distance in range(1, count - 1):
+            for distance in range(1, self.count - 1):
                 block = turn - (distance - 1)
-                for way, item, further, hop in ways:
+                for way, item, further, hop in self.moves(step):
 
                     @pl.when(further & (hop == distance) & (block >= 0) & (block < CHUNKS))
                     def _():
@@ -208,6 +210,15 @@
                             )
                             part[item, rows] = total.astype(part.dtype)
                             self.sum_copy(which, way, item, block).start()
+
+    def near(self, step):
+        place, count = self.place, self.count
+        low = place >= step
+        return jnp.where(low, place - step, place + step), low | (place + step < count)
+
+    def far(self, step):
+        place, count = self.place, self.count
+        return place + step, (step > 0) & (place >= step) & (place + step < count)
 
     def finish(self, which, out):
         place, count = self.place, self.count
@@ -377,7 +388,8 @@
 
         @pl.when(step > 0)
         def _():
-            line.pass_sums(step)
+            line.first_sums(step)
+            line.relay_sums(step)
 
     for item, valid in line.items(count - 1):
 
@@ -551,6 +563,7 @@
 
 
 LANES = 128
+HEAD_UNROLL = 2
 
 
 def turn(value, tables):
@@ -595,18 +608,14 @@
 
 
 def project(mod, weight, raw):
-    size, number = cut(weight.shape[1], 512)
-
-    @pl.loop(0, number)
+    @pl.loop(0, weight.shape[0])
     def _(index):
-        cols = span(index, size)
-        raw[:, cols] = dot(mod, weight[:, cols])
+        raw[index] = dot(mod, weight[index])
 
 
 def soft(queries, keys):
-    scores = dot_rt(queries, keys) * (HD ** (-0.5))
-    shifted = jnp.exp(scores - jnp.max(scores, axis=-1, keepdims=True))
-    return shifted * (1.0 / jnp.sum(shifted, axis=-1, keepdims=True))
+    grown = jnp.exp2(dot_rt(queries, keys) * (HD ** (-0.5) / math.log(2.0)))
+    return grown * (1.0 / jnp.sum(grown, axis=-1, keepdims=True))
 
 
 def attend_kernel(
@@ -643,25 +652,21 @@
     mod_all[line.place] = mod_ref[...]
     for load in loads:
         load.wait()
-    inner = last.shape[0]
-    heads = inner // LANES
+    heads = last.shape[0] // LANES
     wide_size, wide_count = cut(last.shape[1], 384)
 
     def compute(item):
         project(mod_all[item], weight, raw)
         tables = (tables_ref[0], tables_ref[1], tables_ref[2])
 
-        @pl.loop(0, heads)
+        @pl.loop(0, heads, unroll=HEAD_UNROLL)
         def _(head):
-            query_raw = raw[:, span(head, LANES)]
-            key_raw = raw[:, span(heads + head, LANES)]
-            values = raw[:, span(2 * heads + head, LANES)].astype(jnp.bfloat16)
-            queries = turn(unit_norm(query_raw)[0] * gains_ref[0:1, :], tables)
-            keys = turn(unit_norm(key_raw)[0] * gains_ref[1:2, :], tables)
+            lanes = span(head, LANES)
+            queries = turn(unit_norm(raw[0, :, lanes])[0] * gains_ref[0:1, :], tables)
+            keys = turn(unit_norm(raw[1, :, lanes])[0] * gains_ref[1:2, :], tables)
             probs = soft(queries.astype(jnp.bfloat16), keys.astype(jnp.bfloat16))
-            mixed[:, span(head, LANES)] = dot(probs.astype(jnp.bfloat16), values).astype(
-                jnp.bfloat16
-            )
+            values = raw[2, :, lanes].astype(jnp.bfloat16)
+            mixed[:, lanes] = dot(probs.astype(jnp.bfloat16), values).astype(jnp.bfloat16)
 
         @pl.loop(0, wide_count)
         def _(index):
@@ -670,52 +675,79 @@
 
     @pl.loop(0, count)
     def _(step):
+        late, owed = line.far(step - 1)
+        item, valid = line.near(step)
+
         @pl.when(step > 0)
         def _():
             line.receive(step)
 
-        for item, valid in line.items(step):
-
-            @pl.when(valid)
+            @pl.when(owed)
             def _():
-                compute(item)
+                compute(late)
+
+        @pl.when(valid)
+        def _():
+            compute(item)
 
         @pl.when(step > 0)
         def _():
-            line.pass_sums(step)
+            line.first_sums(step)
+            line.relay_sums(step)
 
     mod_out[...] = mod_all[...]
     line.finish(0, branch_out)
     line.drain()
 
 
+def block_copy(array, target, slot, block, size, send, recv, peer):
+    rows = pl.ds(pl.multiple_of(block * size, size), size)
+    source = array.at[rows] if len(array.shape) == 2 else array.at[:, rows]
+    return pltpu.make_async_remote_copy(
+        src_ref=source,
+        dst_ref=target.at[slot],
+        send_sem=send,
+        recv_sem=recv,
+        device_id={"dp": peer},
+    )
+
+
 def attend_back_kernel(
     count,
+    wide,
     grad_ref,
     mod_all,
     tables_ref,
     gains_ref,
+    narrow_ref,
     weight_hbm,
     last_hbm,
-    back_out,
-    weight_out,
-    gain_out,
-    weight,
-    last,
-    grad_all,
-    raw,
-    mixed,
-    mixed_grad,
-    raw_grad,
-    part,
-    land,
-    total,
-    load_sem,
-    ag_send,
-    ag_recv,
-    rs_send,
-    rs_recv,
+    *rest,
 ):
+    if wide:
+        feed_hbm, back_out, weight_out, gain_out, feed_out, *rest = rest
+    else:
+        back_out, weight_out, gain_out, *rest = rest
+    (
+        weight,
+        last,
+        grad_all,
+        raw,
+        mixed,
+        mixed_grad,
+        raw_grad,
+        kept,
+        kept_mixed,
+        part,
+        land,
+        total,
+        load_sem,
+        ag_send,
+        ag_recv,
+        rs_send,
+        rs_recv,
+        *rest,
+    ) = rest
     line = Line(count, [(grad_ref, grad_all)], [(part, land)], (ag_send, ag_recv), (rs_send, rs_recv))
     loads = (
         pltpu.make_async_copy(weight_hbm, weight, load_sem.at[0]),
@@ -723,19 +755,49 @@
     )
     for load in loads:
         load.start()
-    line.barrier()
+    line.barrier(wide or 1)
     line.start_own()
+    width = last.shape[1]
+    here = lax.axis_index("dp")
+    if wide:
+        feed_land, staged, pair_land, quad_land, fs, fr, ps, pr, qs, qr = rest
+        size = width // wide
+        half = wide // 2
+        parity, seat = lax.rem(here, 2), here // 2
+        partner = here + 1 - 2 * parity
+
+        def feed_copy(peer, slot):
+            return block_copy(feed_hbm, feed_land, slot, peer, size, fs.at[peer], fr.at[slot], peer)
+
+        def pair_copy(index):
+            block = 2 * index + 1 - parity
+            return block_copy(
+                staged, pair_land, index, block, size, ps.at[index], pr.at[index], partner
+            )
+
+        def quad_copy(index, slot):
+            block = 2 * index + parity
+            return block_copy(
+                staged, quad_land, slot, block, size, qs.at[index], qr.at[slot], block
+            )
+
+        @pl.loop(1, wide)
+        def _(offset):
+            peer = lax.rem(here + offset, wide)
+            feed_copy(peer, here).start()
+
     grad_all[line.place] = grad_ref[...]
     total[...] = jnp.zeros_like(total)
     gain_out[...] = jnp.zeros_like(gain_out)
     for load in loads:
         load.wait()
-    inner, width = last.shape
+    inner = last.shape[0]
     heads = inner // LANES
     scale = HD ** (-0.5)
     wide_size, wide_count = cut(width, 384)
     inner_size, inner_count = cut(inner, 256)
     tall_size, tall_count = cut(width, 128)
+    first_width = kept.shape[2]
 
     def compute(item):
         project(mod_all[item], weight, raw)
@@ -746,17 +808,18 @@
             cols = span(index, inner_size)
             mixed_grad[:, cols] = dot_rt(grad_all[item], last[cols, :]).astype(jnp.bfloat16)
 
-        @pl.loop(0, heads)
+        @pl.loop(0, heads, unroll=HEAD_UNROLL)
         def _(head):
-            query_norm, query_inverse = unit_norm(raw[:, span(head, LANES)])
-            key_norm, key_inverse = unit_norm(raw[:, span(heads + head, LANES)])
-            values = raw[:, span(2 * heads + head, LANES)].astype(jnp.bfloat16)
+            lanes = span(head, LANES)
+            query_norm, query_inverse = unit_norm(raw[0, :, lanes])
+            key_norm, key_inverse = unit_norm(raw[1, :, lanes])
+            values = raw[2, :, lanes].astype(jnp.bfloat16)
             queries = turn(query_norm * gains_ref[0:1, :], tables).astype(jnp.bfloat16)
             keys = turn(key_norm * gains_ref[1:2, :], tables).astype(jnp.bfloat16)
             probs = soft(queries, keys)
             probs_low = probs.astype(jnp.bfloat16)
-            mixed[item, :, span(head, LANES)] = dot(probs_low, values).astype(jnp.bfloat16)
-            grad = mixed_grad[:, span(head, LANES)]
+            mixed[:, lanes] = dot(probs_low, values).astype(jnp.bfloat16)
+            grad = mixed_grad[:, lanes]
             prob_grad = dot_rt(grad, values)
             score_grad = (
                 probs * (prob_grad - jnp.sum(probs * prob_grad, axis=-1, keepdims=True))
@@ -768,74 +831,165 @@
                 gain_out[which] += jnp.sum(gained.reshape(-1, 8, LANES), axis=0)
                 scaled = turned * gains_ref[which : which + 1, :]
                 mean = jnp.sum(scaled * norm, axis=-1, keepdims=True) * (1.0 / HD)
-                raw_grad[item, :, span(which * heads + head, LANES)] = (
-                    inverse * (scaled - norm * mean)
-                ).astype(jnp.bfloat16)
+                raw_grad[which, :, lanes] = (inverse * (scaled - norm * mean)).astype(
+                    jnp.bfloat16
+                )
 
             back(0, dot(score_grad, keys) * scale, query_norm, query_inverse)
             back(1, dot_lt(score_grad, queries) * scale, key_norm, key_inverse)
-            raw_grad[item, :, span(2 * heads + head, LANES)] = dot_lt(probs_low, grad).astype(
-                jnp.bfloat16
-            )
+            raw_grad[2, :, lanes] = dot_lt(probs_low, grad).astype(jnp.bfloat16)
 
         @pl.loop(0, wide_count)
         def _(index):
             cols = span(index, wide_size)
-            part[item, :, cols] = dot_rt(raw_grad[item], weight[cols, :]).astype(jnp.bfloat16)
+            sums = dot_rt(raw_grad[0], weight[0, cols, :])
+            sums += dot_rt(raw_grad[1], weight[1, cols, :])
+            sums += dot_rt(raw_grad[2], weight[2, cols, :])
+            part[item, :, cols] = sums.astype(jnp.bfloat16)
+
+    def keep(item):
+        one = dot(raw_grad[0], narrow_ref[0])
+        two = dot(raw_grad[1], narrow_ref[1])
+        three = dot(raw_grad[2], narrow_ref[2])
+        side = one.shape[1] - LANES
+        low = jnp.bfloat16
+        kept[item, :, :side] = one[:, :side].astype(low)
+        kept[item, :, side : side + LANES] = (one[:, side:] + two[:, :LANES]).astype(low)
+        kept[item, :, side + LANES : 2 * side] = two[:, LANES:side].astype(low)
+        kept[item, :, 2 * side : 2 * side + LANES] = (two[:, side:] + three[:, :LANES]).astype(low)
+        kept[item, :, 2 * side + LANES :] = three[:, LANES:].astype(low)
+        kept_mixed[item] = dot(mixed[...], narrow_ref[0]).astype(low)
 
     def weigh(item):
         @pl.loop(0, tall_count)
         def _(index):
             rows = span(index, tall_size)
-            total[rows, : 3 * inner] += dot_lt(mod_all[item, :, rows], raw_grad[item])
-            total[rows, 3 * inner :] += dot_lt(grad_all[item, :, rows], mixed[item])
+            total[rows, :first_width] += dot_lt(mod_all[item, :, rows], kept[item])
+            total[rows, first_width:] += dot_lt(grad_all[item, :, rows], kept_mixed[item])
 
     @pl.loop(0, count)
     def _(step):
+        late, owed = line.far(step - 1)
+        item, valid = line.near(step)
+
         @pl.when(step > 0)
         def _():
-            for item, valid in line.items(step - 1):
-
-                @pl.when(valid)
-                def _():
-                    weigh(item)
+            older, kept_older = line.far(step - 2)
+            old, kept_old = line.near(step - 1)
+
+            @pl.when((step > 1) & kept_older)
+            def _():
+                weigh(older)
+
+            @pl.when(kept_old)
+            def _():
+                weigh(old)
 
             line.receive(step)
 
-        for item, valid in line.items(step):
-
+            @pl.when(owed)
+            def _():
+                compute(late)
+                keep(late)
+
+        @pl.when(valid)
+        def _():
+            compute(item)
+
+            @pl.when(step > 0)
+            def _():
+                line.first_sums(step)
+
+            keep(item)
+
+        @pl.when(step == count - 1)
+        def _():
             @pl.when(valid)
             def _():
-                compute(item)
+                weigh(item)
+
+            if wide:
+                staged[...] = total[...].astype(jnp.bfloat16)
+
+                @pl.loop(0, half)
+                def _(index):
+                    pair_copy(index).start()
 
         @pl.when(step > 0)
         def _():
-            line.pass_sums(step)
-
-    for item, valid in line.items(count - 1):
-
-        @pl.when(valid)
-        def _():
-            weigh(item)
-
-    weight_out[...] = total[...].astype(jnp.bfloat16)
+            line.relay_sums(step)
+
+    if wide:
+
+        @pl.loop(0, half)
+        def _(index):
+            pair_copy(index).wait_send()
+            pair_copy(index).wait_recv()
+            rows = pl.ds(pl.multiple_of((2 * index + parity) * size, size), size)
+            staged[rows] = (
+                staged[rows].astype(jnp.float32) + pair_land[index].astype(jnp.float32)
+            ).astype(jnp.bfloat16)
+
+        @pl.loop(1, half)
+        def _(offset):
+            index = lax.rem(seat + offset, half)
+            quad_copy(index, seat).start()
+
     line.finish(0, back_out)
     line.drain()
+    if wide:
+        rows = pl.ds(pl.multiple_of(here * size, size), size)
+        own = pltpu.make_async_copy(feed_hbm.at[:, rows], feed_land.at[here], load_sem.at[0])
+        own.start()
+
+        @pl.loop(1, wide)
+        def _(offset):
+            peer = lax.rem(here + offset, wide)
+            feed_copy(peer, here).wait_send()
+            feed_copy(here, peer).wait_recv()
+
+        own.wait()
+        for which in range(feed_out.shape[0]):
+            feed_out[which] = feed_land[0, which].astype(jnp.float32)
+
+            @pl.loop(1, wide)
+            def _(index):
+                feed_out[which] += feed_land[index, which].astype(jnp.float32)
+
+        weight_out[...] = staged[rows].astype(jnp.float32)
+
+        @pl.loop(1, half)
+        def _(offset):
+            index = lax.rem(seat + offset, half)
+            quad_copy(index, seat).wait_send()
+            quad_copy(seat, index).wait_recv()
+            weight_out[...] += quad_land[index].astype(jnp.float32)
+
+    else:
+        weight_out[...] = total[...].astype(jnp.bfloat16)
 
 
 def attend_arrays(project_weight, output_weight, query_gain, key_gain, length):
-    width, _, inner = project_weight.shape
+    inner = project_weight.shape[2]
     heads = inner // HD
+    low = jnp.bfloat16
+    spot = jnp.arange(heads * LANES)
+    real = spot % LANES < HD
+    column = spot // LANES * HD + spot % LANES
+    spread = (real[None] & (column[None] == jnp.arange(inner)[:, None])).astype(low)
+    window = -(-inner // LANES) * LANES
+    narrow = jnp.stack(
+        [
+            real[:, None]
+            & (column[:, None] + index * (inner % LANES) == jnp.arange(window)[None, :])
+            for index in range(3)
+        ]
+    ).astype(low)
+    weight = jnp.einsum("dke,eh->kdh", project_weight, spread, preferred_element_type=low)
+    last = jnp.einsum("ed,eh->hd", output_weight, spread, preferred_element_type=low)
     pad = LANES - HD
-    weight = jnp.pad(project_weight.reshape(width, 3, heads, HD), ((0, 0),) * 3 + ((0, pad),))
-    last = jnp.pad(output_weight.reshape(heads, HD, width), ((0, 0), (0, pad), (0, 0)))
     gains = jnp.pad(jnp.stack([query_gain, key_gain]).astype(jnp.float32), ((0, 6), (0, pad)))
-    return (
-        turn_tables(length),
-        gains,
-        weight.reshape(width, 3 * heads * LANES),
-        last.reshape(heads * LANES, width),
-    )
+    return turn_tables(length), gains, narrow, weight, last
 
 
 def line_sems(count, gathers, sums):
@@ -850,8 +1004,9 @@
 
 def attend_pass(mod_in, arrays):
     count = lax.axis_size("tensor")
-    weight, last = arrays[2:]
+    tables, gains, _, weight, last = arrays
     item = mod_in.shape
+    inner = last.shape[0]
     vmem, any_space = pl.BlockSpec(memory_space=pltpu.VMEM), pl.BlockSpec(memory_space=pl.ANY)
     low = jnp.bfloat16
     return pl.pallas_call(
@@ -866,8 +1021,8 @@
             pltpu.VMEM(weight.shape, low),
             pltpu.VMEM(last.shape, low),
             pltpu.VMEM((count, *item), low),
-            pltpu.VMEM((item[0], weight.shape[1]), jnp.float32),
-            pltpu.VMEM((item[0], last.shape[0]), low),
+            pltpu.VMEM((3, item[0], inner), jnp.float32),
+            pltpu.VMEM((item[0], inner), low),
             pltpu.VMEM((count, *item), low),
             pltpu.VMEM((count + 1, *item), low),
             *line_sems(count, 1, 1),
@@ -876,46 +1031,78 @@
             collective_id=6, has_side_effects=True, vmem_limit_bytes=60000000
         ),
         name="attend_pass",
-    )(mod_in, *arrays)
-
-
-def attend_back_pass(attend_grad, mod_all, arrays):
-    count = lax.axis_size("tensor")
-    weight, last = arrays[2:]
+    )(mod_in, tables, gains, weight, last)
+
+
+def attend_back_pass(attend_grad, mod_all, arrays, feed_weights):
+    count, wide = lax.axis_size("tensor"), lax.axis_size("dp")
+    tables, gains, narrow, weight, last = arrays
     item = attend_grad.shape
+    length, width = item
     inner = last.shape[0]
     vmem, any_space = pl.BlockSpec(memory_space=pltpu.VMEM), pl.BlockSpec(memory_space=pl.ANY)
-    low = jnp.bfloat16
-    return pl.pallas_call(
-        functools.partial(attend_back_kernel, count),
-        out_shape=(
-            jax.ShapeDtypeStruct(item, jnp.float32),
-            jax.ShapeDtypeStruct((item[1], 4 * inner), low),
-            jax.ShapeDtypeStruct((2, 8, LANES), jnp.float32),
-        ),
-        in_specs=[vmem, vmem, vmem, vmem, any_space, any_space],
-        out_specs=(vmem, vmem, vmem),
-        scratch_shapes=[
-            pltpu.VMEM(weight.shape, low),
-            pltpu.VMEM(last.shape, low),
-            pltpu.VMEM((count, *item), low),
-            pltpu.VMEM((item[0], weight.shape[1]), jnp.float32),
-            pltpu.VMEM((count, item[0], inner), low),
-            pltpu.VMEM((item[0], inner), low),
-            pltpu.VMEM((count, item[0], 3 * inner), low),
-            pltpu.VMEM((count, *item), low),
-            pltpu.VMEM((count + 1, *item), low),
-            pltpu.VMEM((item[1], 4 * inner), jnp.float32),
-            *line_sems(count, 1, 1),
-        ],
+    low, high = jnp.bfloat16, jnp.float32
+    window = narrow.shape[2]
+    first_width = 3 * window - 2 * LANES
+    columns = first_width + window
+    if width % (16 * wide):
+        wide = 0
+    size = width // wide if wide else width
+    outs = [
+        jax.ShapeDtypeStruct(item, high),
+        jax.ShapeDtypeStruct((size, columns), high if wide else low),
+        jax.ShapeDtypeStruct((2, 8, LANES), high),
+    ]
+    scratch = [
+        pltpu.VMEM(weight.shape, low),
+        pltpu.VMEM(last.shape, low),
+        pltpu.VMEM((count, *item), low),
+        pltpu.VMEM((3, length, inner), high),
+        pltpu.VMEM((length, inner), low),
+        pltpu.VMEM((length, inner), low),
+        pltpu.VMEM((3, length, inner), low),
+        pltpu.VMEM((count, length, first_width), low),
+        pltpu.VMEM((count, length, window), low),
+        pltpu.VMEM((count, *item), low),
+        pltpu.VMEM((count + 1, *item), low),
+        pltpu.VMEM((width, columns), high),
+        *line_sems(count, 1, 1),
+    ]
+    ins = [attend_grad, mod_all, tables, gains, narrow, weight, last]
+    specs = [vmem, vmem, vmem, vmem, vmem, any_space, any_space]
+    if wide:
+        ins.append(feed_weights)
+        specs.append(any_space)
+        kinds, _, units = feed_weights.shape
+        outs.append(jax.ShapeDtypeStruct((kinds, size, units), high))
+        half = wide // 2
+        scratch += [
+            pltpu.VMEM((wide, kinds, size, units), low),
+            pltpu.VMEM((width, columns), low),
+            pltpu.VMEM((half, size, columns), low),
+            pltpu.VMEM((half, size, columns), low),
+        ]
+        for number in (wide, wide, half, half, half, half):
+            scratch.append(pltpu.SemaphoreType.DMA((number,)))
+    results = pl.pallas_call(
+        functools.partial(attend_back_kernel, count, wide),
+        out_shape=tuple(outs),
+        in_specs=specs,
+        out_specs=tuple([vmem] * len(outs)),
+        scratch_shapes=scratch,
         compiler_params=pltpu.CompilerParams(
-            collective_id=7, has_side_effects=True, vmem_limit_bytes=60000000
-        ),
-        cost_estimate=pl.CostEstimate(
-            flops=int(4e10), bytes_accessed=int(2e8), transcendentals=int(1e6)
+            collective_id=7, has_side_effects=True, vmem_limit_bytes=66000000
         ),
         name="attend_back_pass",
-    )(attend_grad, mod_all, *arrays)
+    )(*ins)
+    if wide:
+        return results
+
+    def scatter(value, axis):
+        return lax.psum_scatter(value, "dp", scatter_dimension=axis, tiled=True).astype(high)
+
+    back, weights, gain_parts = results
+    return back, scatter(weights, 0), gain_parts, scatter(feed_weights, 1)
 
 
 def shards(
@@ -994,7 +1181,9 @@
     )
     attend_grad = (residual_grad * attend_gate).astype(jnp.bfloat16)
     output_bias_part = jnp.sum(attend_grad.astype(jnp.float32), axis=(0, 1))
-    mod_in_grad, attend_weights, gain_parts = attend_back_pass(attend_grad[0], mod_all, arrays)
+    mod_in_grad, attend_weights, gain_parts, feed_weights = attend_back_pass(
+        attend_grad[0], mod_all, arrays, feed_weights
+    )
     mod_in_grad = mod_in_grad[None]
     query_gain_part, key_gain_part = jnp.sum(gain_parts, axis=1)[:, :HD]
     tokens_grad = (
@@ -1094,18 +1283,10 @@
     )
     time_bias_grad = jnp.sum(pre_grad_mine.astype(jnp.float32), axis=0)
 
-    def scatter(value, axis):
-        value = value.astype(jnp.bfloat16)
-        return lax.psum_scatter(value, "dp", scatter_dimension=axis, tiled=True).astype(
-            jnp.float32
-        )
-
     inner = heads_here * HD
-    attend_weights = attend_weights.reshape(width, 4 * heads_here, LANES)[:, :, :HD]
-    attend_weights = scatter(attend_weights.reshape(width, 4 * inner), 0)
+    first_width = attend_weights.shape[1] - -(-inner // LANES) * LANES
     project_grad = attend_weights[:, : 3 * inner].reshape(-1, 3, inner)
-    output_weight_grad = attend_weights[:, 3 * inner :].T
-    feed_weights = scatter(feed_weights, 1)
+    output_weight_grad = attend_weights[:, first_width : first_width + inner].T
     expand_grad = jnp.transpose(feed_weights[:2], (1, 0, 2))
     down_grad = feed_weights[2].T
     return (

time: 487 us -> 403 us (0.83)
  local copies, waits for them, and re-layouts: 65.4 us -> 17.6 us
  waiting for transfers between devices: 30.5 us -> 0 us
  between operations: 15.2 us -> 1.79 us
  Pallas kernels: 325 us -> 333 us
  matrix products: 16.7 us -> 23.6 us
  other arithmetic: 31.7 us -> 26.3 us
    reduce_scatter x1 -> x0, waiting for transfers between devices: 30 us -> none  [scatter(): lax.psum_scatter(value, 'dp', scatter_dimension=axis, tiled=True)]
    reshape x3 -> x1, local copies, waits for them, and re-layouts: 20.9 us -> 0.44 us  [shards(): project_grad = attend_weights[:, :3 * inner].reshape(-1, 3, inner)]
    unnamed x58 -> x53, local copies, waits for them, and re-layouts: 14.8 us -> 6.63 us
    pad x2 -> x0, local copies, waits for them, and re-layouts: 7.85 us -> none  [the longest x1 5.59 us: attend_arrays(): jnp.pad(project_weight.reshape(width, 3, heads, HD), ((0, 0),) * 3 + ((0,...]
    pallas_call x4, Pallas kernels: 41.3 us -> 48.7 us  [swap(): pl.pallas_call(functools.partial(swap_kernel, tuple(plan), int(total is n...]
    dot_general x0 -> x2, matrix products: none -> 5.82 us  [the longest x1 3.92 us: attend_arrays(): jnp.einsum('dke,eh->kdh', project_weight, spread, preferred_element_type=...]
  transfers between devices with their start and end apart: 2 -> 0, of which waited for: 1 -> 0; matrix products, arithmetic and copies ran while one was open for 8% -> 0% of each run, Pallas kernels for 7% -> 0%
where the time goes in v5:
time: 403 us; the launch traced here: 402 us
  Pallas kernels  333 us (83%)
  other arithmetic  26.3 us (7%)
  matrix products  23.6 us (6%)
  local copies, waits for them, and re-layouts  17.6 us (4%)
    pallas_call x1, Pallas kernels, feed_pass(): pl.pallas_call(functools.partial(feed_kernel, count), out_shape=(jax.Shap...  115 us
    pallas_call x1, Pallas kernels, attend_back_pass(): pl.pallas_call(functools.partial(attend_back_kernel, count, wide), out_sh...  92.8 us
    pallas_call x1, Pallas kernels, attend_pass(): pl.pallas_call(functools.partial(attend_kernel, count), out_shape=(jax.Sh...  76.2 us
    pallas_call x4, Pallas kernels, swap(): pl.pallas_call(functools.partial(swap_kernel, tuple(plan), int(total is n...  48.7 us

profile of v5, /device:TPU:0, one launch (start us, length us, event | category | flops | bytes accessed | tf_op | source)
XLA Modules:
  0.0 402.2 jit_solution(14603464282837033642)
XLA Ops:
  2.2 1.3 convolution_add_fusion.1
  4.1 2.5 gather_fusion
  8.0 2.2 fusion
  10.2 3.5 fusion.58
  14.4 8.7 %modulation_swap.1 = bf16[4,6,288]{2,1,0:T(8,128)(2,1)} custom-call(bf16[4,6,288]{2,1,0:T(8,128)(2,1)} %fusion.48.refs_0_), custom_call_target="tpu_custom_call" | custom-call | tf_op jit(solution)/shard_map/modulation_swap/pallas_call | solution.py:554
  25.2 1.3 fusion.30
  28.0 3.9 convolution_bitcast_fusion.weight_hbm
  31.9 1.9 fusion.32.last_hbm
  34.4 76.2 %attend_pass.1 = (f32[256,1152]{1,0:T(8,128)}, bf16[4,256,1152]{2,1,0:T(8,128)(2,1)}) custom-call(bf16[256,1152]{1,0:T(8,128)(2,1)} %get-tuple-element.124.mod_ref, f32[3,256,128]{2,1,0:T(8,128)} %pad_maximum_fusion.tables_ref, f32[8,128]{1,0:T(8,128)} %fusion.73.gains_ref, bf16[3,1152,512]{2,1,0:T(8,128)(2,1)} %convolution_bitcast_fusion.weight_hbm, ...), custom_call_target="tpu_custom_call" | custom-call | tf_op jit(solution)/shard_map/attend_pass/pallas_call | solution.py:1012
  110.7 1.7 fusion.98
  112.7 1.1 fusion.29.mod_ref
  113.8 2.2 copy.66
  116.0 115.2 %feed_pass.1 = (f32[256,1152]{1,0:T(8,128)}, f32[256,1152]{1,0:T(8,128)}, bf16[3,1152,768]{2,1,0:T(8,128)(2,1)}) custom-call(bf16[256,1152]{1,0:T(8,128)(2,1)} %fusion.29.mod_ref, bf16[256,1152]{1,0:T(8,128)(2,1)} %get-tuple-element.125.grad_ref, bf16[2,1152,768]{2,1,0:T(8,128)(2,1)} %bitcast.95, bf16[768,1152]{1,0:T(8,128)(2,1)} %down_hbm.1), custom_call_target="tpu_custom_call" | custom-call | tf_op jit(solution)/shard_map/feed_pass/pallas_call | solution.py:414
  231.2 1.6 fusion.95
  234.5 2.2 convert_reduce_fusion.1
  236.7 1.0 fusion.41.grad_ref
  238.3 1.3 add_convert_fusion.narrow_ref
  239.6 92.8 %attend_back_pass.1 = (f32[256,1152]{1,0:T(8,128)}, f32[144,1280]{1,0:T(8,128)}, f32[2,8,128]{2,1,0:T(8,128)}, f32[3,144,768]{2,1,0:T(8,128)}) custom-call(bf16[256,1152]{1,0:T(8,128)(2,1)} %fusion.41.grad_ref, bf16[4,256,1152]{2,1,0:T(8,128)(2,1)} %get-tuple-element.33.mod_all, f32[3,256,128]{2,1,0:T(8,128)} %pad_maximum_fusion.tables_ref, ...), custom_call_target="tpu_custom_call" | custom-call | tf_op jit(solution)/shard_map/attend_back_pass/pallas_call | solution.py:1087
  332.4 1.5 fusion.96
  334.0 1.8 fusion.16
  337.9 22.0 %sums_swap.1 = (bf16[4,6,288]{2,1,0:T(8,128)(2,1)}, f32[80,128]{1,0:T(8,128)}) custom-call(bf16[4,6,288]{2,1,0:T(8,128)(2,1)} %bitcast.96, f32[80,128]{1,0:T(8,128)} %pad_bitcast_fusion.refs_1_), custom_call_target="tpu_custom_call" | custom-call | tf_op jit(solution)/shard_map/sums_swap/pallas_call | solution.py:554
  359.9 3.4 convolution_bitcast_fusion.1.refs_0_
  363.3 7.4 %condition_swap.1 = f32[4,4,1152]{2,1,0:T(4,128)} custom-call(f32[4,1152]{1,0:T(4,128)} %convolution_bitcast_fusion.1.refs_0_), custom_call_target="tpu_custom_call" | custom-call | tf_op jit(solution)/shard_map/condition_swap/pallas_call | solution.py:554
  371.7 2.6 fusion.2
  375.3 10.7 %items_swap.1 = (bf16[8,4,6592]{2,1,0:T(4,128)(2,1)}, s32[8,4,128]{2,1,0:T(4,128)}) custom-call(bf16[4,6592]{1,0:T(4,128)(2,1)} %copy-done.14, s32[4,128]{1,0:T(4,128)} %broadcast_in_dim.117.refs_1_), custom_call_target="tpu_custom_call" | custom-call | tf_op jit(solution)/shard_map/items_swap/pallas_call | solution.py:554
  386.0 1.2 reshape.846
  387.5 1.2 fusion.46
  388.7 1.2 fusion.53
  389.9 0.9 fusion.50
  391.1 1.5 fusion.42
  397.8 1.6 copy.56
  399.4 1.3 fusion.15
  (134 shorter events, 21.6 us)
Async XLA Ops:
  0.7 31.2 %copy-start = (bf16[288,1152]{1,0:T(8,128)(2,1)S(1)}, bf16[288,1152]{1,0:T(8,128)(2,1)}, u32[]{:S(2)}) copy-start(bf16[288,1152]{1,0:T(8,128)(2,1)} %param.28) | copy-start | bytes 1990660
  10.2 3.5 copy-start.18
  10.2 13.8 %copy-start.1 = (bf16[1,256,1152]{2,1,0:T(8,128)(2,1)S(1)}, bf16[1,256,1152]{2,1,0:T(8,128)(2,1)}, u32[]{:S(2)}) copy-start(bf16[1,256,1152]{2,1,0:T(8,128)(2,1)} %param.20) | copy-start | bytes 1769476
  13.8 11.5 %copy-start.9 = (bf16[1,256,1152]{2,1,0:T(8,128)(2,1)S(1)}, bf16[1,256,1152]{2,1,0:T(8,128)(2,1)}, u32[]{:S(2)}) copy-start(bf16[1,256,1152]{2,1,0:T(8,128)(2,1)} %param.24) | copy-start | bytes 1769476
  25.2 2.7 copy-start.24
  31.9 1.9 copy-start.21
  31.9 1.9 copy-start.22
  34.4 76.3 %copy-start.19 = (bf16[1152]{0:T(1024)(128)(2,1)S(1)}, bf16[1152]{0:T(1024)(128)(2,1)}, u32[]{:S(2)}) copy-start(bf16[1152]{0:T(1024)(128)(2,1)} %param.29) | copy-start | bytes 6916
  110.7 3.1 copy-start.8
  231.2 1.6 copy-start.4
  232.8 0.7 copy-start.20
  232.9 1.3 copy-start.7
  232.9 1.6 copy-start.11
  236.7 1.6 copy-start.5
  332.4 1.6 copy-start.2
  334.0 2.0 copy-start.17
  371.7 2.8 copy-start.13
  371.7 3.0 copy-start.23
  374.7 0.7 copy-start.14
  386.0 1.2 copy-start.16
  389.9 4.0 copy-start.15
  389.9 5.8 %copy-start.12 = (f32[144,1280]{1,0:T(8,128)S(1)}, f32[144,1280]{1,0:T(8,128)}, u32[]{:S(2)}) copy-start(f32[144,1280]{1,0:T(8,128)} %get-tuple-element.36) | copy-start | bytes 2211844
  396.2 1.6 copy-start.10
  397.8 1.7 copy-start.6
  397.8 1.6 copy-start.3
